TPU v7x, 32 devices: a whole 2x2x4 slice. The times are simulated.
32 devices in a mesh: groups: 2 (over y), rowt: 4 (over z), colt: 2 (over x), site: 2 (over core).
Axes of the slice: x: 2, y: 2, z: 4, core: 2. Of those that a mesh axis runs over, the one named last changes fastest.
Arguments:
- seed_green: bfloat16 [8, 2, 768, 768], P(('groups', 'rowt'), 'colt', None, 'site'), parts along dimension 0, may hold values from -6 to 6
- field_spins: int32 [4, 8, 768], P(None, ('groups', 'rowt')), parts along dimension 1, may hold values from 0 to 1
- hop_matrix: float32 [768, 768], replicated, may hold values from -0.21875 to 0.21875
- vertex: bfloat16 [768, 768], replicated, may hold values from -0.21875 to 0.21875
Outputs:
- measured: bfloat16 [8, 2, 768, 768], P(('groups', 'rowt'), 'colt', None, 'site'), parts along dimension 0
There are 2 independent parts, one for each index of `groups`. A program takes and returns all parts, laid end to end along the dimension named above; an argument that names none is the same for every part. Nothing has to cross between parts.
All inputs are finite; a program needn't handle non-finite values.
Results may differ from a plain program's by a relative error of at most 0.0051.
Values may be sent and summed in bfloat16 or wider, within the bound.
No kernel may reach another device: no remote copies, remote signals or barrier semaphores. Data moves between devices by JAX's collectives and lax.ppermute only.
A program may use at most 64 MiB of HBM per device.

v0:
```python
import jax
import jax.numpy as jnp
from jax import lax
from jax.sharding import PartitionSpec as P

coupling = 0.45
keep_share = 0.8
hop_share = 0.3


def partner(x, axis, distance):
    return lax.ppermute(x, axis, [(i, i ^ 1 << distance) for i in range(lax.axis_size(axis))])


def advance(current, hop_matrix, weights_row, sign_value):
    hopped = jnp.dot(hop_matrix, current, precision=lax.Precision.HIGHEST)
    image = keep_share * current + hop_share * hopped
    return (sign_value * weights_row)[:, None] * image


def measure(current, vertex):
    rounded = current.astype(jnp.bfloat16)
    top_bit = lax.axis_size(("colt", "site")).bit_length() - 2
    local_rows = lax.all_to_all(rounded, "site", split_axis=0, concat_axis=1, tiled=True)
    partner_rows = partner(local_rows, ("colt", "site"), top_bit)
    pair_product = (rounded.astype(jnp.float32) * partner_rows.T.astype(jnp.float32)).astype(
        jnp.bfloat16
    )
    return jnp.dot(vertex, pair_product, preferred_element_type=jnp.float32)


def per_device(seed_green, field_spins, hop_matrix, vertex):
    wraps = field_spins.shape[0]
    row_count = lax.axis_size("rowt")
    row_index = lax.axis_index("rowt")
    weights = jnp.exp(coupling * (2.0 * field_spins.astype(jnp.float32) - 1.0))
    current = seed_green[0, 0].astype(jnp.float32)
    all_weights = lax.all_gather(weights, "rowt", axis=1, tiled=True)
    measured = jnp.zeros_like(current)
    for wrap_step in range(wraps):
        target = (row_index + wrap_step + 1) % row_count
        weights_row = lax.dynamic_index_in_dim(all_weights[wrap_step], target, 0, keepdims=False)
        sign_value = jnp.where(target == 0, -1.0, 1.0).astype(jnp.float32)
        current = advance(current, hop_matrix, weights_row, sign_value)
        measured = measured + measure(current, vertex)
    result = (measured / wraps).astype(jnp.bfloat16)
    return result[None, None]


def solution(mesh):
    return jax.shard_map(
        per_device,
        mesh=mesh,
        in_specs=(
            P(("groups", "rowt"), "colt", None, "site"),
            P(None, ("groups", "rowt"), None),
            P(),
            P(),
        ),
        out_specs=P(("groups", "rowt"), "colt", None, "site"),
        check_vma=False,
    )
```

profile of v0, /device:TPU:0, one launch (start us, length us, event | category | flops | bytes accessed | tf_op | source)
XLA Modules:
  0.0 87.3 jit_solution(8937611655515566812)
XLA Ops:
  0.0 0.0 copy-start
  0.0 0.9 fusion.28
  0.9 14.8 %all_gather.3 = f32[4,4,768]{2,0,1:T(4,128)S(1)} all-gather(f32[4,1,768]{2,0,1:T(4,128)S(1)} %fusion.28), channel_id=1, replica_groups=mesh['groups'=2,'rowt'=4,'colt'=2,'site'=2] {'rowt'}, dimensions={1}, use_global_device_ids=true | all-gather | bytes 61440 | tf_op jit(solution)/shard_map/all_gather | solution.py:38
  15.7 0.0 copy-done
  15.8 3.3 %fusion.31 = (bf16[768,384]{1,0:T(8,128)(2,1)S(1)}, f32[768,384]{1,0:T(8,128)S(1)}) fusion(f32[768,768]{1,0:T(8,128)S(1)} %copy-done, bf16[1,1,768,384]{3,2,1,0:T(8,128)(2,1)} %param.4, f32[768]{0:T(1024)S(1)} %multiply_reduce_fusion.3), kind=kOutput, calls=%fused_computation.43 | convolution fusion | flops 2719678464 | bytes 4721664 | tf_op jit(solution)/shard_map/dot_general | solution.py:16
  19.1 0.0 copy-start.5
  19.1 5.0 %fusion.30 = (bf16[768,384]{1,0:T(8,128)(2,1)S(1)}, f32[768,384]{1,0:T(8,128)}) fusion(f32[768,384]{1,0:T(8,128)S(1)} %get-tuple-element.12, f32[768,768]{1,0:T(8,128)S(1)} %copy-done, f32[768]{0:T(1024)S(1)} %get-tuple-element.16), kind=kOutput, calls=%fused_computation.42 | convolution fusion | flops 2719383552 | bytes 5311488 | tf_op jit(solution)/shard_map/dot_general | solution.py:16
  24.1 0.0 copy-start.4
  24.1 0.8 copy-done.4
  24.9 4.2 %all_to_all.76 = bf16[2,384,384]{2,1,0:T(8,128)(2,1)S(1)} all-to-all(bf16[2,384,384]{2,1,0:T(8,128)(2,1)S(1)} %bitcast.73), channel_id=1, replica_groups=mesh['groups'=2,'rowt'=4,'colt'=2,'site'=2] {'site'}, dimensions={0} | all-to-all | bytes 1179648 | tf_op jit(solution)/shard_map/all_to_all | solution.py:24
  29.1 1.1 %copy.16 = bf16[384,2,384]{0,2,1:T(8,128)(2,1)} copy(bf16[384,2,384]{2,0,1:T(8,128)(2,1)S(1)} %bitcast.76) | data formatting | bytes 1179648 | tf_op jit(solution)/shard_map/all_to_all | solution.py:24
  30.2 1.5 %collective-permute-start.1 = (bf16[384,768]{0,1:T(8,128)(2,1)}, bf16[384,768]{0,1:T(8,128)(2,1)}, u32[]{:S(2)}, u32[]{:S(2)}) collective-permute-start(bf16[384,768]{0,1:T(8,128)(2,1)} %bitcast.80), channel_id=1, source_target_pairs={{0,2},{1,3},{2,0},{3,1},{4,6},{5,7},{6,4},{7,5},{8,10},{9,11},{10,... | collective-permute-start | bytes 1769480 | tf_op jit(solution)/shard_map/ppermute | solution.py:12
  31.7 0.0 copy-done.5
  31.7 4.2 %all_to_all.77 = bf16[2,384,384]{2,1,0:T(8,128)(2,1)S(1)} all-to-all(bf16[2,384,384]{2,1,0:T(8,128)(2,1)S(1)} %bitcast.74), channel_id=1, replica_groups=mesh['groups'=2,'rowt'=4,'colt'=2,'site'=2] {'site'}, dimensions={0} | all-to-all | bytes 1179648 | tf_op jit(solution)/shard_map/all_to_all | solution.py:24
  35.8 1.1 %copy.14 = bf16[384,2,384]{0,2,1:T(8,128)(2,1)} copy(bf16[384,2,384]{2,0,1:T(8,128)(2,1)S(1)} %bitcast.77) | data formatting | bytes 1179648 | tf_op jit(solution)/shard_map/all_to_all | solution.py:24
  36.9 0.5 collective-permute-start
  37.5 5.6 %fusion.32 = (bf16[768,384]{1,0:T(8,128)(2,1)S(1)}, f32[768,384]{1,0:T(8,128)S(1)}) fusion(f32[768,384]{1,0:T(8,128)} %get-tuple-element.10, f32[768,768]{1,0:T(8,128)S(1)} %copy-done, f32[768]{0:T(1024)S(1)} %get-tuple-element.15), kind=kOutput, calls=%fused_computation.44 | convolution fusion | flops 2719383552 | bytes 5311488 | tf_op jit(solution)/shard_map/dot_general | solution.py:16
  43.1 0.0 copy-start.2
  43.1 0.8 copy-done.2
  43.9 4.9 %all_to_all.78 = bf16[2,384,384]{2,1,0:T(8,128)(2,1)} all-to-all(bf16[2,384,384]{2,1,0:T(8,128)(2,1)S(1)} %bitcast.72), channel_id=1, replica_groups=mesh['groups'=2,'rowt'=4,'colt'=2,'site'=2] {'site'}, dimensions={0} | all-to-all | bytes 1179648 | tf_op jit(solution)/shard_map/all_to_all | solution.py:24
  48.8 2.1 %copy.18 = bf16[384,2,384]{0,2,1:T(8,128)(2,1)} copy(bf16[384,2,384]{2,0,1:T(8,128)(2,1)} %bitcast.78) | data formatting | bytes 1179648 | tf_op jit(solution)/shard_map/all_to_all | solution.py:24
  51.0 1.5 %collective-permute-start.2 = (bf16[384,768]{0,1:T(8,128)(2,1)}, bf16[384,768]{0,1:T(8,128)(2,1)}, u32[]{:S(2)}, u32[]{:S(2)}) collective-permute-start(bf16[384,768]{0,1:T(8,128)(2,1)} %bitcast.81), channel_id=1, source_target_pairs={{0,2},{1,3},{2,0},{3,1},{4,6},{5,7},{6,4},{7,5},{8,10},{9,11},{10,... | collective-permute-start | bytes 1769480 | tf_op jit(solution)/shard_map/ppermute | solution.py:12
  52.5 3.9 %fusion.12 = bf16[768,384]{1,0:T(8,128)(2,1)S(1)} fusion(f32[768,384]{1,0:T(8,128)S(1)} %get-tuple-element.14, f32[768,768]{1,0:T(8,128)S(1)} %copy-done, f32[768]{0:T(1024)S(1)} %multiply_reduce_fusion), kind=kOutput, calls=%fused_computation.19 | convolution fusion | flops 2719383552 | bytes 4131840 | tf_op jit(solution)/shard_map/dot_general | solution.py:16
  56.4 0.0 copy-start.7
  56.4 0.8 copy-done.7
  57.2 0.0 copy-start.1
  57.2 5.1 %all_to_all.79 = bf16[2,384,384]{2,1,0:T(8,128)(2,1)} all-to-all(bf16[2,384,384]{2,1,0:T(8,128)(2,1)S(1)} %bitcast.75), channel_id=1, replica_groups=mesh['groups'=2,'rowt'=4,'colt'=2,'site'=2] {'site'}, dimensions={0} | all-to-all | bytes 1179648 | tf_op jit(solution)/shard_map/all_to_all | solution.py:24
  62.3 2.2 %copy.20 = bf16[384,2,384]{0,2,1:T(8,128)(2,1)} copy(bf16[384,2,384]{2,0,1:T(8,128)(2,1)} %bitcast.79) | data formatting | bytes 1179648 | tf_op jit(solution)/shard_map/all_to_all | solution.py:24
  64.5 0.0 copy-start.6
  64.5 0.5 collective-permute-start.3
  65.0 0.0 collective-permute-done.1
  65.0 0.0 copy-done.1
  65.0 1.9 %fusion.20 = f32[384,768]{1,0:T(8,128)S(1)} fusion(bf16[768,768]{1,0:T(8,128)(2,1)S(1)} %copy-done.1, bf16[384,768]{0,1:T(8,128)(2,1)} %collective-permute-done.1, bf16[768,384]{1,0:T(8,128)(2,1)} %copy-done.4), kind=kOutput, calls=%fused_computation.30 | convolution fusion | flops 454164480 | bytes 3538944 | tf_op jit(solution)/shard_map/dot_general | solution.py:29
  66.9 0.0 copy-start.3
  67.0 0.0 collective-permute-done
  67.0 0.0 copy-done.6
  67.0 1.8 %convolution_add_fusion.2 = f32[384,768]{1,0:T(8,128)S(1)} fusion(f32[384,768]{1,0:T(8,128)S(1)} %fusion.20, bf16[768,768]{1,0:T(8,128)(2,1)S(1)} %copy-done.1, bf16[384,768]{0,1:T(8,128)(2,1)} %collective-permute-done, bf16[768,384]{1,0:T(8,128)(2,1)S(1)} %copy-done.6), kind=kOutput, calls=%fused_computation.6 | convolution fusion | flops 454459392 | bytes 4718592 | tf_op jit(solution)/shard_map/dot_general | solution.py:29
  68.8 0.0 copy-start.8
  68.8 3.1 %collective-permute-done.2 = bf16[384,768]{0,1:T(8,128)(2,1)} collective-permute-done((bf16[384,768]{0,1:T(8,128)(2,1)}, bf16[384,768]{0,1:T(8,128)(2,1)}, u32[]{:S(2)}, u32[]{:S(2)}) %collective-permute-start.2) | collective-permute-done | bytes 589856 | tf_op jit(solution)/shard_map/ppermute | solution.py:12
  72.0 0.0 copy-done.3
  72.0 1.8 %convolution_add_fusion.1 = f32[384,768]{1,0:T(8,128)S(1)} fusion(f32[384,768]{1,0:T(8,128)S(1)} %convolution_add_fusion.2, bf16[768,768]{1,0:T(8,128)(2,1)S(1)} %copy-done.1, bf16[384,768]{0,1:T(8,128)(2,1)} %collective-permute-done.2, bf16[768,384]{1,0:T(8,128)(2,1)S(1)} %copy-done.3), kind=kOutput, calls=%fused_computation.3 | convolution fusion | flops 454459392 | bytes 4718592 | tf_op jit(solution)/shard_map/dot_general | solution.py:29
  73.7 9.9 %collective-permute-done.3 = bf16[384,768]{0,1:T(8,128)(2,1)S(1)} collective-permute-done((bf16[384,768]{0,1:T(8,128)(2,1)}, bf16[384,768]{0,1:T(8,128)(2,1)S(1)}, u32[]{:S(2)}, u32[]{:S(2)}) %collective-permute-start.3) | collective-permute-done | bytes 589856 | tf_op jit(solution)/shard_map/ppermute | solution.py:12
  83.7 0.0 copy-done.8
  83.7 1.5 %fusion.14 = bf16[1,1,768,384]{2,3,1,0:T(8,128)(2,1)} fusion(f32[384,768]{1,0:T(8,128)S(1)} %convolution_add_fusion.1, bf16[768,768]{1,0:T(8,128)(2,1)S(1)} %copy-done.1, bf16[384,768]{0,1:T(8,128)(2,1)S(1)} %collective-permute-done.3, bf16[768,384]{1,0:T(8,128)(2,1)S(1)} %copy-done.8), kind=kOutput, calls=%fused_computation.21 | convolution fusion | flops 455049216 | bytes 4128768 | tf_op jit(solution)/shard_map/dot_general | solution.py:29
  85.2 2.1 %copy.21 = bf16[1,1,768,384]{3,2,1,0:T(8,128)(2,1)} copy(bf16[1,1,768,384]{2,3,1,0:T(8,128)(2,1)} %fusion.14) | data formatting | bytes 1179648 | tf_op jit(solution)/shard_map/broadcast_in_dim | solution.py:47
  (4 shorter events, 0.1 us)
Async XLA Ops:
  0.0 15.8 %copy-start = (f32[768,768]{1,0:T(8,128)S(1)}, f32[768,768]{1,0:T(8,128)}, u32[]{:S(2)}) copy-start(f32[768,768]{1,0:T(8,128)} %param.6) | copy-start | bytes 7077892
  19.1 12.6 %copy-start.5 = (bf16[768,384]{1,0:T(8,128)(2,1)}, bf16[768,384]{1,0:T(8,128)(2,1)S(1)}, u32[]{:S(2)}) copy-start(bf16[768,384]{1,0:T(8,128)(2,1)S(1)} %get-tuple-element.11) | copy-start | bytes 1769476
  24.1 0.8 copy-start.4
  30.2 34.9 %collective-permute-start.1 = (bf16[384,768]{0,1:T(8,128)(2,1)}, bf16[384,768]{0,1:T(8,128)(2,1)}, u32[]{:S(2)}, u32[]{:S(2)}) collective-permute-start(bf16[384,768]{0,1:T(8,128)(2,1)} %bitcast.80), channel_id=1, source_target_pairs={{0,2},{1,3},{2,0},{3,1},{4,6},{5,7},{6,4},{7,5},{8,10},{9,11},{10,... | collective-permute-start | bytes 1769480 | tf_op jit(solution)/shard_map/ppermute | solution.py:12
  36.9 30.0 %collective-permute-start = (bf16[384,768]{0,1:T(8,128)(2,1)}, bf16[384,768]{0,1:T(8,128)(2,1)}, u32[]{:S(2)}, u32[]{:S(2)}) collective-permute-start(bf16[384,768]{0,1:T(8,128)(2,1)} %bitcast.3), channel_id=1, source_target_pairs={{0,2},{1,3},{2,0},{3,1},{4,6},{5,7},{6,4},{7,5},{8,10},{9,11},{10,... | collective-permute-start | bytes 1769480 | tf_op jit(solution)/shard_map/ppermute | solution.py:12
  43.1 0.8 copy-start.2
  51.0 21.0 %collective-permute-start.2 = (bf16[384,768]{0,1:T(8,128)(2,1)}, bf16[384,768]{0,1:T(8,128)(2,1)}, u32[]{:S(2)}, u32[]{:S(2)}) collective-permute-start(bf16[384,768]{0,1:T(8,128)(2,1)} %bitcast.81), channel_id=1, source_target_pairs={{0,2},{1,3},{2,0},{3,1},{4,6},{5,7},{6,4},{7,5},{8,10},{9,11},{10,... | collective-permute-start | bytes 1769480 | tf_op jit(solution)/shard_map/ppermute | solution.py:12
  56.4 0.8 copy-start.7
  57.2 7.8 %copy-start.1 = (bf16[768,768]{1,0:T(8,128)(2,1)S(1)}, bf16[768,768]{1,0:T(8,128)(2,1)}, u32[]{:S(2)}) copy-start(bf16[768,768]{1,0:T(8,128)(2,1)} %param.7) | copy-start | bytes 3538948
  64.5 2.5 %copy-start.6 = (bf16[768,384]{1,0:T(8,128)(2,1)S(1)}, bf16[768,384]{1,0:T(8,128)(2,1)}, u32[]{:S(2)}) copy-start(bf16[768,384]{1,0:T(8,128)(2,1)} %copy-done.5) | copy-start | bytes 1769476
  64.5 19.2 %collective-permute-start.3 = (bf16[384,768]{0,1:T(8,128)(2,1)}, bf16[384,768]{0,1:T(8,128)(2,1)S(1)}, u32[]{:S(2)}, u32[]{:S(2)}) collective-permute-start(bf16[384,768]{0,1:T(8,128)(2,1)} %bitcast.82), channel_id=1, source_target_pairs={{0,2},{1,3},{2,0},{3,1},{4,6},{5,7},{6,4},{7,5},{8,10},{9,11},{10,... | collective-permute-start | bytes 1769480 | tf_op jit(solution)/shard_map/ppermute | solution.py:12
  66.9 5.0 %copy-start.3 = (bf16[768,384]{1,0:T(8,128)(2,1)S(1)}, bf16[768,384]{1,0:T(8,128)(2,1)}, u32[]{:S(2)}) copy-start(bf16[768,384]{1,0:T(8,128)(2,1)} %copy-done.2) | copy-start | bytes 1769476
  68.8 14.9 %copy-start.8 = (bf16[768,384]{1,0:T(8,128)(2,1)S(1)}, bf16[768,384]{1,0:T(8,128)(2,1)}, u32[]{:S(2)}) copy-start(bf16[768,384]{1,0:T(8,128)(2,1)} %copy-done.7) | copy-start | bytes 1769476
where the time goes:
time: 87.9 us; the launch traced here: 87.3 us
  blocking collectives  33.2 us (38%)
  matrix products  24.8 us (28%)
  waiting for transfers between devices  13.1 us (15%)
  local copies, waits for them, and re-layouts  11.1 us (13%)
  starting transfers between devices  4.05 us (5%)
  other arithmetic  0.94 us (1%)
    all_to_all x4, blocking collectives, measure(): lax.all_to_all(rounded, 'site', split_axis=0, concat_axis=1, tiled=True)  18.4 us
    dot_general x4, matrix products, advance(): hopped = jnp.dot(hop_matrix, current, precision=lax.Precision.HIGHEST)  17.8 us
    all_gather x1, blocking collectives, per_device(): all_weights = lax.all_gather(weights, 'rowt', axis=1, tiled=True)  14.8 us
    ppermute x4, waiting for transfers between devices, partner(): lax.ppermute(x, axis, [(i, i ^ 1 << distance) for i in range(lax.axis_siz...  13.1 us
    dot_general x4, matrix products, measure(): return jnp.dot(vertex, pair_product, preferred_element_type=jnp.float32)  7.02 us
    all_to_all x4, local copies, waits for them, and re-layouts, measure(): lax.all_to_all(rounded, 'site', split_axis=0, concat_axis=1, tiled=True)  6.42 us
    ppermute x4, starting transfers between devices, partner(): lax.ppermute(x, axis, [(i, i ^ 1 << distance) for i in range(lax.axis_siz...  4.05 us
    unnamed x18, local copies, waits for them, and re-layouts  2.48 us
  transfers between devices with their start and end apart: 4, of which 2 were waited for; matrix products, arithmetic and copies ran while one was open for 23% of the time, Pallas kernels for 0%

commit v1 on v0

v1 whole, which is shorter than its diff:
```python
import functools

import jax
import jax.numpy as jnp
from jax import lax
from jax.experimental import pallas as pl
from jax.experimental.pallas import tpu as pltpu
from jax.sharding import PartitionSpec as P


coupling = 0.45
keep_share = 0.8
hop_share = 0.3
LANES = 128


VMEM = pl.BlockSpec(memory_space=pltpu.VMEM)
HBM = pl.BlockSpec(memory_space=pltpu.HBM)


def limit(mebibytes):
    return pltpu.CompilerParams(vmem_limit_bytes=mebibytes << 20)


def in_hbm(array):
    return pltpu.with_memory_space_constraint(array, pltpu.HBM)


def split_halves(value):
    high = value.astype(jnp.bfloat16)
    low = (value - high.astype(jnp.float32)).astype(jnp.bfloat16)
    return high, low


def cut_kernel(spans, seed_ref, spins_ref, *refs):
    pieces, lines = refs[: len(spans)], refs[len(spans) : -3]
    spins_in, piece_sems, spin_sem = refs[-3:]
    spin_copy = pltpu.make_async_copy(spins_ref, spins_in, spin_sem)
    copies = [
        pltpu.make_async_copy(seed_ref.at[:, pl.ds(a, b - a)], piece, piece_sems.at[number])
        for number, ((a, b), piece) in enumerate(zip(spans, pieces))
    ]
    for copy in copies:
        copy.start()
    spin_copy.start()
    spin_copy.wait()
    for step, line in enumerate(lines):
        line[...] = spins_in[step].astype(jnp.float32).astype(jnp.bfloat16)
    for copy in copies:
        copy.wait()


def prepare_kernel(hop_ref, *refs):
    pieces = refs[:-4]
    hop_out, high_t, low_t, turned_out = refs[-4:]
    start = 0
    for piece in pieces:
        turned_out[start : start + piece.shape[1], :] = piece[...].T
        start += piece.shape[1]
    for start in range(0, hop_ref.shape[0], LANES):
        span = slice(start, start + LANES)
        high, low = split_halves(hop_share * hop_ref[span, :])
        hop_out[span, :] = high
        high_t[:, span] = high.T
        low_t[:, span] = low.T


def own_kernel(row_count, seed_t, high_t, low_t, *refs):
    wraps = len(refs) - 2
    turned_out, scale_out = refs[wraps:]
    row_index = lax.axis_index("rowt")
    turned = seed_t[...].astype(jnp.float32)
    narrow = seed_t[...]
    for step in range(wraps):
        spins = refs[step][...].astype(jnp.float32)
        sign = jnp.where((row_index + step + 1) % row_count == 0, -1.0, 1.0)
        scale = sign * jnp.exp(coupling * (2.0 * spins - 1.0))
        column = jnp.broadcast_to(scale, (8, scale.shape[1])).T[:, :1]
        scale_out[step] = jnp.broadcast_to(column, scale_out.shape[1:])
        hopped = jnp.dot(narrow, high_t[...], preferred_element_type=jnp.float32)
        hopped += jnp.dot(narrow, low_t[...], preferred_element_type=jnp.float32)
        turned = scale * (keep_share * turned + hopped)
        narrow = turned.astype(jnp.bfloat16)
        turned_out[step] = narrow


def site_spans(width):
    site = lax.axis_index("site")
    places = (site, lax.axis_size("site") - 1 - site)
    return [pl.ds(pl.multiple_of(place * width, LANES), width) for place in places]


def advance(step, spans, hop_ref, scale_ref, level, narrow):
    source, target = step % 2, (step + 1) % 2
    copies = level.shape[1] // LANES
    for span in spans:
        hopped = jnp.dot(hop_ref[span, :], narrow[source], preferred_element_type=jnp.float32)
        scale = jnp.concatenate([scale_ref[step, span, :]] * copies, axis=1)
        moved = scale * (keep_share * level[span, :] + hopped)
        rounded = moved.astype(jnp.bfloat16)
        level[span, :] = moved
        narrow[target, span, :] = rounded
        yield rounded


def chain_kernel(arrived, hop_ref, scale_ref, keep_out, send_out, level, narrow):
    spans = site_spans(keep_out.shape[1])
    narrow[0] = arrived[...]
    level[...] = arrived[...].astype(jnp.float32)
    for step in range(keep_out.shape[0]):
        rounded = advance(step, spans, hop_ref, scale_ref, level, narrow)
        for out, value in zip((keep_out, send_out), rounded):
            out[step] = value


def multiply(met, own):
    product = met.astype(jnp.float32) * own.astype(jnp.float32)
    return product.astype(jnp.bfloat16).astype(jnp.float32)


def columns_at(offset, part, width):
    site = lax.axis_index("site")
    places = (site, lax.axis_size("site") - 1 - site)
    return [pl.ds(pl.multiple_of(place * width + offset, LANES), part) for place in places]


def sum_kernel(offset, ours, theirs, turned_ref, vertex_ref, out_ref):
    wraps, width, _ = turned_ref.shape
    total = None
    for met_ref, spot in zip((ours, theirs), columns_at(offset, ours.shape[2], width)):
        pairs = None
        for step in range(wraps):
            product = multiply(met_ref[step], turned_ref[step, :, spot])
            pairs = product if pairs is None else pairs + product
        for half in split_halves(pairs):
            part = lax.dot_general(
                vertex_ref[:, spot],
                half,
                (((1,), (1,)), ((), ())),
                preferred_element_type=jnp.float32,
            )
            total = part if total is None else total + part
    out_ref[...] = total


def finish_kernel(offset, *refs):
    ours, theirs, turned_ref, hop_ref, scale_ref, vertex_ref, total_ref = refs[:7]
    out_ref, level, narrow, result, sems = refs[7:]
    wraps, width, sites = turned_ref.shape
    spans = site_spans(width)
    spots = columns_at(offset, ours.shape[1], width)
    arrived = jnp.concatenate([ours[...], theirs[...]], axis=1)
    narrow[0] = arrived
    level[...] = arrived.astype(jnp.float32)
    pairs = None
    for step in range(wraps):
        needed = spans if step < wraps - 1 else spans[:1]
        met = list(advance(step, needed, hop_ref, scale_ref, level, narrow))[0]
        own = jnp.concatenate([turned_ref[step, :, spot] for spot in spots], axis=1)
        product = multiply(met, own)
        pairs = product if pairs is None else pairs + product
    halves = split_halves(pairs)
    blocks = sems.shape[0]
    size = sites // blocks
    copies = []
    for block in range(blocks):
        span = slice(block * size, (block + 1) * size)
        corner = jnp.concatenate([vertex_ref[span, spot] for spot in spots], axis=1)
        total = total_ref[span, :]
        for half in halves:
            total = total + lax.dot_general(
                corner, half, (((1,), (1,)), ((), ())), preferred_element_type=jnp.float32
            )
        result[span, :] = (total / wraps).astype(result.dtype)
        copy = pltpu.make_async_copy(
            result.at[pl.ds(block * size, size)],
            out_ref.at[pl.ds(block * size, size)],
            sems.at[block],
        )
        copy.start()
        copies.append(copy)
    for copy in copies:
        copy.wait()


def cut(seed, spins, spans):
    wraps, sites = spins.shape[0], seed.shape[0]
    outs = [jax.ShapeDtypeStruct((sites, b - a), jnp.bfloat16) for a, b in spans]
    outs += [jax.ShapeDtypeStruct((1, sites), jnp.bfloat16)] * wraps
    result = pl.pallas_call(
        functools.partial(cut_kernel, spans),
        out_shape=outs,
        in_specs=[HBM, HBM],
        out_specs=[VMEM] * len(outs),
        scratch_shapes=[
            pltpu.VMEM(spins.shape, spins.dtype),
            pltpu.SemaphoreType.DMA((len(spans),)),
            pltpu.SemaphoreType.DMA,
        ],
        compiler_params=limit(8),
        name="cut",
    )(in_hbm(seed), in_hbm(spins))
    return result[: len(spans)], result[len(spans) :]


def prepare(hop_matrix, pieces):
    sites = hop_matrix.shape[0]
    width = sum(piece.shape[1] for piece in pieces)
    square = jax.ShapeDtypeStruct((sites, sites), jnp.bfloat16)
    return pl.pallas_call(
        prepare_kernel,
        out_shape=[square] * 3 + [jax.ShapeDtypeStruct((width, sites), jnp.bfloat16)],
        in_specs=[VMEM] * (1 + len(pieces)),
        out_specs=[VMEM] * 4,
        compiler_params=limit(8),
        cost_estimate=pl.CostEstimate(flops=1 << 28, bytes_accessed=1 << 22, transcendentals=0),
        name="prepare",
    )(hop_matrix, *pieces)


def propagate(row_count, seed_t, high_t, low_t, lines):
    width, sites = seed_t.shape
    wraps = len(lines)
    return pl.pallas_call(
        functools.partial(own_kernel, row_count),
        out_shape=[
            jax.ShapeDtypeStruct((wraps, width, sites), jnp.bfloat16),
            jax.ShapeDtypeStruct((wraps, sites, LANES), jnp.float32),
        ],
        in_specs=[VMEM] * (3 + wraps),
        out_specs=[VMEM] * 2,
        compiler_params=limit(16),
        cost_estimate=pl.CostEstimate(
            flops=4 * wraps * sites * sites * width, bytes_accessed=1 << 22, transcendentals=0
        ),
        name="propagate",
    )(seed_t, high_t, low_t, *lines)


def work(columns, sites, wraps):
    return pl.CostEstimate(
        flops=2 * wraps * sites * sites * columns, bytes_accessed=1 << 22, transcendentals=0
    )


def levels(sites, columns):
    return [
        pltpu.VMEM((sites, columns), jnp.float32),
        pltpu.VMEM((2, sites, columns), jnp.bfloat16),
    ]


def chain(arrived, hop, scale, width):
    sites, columns = arrived.shape
    wraps = scale.shape[0]
    shape = jax.ShapeDtypeStruct((wraps, width, columns), jnp.bfloat16)
    return pl.pallas_call(
        chain_kernel,
        out_shape=[shape] * 2,
        in_specs=[VMEM] * 3,
        out_specs=[VMEM] * 2,
        scratch_shapes=levels(sites, columns),
        compiler_params=limit(16),
        cost_estimate=work(columns, sites, wraps),
        name="chain",
    )(arrived, hop, scale)


def add_up(offset, ours, theirs, turned, vertex):
    _, width, sites = turned.shape
    return pl.pallas_call(
        functools.partial(sum_kernel, offset),
        out_shape=jax.ShapeDtypeStruct((sites, width), jnp.float32),
        in_specs=[VMEM] * 4,
        out_specs=VMEM,
        compiler_params=limit(16),
        cost_estimate=work(ours.shape[2], sites, 2),
        name="add_up",
    )(ours, theirs, turned, vertex)


def finish(offset, *operands):
    ours, turned = operands[0], operands[2]
    wraps, width, sites = turned.shape
    blocks = 4
    return pl.pallas_call(
        functools.partial(finish_kernel, offset),
        out_shape=jax.ShapeDtypeStruct((sites, width), jnp.bfloat16),
        in_specs=[VMEM] * len(operands),
        out_specs=HBM,
        scratch_shapes=levels(sites, 2 * ours.shape[1])
        + [pltpu.VMEM((sites, width), jnp.bfloat16), pltpu.SemaphoreType.DMA((blocks,))],
        compiler_params=limit(16),
        cost_estimate=work(2 * ours.shape[1], sites, wraps),
        name="finish",
    )(*operands)


def fetch_lines(spins):
    rows, count = lax.axis_size("rowt"), len(spins)
    lines = [None] * count
    if rows == count and rows & (rows - 1) == 0:
        index = lax.axis_index("rowt")
        every = jnp.concatenate(spins, axis=0)
        for bits in range(1, rows):
            back = (index - (index ^ bits)) % rows
            line = lax.dynamic_slice_in_dim(every, back - 1, 1, 0)
            lines[bits - 1] = lax.ppermute(line, "rowt", [(i, i ^ bits) for i in range(rows)])
        came = jnp.concatenate(lines[:-1] + [spins[-1]], axis=0)
        ordered = [
            lax.dynamic_slice_in_dim(came, (index ^ (index + w) % rows) - 1, 1, 0)
            for w in range(1, rows)
        ]
        return ordered + [spins[-1]]
    for step, line in enumerate(spins):
        shift = (step + 1) % rows
        if shift:
            line = lax.ppermute(line, "rowt", [((i + shift) % rows, i) for i in range(rows)])
        lines[step] = line
    return lines


def per_device(seed_green, field_spins, hop_matrix, vertex):
    cols, sites = lax.axis_size("colt"), lax.axis_size("site")
    width = seed_green.shape[-1]
    edge = width - LANES
    across = [(i, (i + cols // 2) % cols) for i in range(cols)]
    swap = [(i, sites - 1 - i) for i in range(sites)]

    pieces, spins = cut(seed_green[0, 0], field_spins, [(0, edge), (edge, width)])
    first = lax.ppermute(pieces[0], "colt", across)
    second = lax.ppermute(pieces[1], "colt", across)
    lines = fetch_lines(spins)
    hop, high_t, low_t, seed_t = prepare(hop_matrix, pieces)
    turned, scale = propagate(lax.axis_size("rowt"), seed_t, high_t, low_t, lines)
    keep, send = chain(first, hop, scale, width)
    came = lax.ppermute(send, "site", swap)
    other = lax.ppermute(second, "site", swap)
    total = add_up(0, keep, came, turned, vertex)
    result = finish(edge, second, other, turned, hop, scale, vertex, total)
    return result[None, None]


def solution(mesh):
    return jax.shard_map(
        per_device,
        mesh=mesh,
        in_specs=(
            P(("groups", "rowt"), "colt", None, "site"),
            P(None, ("groups", "rowt"), None),
            P(),
            P(),
        ),
        out_specs=P(("groups", "rowt"), "colt", None, "site"),
        check_vma=False,
    )
```

time: 87.9 us -> 36.3 us (0.41)
  blocking collectives: 33.2 us -> 0 us
  matrix products: 24.8 us -> 0 us
  Pallas kernels: 0 us -> 15.7 us
  waiting for transfers between devices: 13.1 us -> 5.93 us
  local copies, waits for them, and re-layouts: 11.1 us -> 4.58 us
  starting transfers between devices: 4.05 us -> 8.99 us
    dot_general x8 -> x0, matrix products: 24.8 us -> none  [the longest x4 17.8 us: advance(): hopped = jnp.dot(hop_matrix, current, precision=lax.Precision.HIGHEST)]
    all_to_all x4 -> x0, blocking collectives: 18.4 us -> none  [measure(): lax.all_to_all(rounded, 'site', split_axis=0, concat_axis=1, tiled=True)]
    pallas_call x0 -> x6, Pallas kernels: none -> 15.7 us  [the longest x1 4.69 us: propagate(): pl.pallas_call(functools.partial(own_kernel, row_count), out_shape=[jax.S...]
    all_gather x1 -> x0, blocking collectives: 14.8 us -> none  [per_device(): all_weights = lax.all_gather(weights, 'rowt', axis=1, tiled=True)]
    ppermute x4 -> x7, waiting for transfers between devices: 13.1 us -> 5.93 us  [the longest x1 5.74 us: per_device(): second = lax.ppermute(pieces[1], 'colt', across)]
    all_to_all x4 -> x0, local copies, waits for them, and re-layouts: 6.42 us -> none  [measure(): lax.all_to_all(rounded, 'site', split_axis=0, concat_axis=1, tiled=True)]
    ppermute x4 -> x7, starting transfers between devices: 4.05 us -> 8.99 us  [the longest x3 5.64 us: fetch_lines(): lax.ppermute(line, 'rowt', [(i, i ^ bits) for i in range(rows)])]
    broadcast_in_dim x1 -> x0, local copies, waits for them, and re-layouts: 2.12 us -> none  [per_device(): return result[None, None]]
  transfers between devices with their start and end apart: 4 -> 7, of which waited for: 2 -> 3; matrix products, arithmetic and copies ran while one was open for 23% -> 2% of each run, Pallas kernels for 0% -> 19%
where the time goes in v1:
time: 36.3 us; the launch traced here: 36 us
  Pallas kernels  15.7 us (43%)
  starting transfers between devices  8.99 us (25%)
  waiting for transfers between devices  5.93 us (16%)
  local copies, waits for them, and re-layouts  4.58 us (13%)
  other arithmetic  0.73 us (2%)
    ppermute x1, waiting for transfers between devices, per_device(): second = lax.ppermute(pieces[1], 'colt', across)  5.74 us
    ppermute x3, starting transfers between devices, fetch_lines(): lax.ppermute(line, 'rowt', [(i, i ^ bits) for i in range(rows)])  5.64 us
    pallas_call x1, Pallas kernels, propagate(): pl.pallas_call(functools.partial(own_kernel, row_count), out_shape=[jax.S...  4.69 us
    unnamed x8, local copies, waits for them, and re-layouts  3.96 us
    pallas_call x1, Pallas kernels, finish(): pl.pallas_call(functools.partial(finish_kernel, offset), out_shape=jax.Sh...  3.89 us
    pallas_call x1, Pallas kernels, chain(): pl.pallas_call(chain_kernel, out_shape=[shape] * 2, in_specs=[VMEM] * 3,...  3.74 us
    ppermute x1, starting transfers between devices, per_device(): first = lax.ppermute(pieces[0], 'colt', across)  1.71 us
    ppermute x1, starting transfers between devices, per_device(): second = lax.ppermute(pieces[1], 'colt', across)  1.56 us
  transfers between devices with their start and end apart: 7, of which 3 were waited for; matrix products, arithmetic and copies ran while one was open for 2% of the time, Pallas kernels for 19%

profile of v1, /device:TPU:0, one launch (start us, length us, event | category | flops | bytes accessed | tf_op | source)
XLA Modules:
  0.0 36.0 jit_solution(9754539991294797235)
XLA Ops:
  0.0 1.1 %cut.1 = (bf16[768,256]{1,0:T(8,128)(2,1)S(1)}, bf16[768,128]{1,0:T(8,128)(2,1)S(1)}, bf16[1,768]{1,0:T(2,128)(2,1)S(1)}, bf16[1,768]{1,0:T(2,128)(2,1)S(1)}, bf...) custom-call(bf16[768,384]{1,0:T(8,128)(2,1)} %bitcast.2, s32[4,1,768]{2,1,0:T(1,128)} %spins_ref.1), custom_call_target="tpu_custom_call" | custom-call | tf_op jit(solution)/shard_map/cut/pallas_call | solution.py:190
  1.1 0.6 %constant_dynamic-slice_fusion.5 = (bf16[1,768]{1,0:T(2,128)(2,1)}, bf16[1,768]{1,0:T(2,128)(2,1)S(1)}, bf16[1,768]{1,0:T(2,128)(2,1)S(1)}) fusion(bf16[4,768]{1,0:T(4,128)(2,1)S(1)} %pad_maximum_fusion.1, s32[]{:T(128)S(6)} %select_n.46, s32[]{:T(128)S(6)} %select_n.50, s32[]{:T(128)S(6)} %select_n.48), kind=kLoop, calls=%fused_computation.7 | loop fusion | bytes 9228 | tf_op jit(solution)/shard_map/dynamic_slice | solution.py:307
  1.7 3.1 %collective-permute-start.2 = (bf16[1,768]{1,0:T(2,128)(2,1)}, bf16[1,768]{1,0:T(2,128)(2,1)S(1)}, u32[]{:S(2)}, u32[]{:S(2)}) collective-permute-start(bf16[1,768]{1,0:T(2,128)(2,1)} %get-tuple-element.36), channel_id=1, source_target_pairs={{0,4},{4,0},{8,12},{12,8},{1,5},{5,1},{9,13},{13,9},{2,6},{6,2},{1... | collective-permute-start | bytes 4616 | tf_op jit(solution)/shard_map/ppermute | solution.py:308
  4.8 2.6 %collective-permute-start.3 = (bf16[1,768]{1,0:T(2,128)(2,1)S(1)}, bf16[1,768]{1,0:T(2,128)(2,1)}, u32[]{:S(2)}, u32[]{:S(2)}) collective-permute-start(bf16[1,768]{1,0:T(2,128)(2,1)S(1)} %get-tuple-element.38), channel_id=1, source_target_pairs={{0,8},{4,12},{8,0},{12,4},{1,9},{5,13},{9,1},{13,5},{2,10},{6,14},... | collective-permute-start | bytes 4616 | tf_op jit(solution)/shard_map/ppermute | solution.py:308
  7.4 0.0 collective-permute-start.4
  7.4 1.7 %collective-permute-start.5 = (bf16[768,256]{1,0:T(8,128)(2,1)S(1)}, bf16[768,256]{1,0:T(8,128)(2,1)}, u32[]{:S(2)}, u32[]{:S(2)}) collective-permute-start(bf16[768,256]{1,0:T(8,128)(2,1)S(1)} %get-tuple-element.20.refs_0_), channel_id=1, source_target_pairs={{0,2},{2,0},{1,3},{3,1},{4,6},{6,4},{5,7},{7,5},{8,10},{10,8},{9,1... | collective-permute-start | bytes 1179656 | tf_op jit(solution)/shard_map/ppermute | solution.py:331
  9.1 0.0 copy-start.1
  9.1 1.7 %copy-done.1 = f32[768,768]{1,0:T(8,128)S(1)} copy-done((f32[768,768]{1,0:T(8,128)S(1)}, f32[768,768]{1,0:T(8,128)}, u32[]{:S(2)}) %copy-start.1) | copy-done | bytes 2359320
  10.7 1.0 %prepare.1 = (bf16[768,768]{1,0:T(8,128)(2,1)S(1)}, bf16[768,768]{1,0:T(8,128)(2,1)S(1)}, bf16[768,768]{1,0:T(8,128)(2,1)S(1)}, bf16[384,768]{1,0:T(8,128)(2,1)S(1)}) custom-call(f32[768,768]{1,0:T(8,128)S(1)} %copy-done.1, bf16[768,256]{1,0:T(8,128)(2,1)S(1)} %get-tuple-element.20.refs_0_, bf16[768,128]{1,0:T(8,128)(2,1)S(1)} %get-tuple-element.19.refs_1_), custom_call_target="tpu_custom_call" | custom-call | flops 268435456 | bytes 4194304 | tf_op jit(solution)/shard_map/prepare/pallas_call | solution.py:210
  11.8 0.0 copy-start.2
  11.8 1.0 %copy-done.2 = bf16[768,768]{1,0:T(8,128)(2,1)} copy-done((bf16[768,768]{1,0:T(8,128)(2,1)}, bf16[768,768]{1,0:T(8,128)(2,1)S(1)}, u32[]{:S(2)}) %copy-start.2) | copy-done | bytes 1179672
  12.8 0.0 collective-permute-done.2
  12.8 0.0 collective-permute-done.3
  12.8 0.1 collective-permute-done.4
  12.9 0.7 %pad_maximum_fusion = bf16[4,768]{1,0:T(4,128)(2,1)S(1)} fusion(bf16[1,768]{1,0:T(2,128)(2,1)S(1)} %get-tuple-element.27.refs_3_, bf16[1,768]{1,0:T(2,128)(2,1)} %collective-permute-done.4, bf16[1,768]{1,0:T(2,128)(2,1)} %collective-permute-done.3, bf16[1,768]{1,0:T(2,128)(2,1)S(1)} %collective-permute-done.2), kind=kLoop, calls=%fused_computation | loop fusion | flops 24576 | bytes 12288 | tf_op jit(solution)/shard_map/concatenate | solution.py:309
  13.6 0.0 copy-start.3
  13.6 1.3 %copy-done.3 = bf16[768,768]{1,0:T(8,128)(2,1)S(1)} copy-done((bf16[768,768]{1,0:T(8,128)(2,1)S(1)}, bf16[768,768]{1,0:T(8,128)(2,1)}, u32[]{:S(2)}) %copy-start.3) | copy-done | bytes 1179672
  14.9 4.7 %propagate.1 = (bf16[4,384,768]{2,1,0:T(8,128)(2,1)S(1)}, f32[4,768,128]{2,1,0:T(8,128)S(1)}) custom-call(bf16[384,768]{1,0:T(8,128)(2,1)S(1)} %get-tuple-element.21.seed_t, bf16[768,768]{1,0:T(8,128)(2,1)S(1)} %get-tuple-element.22.high_t, bf16[768,768]{1,0:T(8,128)(2,1)S(1)} %copy-done.3, bf16[1,768]{1,0:T(2,128)(2,1)S(1)} %get-tuple-element.35.refs_0_, ...), custom_call_target="tpu_custom_call" | custom-call | flops 3623878656 | bytes 4194304 | tf_op jit(solution)/shard_map/propagate/pallas_call | solution.py:224
  19.6 0.0 collective-permute-done.5.arrived
  19.6 0.0 copy-start
  19.6 3.7 %chain.1 = (bf16[4,384,256]{2,1,0:T(8,128)(2,1)S(1)}, bf16[4,384,256]{2,1,0:T(8,128)(2,1)S(1)}) custom-call(bf16[768,256]{1,0:T(8,128)(2,1)} %collective-permute-done.5.arrived, bf16[768,768]{1,0:T(8,128)(2,1)S(1)} %get-tuple-element.29.hop_ref.refs_3_, f32[4,768,128]{2,1,0:T(8,128)S(1)} %get-tuple-element.30.scale_ref.refs_4_), custom_call_target="tpu_custom_call" | custom-call | flops 1207959552 | bytes 4194304 | tf_op jit(solution)/shard_map/chain/pallas_call | solution.py:257
  23.3 0.1 collective-permute-start.6
  23.4 1.6 %collective-permute-start = (bf16[768,128]{1,0:T(8,128)(2,1)S(1)}, bf16[768,128]{1,0:T(8,128)(2,1)S(1)}, u32[]{:S(2)}, u32[]{:S(2)}) collective-permute-start(bf16[768,128]{1,0:T(8,128)(2,1)S(1)} %get-tuple-element.19.refs_1_), channel_id=1, source_target_pairs={{0,2},{2,0},{1,3},{3,1},{4,6},{6,4},{5,7},{7,5},{8,10},{10,8},{9,1... | collective-permute-start | bytes 589832 | tf_op jit(solution)/shard_map/ppermute | solution.py:332
  25.0 5.7 %collective-permute-done.refs_0_ = bf16[768,128]{1,0:T(8,128)(2,1)S(1)} collective-permute-done((bf16[768,128]{1,0:T(8,128)(2,1)S(1)}, bf16[768,128]{1,0:T(8,128)(2,1)S(1)}, u32[]{:S(2)}, u32[]{:S(2)}) %collective-permute-start) | collective-permute-done | bytes 196640 | tf_op jit(solution)/shard_map/ppermute | solution.py:332
  30.7 0.0 collective-permute-start.1
  30.7 0.0 collective-permute-done.6.theirs
  30.7 0.0 copy-done
  30.7 1.3 %add_up.1.refs_6_ = f32[768,384]{1,0:T(8,128)S(1)} custom-call(bf16[4,384,256]{2,1,0:T(8,128)(2,1)S(1)} %get-tuple-element.31.ours, bf16[4,384,256]{2,1,0:T(8,128)(2,1)S(1)} %collective-permute-done.6.theirs, bf16[4,384,768]{2,1,0:T(8,128)(2,1)S(1)} %get-tuple-element.28.turned_ref.refs_2_, bf16[768,768]{1,0:T(8,128)(2,1)S(1)} %copy-done), custom_call_target="tpu_custom_call" | custom-call | flops 603979776 | bytes 4194304 | tf_op jit(solution)/shard_map/add_up/pallas_call | solution.py:271
  32.0 0.1 collective-permute-done.1.refs_1_
  32.1 3.9 %finish.1 = bf16[768,384]{1,0:T(8,128)(2,1)} custom-call(bf16[768,128]{1,0:T(8,128)(2,1)S(1)} %collective-permute-done.refs_0_, bf16[768,128]{1,0:T(8,128)(2,1)S(1)} %collective-permute-done.1.refs_1_, bf16[4,384,768]{2,1,0:T(8,128)(2,1)S(1)} %get-tuple-element.28.turned_ref.refs_2_, bf16[768,768]{1,0:T(8,128)(2,1)S(1)} %get-tuple-element.29.hop_ref.refs_3_, ...), custom_call_target="tpu_custom_call" | custom-call | flops 1207959552 | bytes 4194304 | tf_op jit(solution)/shard_map/finish/pallas_call | solution.py:286
  (2 shorter events, 0.0 us)
Async XLA Ops:
  1.7 11.1 %collective-permute-start.2 = (bf16[1,768]{1,0:T(2,128)(2,1)}, bf16[1,768]{1,0:T(2,128)(2,1)S(1)}, u32[]{:S(2)}, u32[]{:S(2)}) collective-permute-start(bf16[1,768]{1,0:T(2,128)(2,1)} %get-tuple-element.36), channel_id=1, source_target_pairs={{0,4},{4,0},{8,12},{12,8},{1,5},{5,1},{9,13},{13,9},{2,6},{6,2},{1... | collective-permute-start | bytes 4616 | tf_op jit(solution)/shard_map/ppermute | solution.py:308
  4.8 8.0 %collective-permute-start.3 = (bf16[1,768]{1,0:T(2,128)(2,1)S(1)}, bf16[1,768]{1,0:T(2,128)(2,1)}, u32[]{:S(2)}, u32[]{:S(2)}) collective-permute-start(bf16[1,768]{1,0:T(2,128)(2,1)S(1)} %get-tuple-element.38), channel_id=1, source_target_pairs={{0,8},{4,12},{8,0},{12,4},{1,9},{5,13},{9,1},{13,5},{2,10},{6,14},... | collective-permute-start | bytes 4616 | tf_op jit(solution)/shard_map/ppermute | solution.py:308
  7.4 5.5 %collective-permute-start.4 = (bf16[1,768]{1,0:T(2,128)(2,1)S(1)}, bf16[1,768]{1,0:T(2,128)(2,1)}, u32[]{:S(2)}, u32[]{:S(2)}) collective-permute-start(bf16[1,768]{1,0:T(2,128)(2,1)S(1)} %get-tuple-element.37), channel_id=1, source_target_pairs={{0,12},{4,8},{8,4},{12,0},{1,13},{5,9},{9,5},{13,1},{2,14},{6,10},... | collective-permute-start | bytes 4616 | tf_op jit(solution)/shard_map/ppermute | solution.py:308
  7.4 12.2 %collective-permute-start.5 = (bf16[768,256]{1,0:T(8,128)(2,1)S(1)}, bf16[768,256]{1,0:T(8,128)(2,1)}, u32[]{:S(2)}, u32[]{:S(2)}) collective-permute-start(bf16[768,256]{1,0:T(8,128)(2,1)S(1)} %get-tuple-element.20.refs_0_), channel_id=1, source_target_pairs={{0,2},{2,0},{1,3},{3,1},{4,6},{6,4},{5,7},{7,5},{8,10},{10,8},{9,1... | collective-permute-start | bytes 1179656 | tf_op jit(solution)/shard_map/ppermute | solution.py:331
  9.1 1.7 %copy-start.1 = (f32[768,768]{1,0:T(8,128)S(1)}, f32[768,768]{1,0:T(8,128)}, u32[]{:S(2)}) copy-start(f32[768,768]{1,0:T(8,128)} %hop_ref.1) | copy-start | bytes 7077892
  11.8 1.0 %copy-start.2 = (bf16[768,768]{1,0:T(8,128)(2,1)}, bf16[768,768]{1,0:T(8,128)(2,1)S(1)}, u32[]{:S(2)}) copy-start(bf16[768,768]{1,0:T(8,128)(2,1)S(1)} %get-tuple-element.23.low_t) | copy-start | bytes 3538948
  13.6 1.3 %copy-start.3 = (bf16[768,768]{1,0:T(8,128)(2,1)S(1)}, bf16[768,768]{1,0:T(8,128)(2,1)}, u32[]{:S(2)}) copy-start(bf16[768,768]{1,0:T(8,128)(2,1)} %copy-done.2) | copy-start | bytes 3538948
  19.6 11.2 %copy-start = (bf16[768,768]{1,0:T(8,128)(2,1)S(1)}, bf16[768,768]{1,0:T(8,128)(2,1)}, u32[]{:S(2)}) copy-start(bf16[768,768]{1,0:T(8,128)(2,1)} %refs_5_.1) | copy-start | bytes 3538948
  23.3 7.4 %collective-permute-start.6 = (bf16[4,384,256]{2,1,0:T(8,128)(2,1)S(1)}, bf16[4,384,256]{2,1,0:T(8,128)(2,1)S(1)}, u32[]{:S(2)}, u32[]{:S(2)}) collective-permute-start(bf16[4,384,256]{2,1,0:T(8,128)(2,1)S(1)} %get-tuple-element.32), channel_id=1, source_target_pairs={{0,1},{1,0},{2,3},{3,2},{4,5},{5,4},{6,7},{7,6},{8,9},{9,8},{10,11... | collective-permute-start | bytes 2359304 | tf_op jit(solution)/shard_map/ppermute | solution.py:337
  23.4 7.3 %collective-permute-start = (bf16[768,128]{1,0:T(8,128)(2,1)S(1)}, bf16[768,128]{1,0:T(8,128)(2,1)S(1)}, u32[]{:S(2)}, u32[]{:S(2)}) collective-permute-start(bf16[768,128]{1,0:T(8,128)(2,1)S(1)} %get-tuple-element.19.refs_1_), channel_id=1, source_target_pairs={{0,2},{2,0},{1,3},{3,1},{4,6},{6,4},{5,7},{7,5},{8,10},{10,8},{9,1... | collective-permute-start | bytes 589832 | tf_op jit(solution)/shard_map/ppermute | solution.py:332
  30.7 1.4 %collective-permute-start.1 = (bf16[768,128]{1,0:T(8,128)(2,1)S(1)}, bf16[768,128]{1,0:T(8,128)(2,1)S(1)}, u32[]{:S(2)}, u32[]{:S(2)}) collective-permute-start(bf16[768,128]{1,0:T(8,128)(2,1)S(1)} %collective-permute-done.refs_0_), channel_id=1, source_target_pairs={{0,1},{1,0},{2,3},{3,2},{4,5},{5,4},{6,7},{7,6},{8,9},{9,8},{10,11... | collective-permute-start | bytes 589832 | tf_op jit(solution)/shard_map/ppermute | solution.py:338

commit v2 on v1

--- a/solution.py
+++ b/solution.py
@@ -32,62 +32,92 @@
     return high, low
 
 
+def site_spans(width):
+    site = lax.axis_index("site")
+    places = (site, lax.axis_size("site") - 1 - site)
+    return [pl.ds(pl.multiple_of(place * width, LANES), width) for place in places]
+
+
 def cut_kernel(spans, seed_ref, spins_ref, *refs):
-    pieces, lines = refs[: len(spans)], refs[len(spans) : -3]
+    pieces, lines = refs[: len(spans)], refs[len(spans)]
     spins_in, piece_sems, spin_sem = refs[-3:]
+    width = seed_ref.shape[1]
+    sources = site_spans(width)
+    copies = []
+    for (a, b), piece in zip(spans, pieces):
+        for half, source in enumerate(sources):
+            copy = pltpu.make_async_copy(
+                seed_ref.at[source, pl.ds(a, b - a)],
+                piece.at[pl.ds(half * width, width)],
+                piece_sems.at[len(copies)],
+            )
+            copy.start()
+            copies.append(copy)
     spin_copy = pltpu.make_async_copy(spins_ref, spins_in, spin_sem)
-    copies = [
-        pltpu.make_async_copy(seed_ref.at[:, pl.ds(a, b - a)], piece, piece_sems.at[number])
-        for number, ((a, b), piece) in enumerate(zip(spans, pieces))
-    ]
-    for copy in copies:
-        copy.start()
     spin_copy.start()
     spin_copy.wait()
-    for step, line in enumerate(lines):
-        line[...] = spins_in[step].astype(jnp.float32).astype(jnp.bfloat16)
+    parts = []
+    for step in range(lines.shape[0]):
+        parts.append(
+            jnp.concatenate([spins_in[step, :, source] for source in sources], axis=1)
+        )
+    lines[...] = jnp.concatenate(parts, axis=0).astype(jnp.float32).astype(jnp.bfloat16)
     for copy in copies:
         copy.wait()
+
+
+def hold_kernel(lines_ref, out_ref):
+    out_ref[...] = lines_ref[...]
 
 
 def prepare_kernel(hop_ref, *refs):
     pieces = refs[:-4]
     hop_out, high_t, low_t, turned_out = refs[-4:]
+    width, _ = turned_out.shape
     start = 0
     for piece in pieces:
         turned_out[start : start + piece.shape[1], :] = piece[...].T
         start += piece.shape[1]
-    for start in range(0, hop_ref.shape[0], LANES):
-        span = slice(start, start + LANES)
-        high, low = split_halves(hop_share * hop_ref[span, :])
-        hop_out[span, :] = high
-        high_t[:, span] = high.T
-        low_t[:, span] = low.T
-
-
-def own_kernel(row_count, seed_t, high_t, low_t, *refs):
+    site = lax.axis_index("site")
+    places = (site, lax.axis_size("site") - 1 - site)
+    for half, place in enumerate(places):
+        for start in range(0, width, LANES):
+            rows = pl.ds(pl.multiple_of(place * width + start, LANES), LANES)
+            strip = jnp.concatenate([hop_ref[rows, span] for span in site_spans(width)], axis=1)
+            high, low = split_halves(hop_share * strip)
+            spot = slice(half * width + start, half * width + start + LANES)
+            hop_out[spot, :] = high
+            high_t[:, spot] = high.T
+            low_t[:, spot] = low.T
+
+
+def hop_turned(narrow, high_t, low_t):
+    hopped = jnp.dot(narrow, high_t[...], preferred_element_type=jnp.float32)
+    return hopped + jnp.dot(narrow, low_t[...], preferred_element_type=jnp.float32)
+
+
+def lift_kernel(seed_t, high_t, low_t, image_out):
+    narrow = seed_t[...]
+    hopped = hop_turned(narrow, high_t, low_t)
+    image_out[...] = keep_share * narrow.astype(jnp.float32) + hopped
+
+
+def own_kernel(row_count, image_ref, high_t, low_t, *refs):
     wraps = len(refs) - 2
     turned_out, scale_out = refs[wraps:]
     row_index = lax.axis_index("rowt")
-    turned = seed_t[...].astype(jnp.float32)
-    narrow = seed_t[...]
+    image = image_ref[...]
     for step in range(wraps):
         spins = refs[step][...].astype(jnp.float32)
         sign = jnp.where((row_index + step + 1) % row_count == 0, -1.0, 1.0)
         scale = sign * jnp.exp(coupling * (2.0 * spins - 1.0))
         column = jnp.broadcast_to(scale, (8, scale.shape[1])).T[:, :1]
         scale_out[step] = jnp.broadcast_to(column, scale_out.shape[1:])
-        hopped = jnp.dot(narrow, high_t[...], preferred_element_type=jnp.float32)
-        hopped += jnp.dot(narrow, low_t[...], preferred_element_type=jnp.float32)
-        turned = scale * (keep_share * turned + hopped)
+        turned = scale * image
         narrow = turned.astype(jnp.bfloat16)
         turned_out[step] = narrow
-
-
-def site_spans(width):
-    site = lax.axis_index("site")
-    places = (site, lax.axis_size("site") - 1 - site)
-    return [pl.ds(pl.multiple_of(place * width, LANES), width) for place in places]
+        if step < wraps - 1:
+            image = keep_share * turned + hop_turned(narrow, high_t, low_t)
 
 
 def advance(step, spans, hop_ref, scale_ref, level, narrow):
@@ -104,7 +134,8 @@
 
 
 def chain_kernel(arrived, hop_ref, scale_ref, keep_out, send_out, level, narrow):
-    spans = site_spans(keep_out.shape[1])
+    width = keep_out.shape[1]
+    spans = [slice(0, width), slice(width, 2 * width)]
     narrow[0] = arrived[...]
     level[...] = arrived[...].astype(jnp.float32)
     for step in range(keep_out.shape[0]):
@@ -121,16 +152,17 @@
 def columns_at(offset, part, width):
     site = lax.axis_index("site")
     places = (site, lax.axis_size("site") - 1 - site)
-    return [pl.ds(pl.multiple_of(place * width + offset, LANES), part) for place in places]
+    held = [slice(offset, offset + part), slice(width + offset, width + offset + part)]
+    return held, [pl.ds(pl.multiple_of(p * width + offset, LANES), part) for p in places]
 
 
 def sum_kernel(offset, ours, theirs, turned_ref, vertex_ref, out_ref):
     wraps, width, _ = turned_ref.shape
     total = None
-    for met_ref, spot in zip((ours, theirs), columns_at(offset, ours.shape[2], width)):
+    for met_ref, held, spot in zip((ours, theirs), *columns_at(offset, ours.shape[2], width)):
         pairs = None
         for step in range(wraps):
-            product = multiply(met_ref[step], turned_ref[step, :, spot])
+            product = multiply(met_ref[step], turned_ref[step, :, held])
             pairs = product if pairs is None else pairs + product
         for half in split_halves(pairs):
             part = lax.dot_general(
@@ -147,16 +179,17 @@
     ours, theirs, turned_ref, hop_ref, scale_ref, vertex_ref, total_ref = refs[:7]
     out_ref, level, narrow, result, sems = refs[7:]
     wraps, width, sites = turned_ref.shape
-    spans = site_spans(width)
-    spots = columns_at(offset, ours.shape[1], width)
-    arrived = jnp.concatenate([ours[...], theirs[...]], axis=1)
+    spans = [slice(0, width), slice(width, 2 * width)]
+    held, spots = columns_at(offset, ours.shape[1], width)
+    other = jnp.concatenate([theirs[span, :] for span in reversed(spans)], axis=0)
+    arrived = jnp.concatenate([ours[...], other], axis=1)
     narrow[0] = arrived
     level[...] = arrived.astype(jnp.float32)
     pairs = None
     for step in range(wraps):
         needed = spans if step < wraps - 1 else spans[:1]
         met = list(advance(step, needed, hop_ref, scale_ref, level, narrow))[0]
-        own = jnp.concatenate([turned_ref[step, :, spot] for spot in spots], axis=1)
+        own = jnp.concatenate([turned_ref[step, :, span] for span in held], axis=1)
         product = multiply(met, own)
         pairs = product if pairs is None else pairs + product
     halves = split_halves(pairs)
@@ -186,21 +219,33 @@
 def cut(seed, spins, spans):
     wraps, sites = spins.shape[0], seed.shape[0]
     outs = [jax.ShapeDtypeStruct((sites, b - a), jnp.bfloat16) for a, b in spans]
-    outs += [jax.ShapeDtypeStruct((1, sites), jnp.bfloat16)] * wraps
-    result = pl.pallas_call(
+    outs.append(jax.ShapeDtypeStruct((wraps, sites), jnp.bfloat16))
+    *pieces, lines = pl.pallas_call(
         functools.partial(cut_kernel, spans),
         out_shape=outs,
         in_specs=[HBM, HBM],
         out_specs=[VMEM] * len(outs),
         scratch_shapes=[
             pltpu.VMEM(spins.shape, spins.dtype),
-            pltpu.SemaphoreType.DMA((len(spans),)),
+            pltpu.SemaphoreType.DMA((2 * len(spans),)),
             pltpu.SemaphoreType.DMA,
         ],
         compiler_params=limit(8),
         name="cut",
     )(in_hbm(seed), in_hbm(spins))
-    return result[: len(spans)], result[len(spans) :]
+    return pieces, lines
+
+
+def hold(lines):
+    return pl.pallas_call(
+        hold_kernel,
+        out_shape=jax.ShapeDtypeStruct(lines.shape, lines.dtype),
+        in_specs=[VMEM],
+        out_specs=VMEM,
+        compiler_params=limit(4),
+        cost_estimate=pl.CostEstimate(flops=1 << 32, bytes_accessed=1 << 24, transcendentals=0),
+        name="hold",
+    )(lines)
 
 
 def prepare(hop_matrix, pieces):
@@ -218,8 +263,21 @@
     )(hop_matrix, *pieces)
 
 
-def propagate(row_count, seed_t, high_t, low_t, lines):
+def lift(seed_t, high_t, low_t):
     width, sites = seed_t.shape
+    return pl.pallas_call(
+        lift_kernel,
+        out_shape=jax.ShapeDtypeStruct((width, sites), jnp.float32),
+        in_specs=[VMEM] * 3,
+        out_specs=VMEM,
+        compiler_params=limit(16),
+        cost_estimate=work(width, sites, 2),
+        name="lift",
+    )(seed_t, high_t, low_t)
+
+
+def propagate(row_count, image, high_t, low_t, lines):
+    width, sites = image.shape
     wraps = len(lines)
     return pl.pallas_call(
         functools.partial(own_kernel, row_count),
@@ -230,11 +288,9 @@
         in_specs=[VMEM] * (3 + wraps),
         out_specs=[VMEM] * 2,
         compiler_params=limit(16),
-        cost_estimate=pl.CostEstimate(
-            flops=4 * wraps * sites * sites * width, bytes_accessed=1 << 22, transcendentals=0
-        ),
+        cost_estimate=work(width, sites, 2 * (wraps - 1)),
         name="propagate",
-    )(seed_t, high_t, low_t, *lines)
+    )(image, high_t, low_t, *lines)
 
 
 def work(columns, sites, wraps):
@@ -282,7 +338,7 @@
 def finish(offset, *operands):
     ours, turned = operands[0], operands[2]
     wraps, width, sites = turned.shape
-    blocks = 4
+    blocks = 2
     return pl.pallas_call(
         functools.partial(finish_kernel, offset),
         out_shape=jax.ShapeDtypeStruct((sites, width), jnp.bfloat16),
@@ -296,28 +352,25 @@
     )(*operands)
 
 
-def fetch_lines(spins):
-    rows, count = lax.axis_size("rowt"), len(spins)
-    lines = [None] * count
+def fetch_lines(lines):
+    rows, count = lax.axis_size("rowt"), lines.shape[0]
     if rows == count and rows & (rows - 1) == 0:
+        bit = 1
+        while bit < rows:
+            came = lax.ppermute(lines, "rowt", [(i, i ^ bit) for i in range(rows)])
+            lines = jnp.concatenate([lines, came], axis=0)
+            bit *= 2
         index = lax.axis_index("rowt")
-        every = jnp.concatenate(spins, axis=0)
-        for bits in range(1, rows):
-            back = (index - (index ^ bits)) % rows
-            line = lax.dynamic_slice_in_dim(every, back - 1, 1, 0)
-            lines[bits - 1] = lax.ppermute(line, "rowt", [(i, i ^ bits) for i in range(rows)])
-        came = jnp.concatenate(lines[:-1] + [spins[-1]], axis=0)
-        ordered = [
-            lax.dynamic_slice_in_dim(came, (index ^ (index + w) % rows) - 1, 1, 0)
-            for w in range(1, rows)
-        ]
-        return ordered + [spins[-1]]
-    for step, line in enumerate(spins):
-        shift = (step + 1) % rows
+        picks = [(index ^ (index + w) % rows) * count + w - 1 for w in range(1, rows)]
+        found = [lax.dynamic_slice_in_dim(lines, pick, 1, 0) for pick in picks]
+        return found + [lines[count - 1 : count]]
+    found = []
+    for step in range(count):
+        line, shift = lines[step : step + 1], (step + 1) % rows
         if shift:
             line = lax.ppermute(line, "rowt", [((i + shift) % rows, i) for i in range(rows)])
-        lines[step] = line
-    return lines
+        found.append(line)
+    return found
 
 
 def per_device(seed_green, field_spins, hop_matrix, vertex):
@@ -327,12 +380,13 @@
     across = [(i, (i + cols // 2) % cols) for i in range(cols)]
     swap = [(i, sites - 1 - i) for i in range(sites)]
 
-    pieces, spins = cut(seed_green[0, 0], field_spins, [(0, edge), (edge, width)])
+    pieces, lines = cut(seed_green[0, 0], field_spins, [(0, edge), (edge, width)])
     first = lax.ppermute(pieces[0], "colt", across)
     second = lax.ppermute(pieces[1], "colt", across)
-    lines = fetch_lines(spins)
+    lines = fetch_lines(hold(lines))
     hop, high_t, low_t, seed_t = prepare(hop_matrix, pieces)
-    turned, scale = propagate(lax.axis_size("rowt"), seed_t, high_t, low_t, lines)
+    image = lift(seed_t, high_t, low_t)
+    turned, scale = propagate(lax.axis_size("rowt"), image, high_t, low_t, lines)
     keep, send = chain(first, hop, scale, width)
     came = lax.ppermute(send, "site", swap)
     other = lax.ppermute(second, "site", swap)

time: 36.3 us -> 35.1 us (0.967)
  local copies, waits for them, and re-layouts: 4.58 us -> 2.36 us
  starting transfers between devices: 8.99 us -> 7.84 us
  waiting for transfers between devices: 5.93 us -> 7.03 us
  other arithmetic: 0.73 us -> 1.33 us
  Pallas kernels: 15.7 us -> 16.1 us
    unnamed x8 -> x14, local copies, waits for them, and re-layouts: 3.96 us -> 2.32 us
    pallas_call x1, Pallas kernels: 4.69 us -> 3.54 us  [propagate(): pl.pallas_call(functools.partial(own_kernel, row_count), out_shape=[jax.S...]
    pallas_call x0 -> x2, Pallas kernels: none -> 1.1 us  [the longest x1 1.09 us: lift(): pl.pallas_call(lift_kernel, out_shape=jax.ShapeDtypeStruct((width, sites)...]
    pallas_call x1, Pallas kernels: 1.02 us -> 2.07 us  [prepare(): pl.pallas_call(prepare_kernel, out_shape=[square] * 3 + [jax.ShapeDtypeSt...]
    ppermute x1, starting transfers between devices: 1.56 us -> 0.57 us  [per_device(): second = lax.ppermute(pieces[1], 'colt', across)]
    ppermute x1, waiting for transfers between devices: 5.74 us -> 6.72 us  [per_device(): second = lax.ppermute(pieces[1], 'colt', across)]
    pallas_call x1, Pallas kernels: 1.07 us -> 1.92 us  [cut(): pl.pallas_call(functools.partial(cut_kernel, spans), out_shape=outs, in_s...]
    pallas_call x1, Pallas kernels: 3.74 us -> 2.91 us  [chain(): pl.pallas_call(chain_kernel, out_shape=[shape] * 2, in_specs=[VMEM] * 3,...]
  transfers between devices with their start and end apart: 7 -> 6, of which waited for: 3 -> 3; matrix products, arithmetic and copies ran while one was open for 2% -> 4% of each run, Pallas kernels for 19% -> 23%
where the time goes in v2:
time: 35.1 us; the launch traced here: 34.8 us
  Pallas kernels  16.1 us (46%)
  starting transfers between devices  7.84 us (22%)
  waiting for transfers between devices  7.03 us (20%)
  local copies, waits for them, and re-layouts  2.36 us (7%)
  other arithmetic  1.33 us (4%)
    ppermute x1, waiting for transfers between devices, per_device(): second = lax.ppermute(pieces[1], 'colt', across)  6.72 us
    ppermute x2, starting transfers between devices, fetch_lines(): came = lax.ppermute(lines, 'rowt', [(i, i ^ bit) for i in range(rows)])  5.71 us
    pallas_call x1, Pallas kernels, propagate(): pl.pallas_call(functools.partial(own_kernel, row_count), out_shape=[jax.S...  3.54 us
    pallas_call x1, Pallas kernels, finish(): pl.pallas_call(functools.partial(finish_kernel, offset), out_shape=jax.Sh...  3.2 us
    pallas_call x1, Pallas kernels, chain(): pl.pallas_call(chain_kernel, out_shape=[shape] * 2, in_specs=[VMEM] * 3,...  2.91 us
    unnamed x14, local copies, waits for them, and re-layouts  2.32 us
    pallas_call x1, Pallas kernels, prepare(): pl.pallas_call(prepare_kernel, out_shape=[square] * 3 + [jax.ShapeDtypeSt...  2.07 us
    pallas_call x1, Pallas kernels, cut(): pl.pallas_call(functools.partial(cut_kernel, spans), out_shape=outs, in_s...  1.92 us
  transfers between devices with their start and end apart: 6, of which 3 were waited for; matrix products, arithmetic and copies ran while one was open for 4% of the time, Pallas kernels for 23%

profile of v2, /device:TPU:0, one launch (start us, length us, event | category | flops | bytes accessed | tf_op | source)
XLA Modules:
  0.0 34.8 jit_solution(17702944792741527125)
XLA Ops:
  0.0 1.9 %cut.1 = (bf16[768,256]{1,0:T(8,128)(2,1)}, bf16[768,128]{1,0:T(8,128)(2,1)S(1)}, bf16[4,768]{1,0:T(4,128)(2,1)S(1)}) custom-call(bf16[768,384]{1,0:T(8,128)(2,1)} %bitcast.2, s32[4,1,768]{2,1,0:T(1,128)} %spins_ref.1), custom_call_target="tpu_custom_call" | custom-call | tf_op jit(solution)/shard_map/cut/pallas_call | solution.py:223
  1.9 0.0 copy-start.4
  1.9 0.0 copy-start.1
  2.0 3.1 %collective-permute-start.2 = (bf16[4,768]{1,0:T(4,128)(2,1)S(1)}, bf16[4,768]{1,0:T(4,128)(2,1)S(1)}, u32[]{:S(2)}, u32[]{:S(2)}) collective-permute-start(bf16[4,768]{1,0:T(4,128)(2,1)S(1)} %hold.1), channel_id=1, source_target_pairs={{0,4},{4,0},{8,12},{12,8},{1,5},{5,1},{9,13},{13,9},{2,6},{6,2},{1... | collective-permute-start | bytes 18440 | tf_op jit(solution)/shard_map/ppermute | solution.py:360
  5.1 1.5 %collective-permute-start.4 = (bf16[768,256]{1,0:T(8,128)(2,1)}, bf16[768,256]{1,0:T(8,128)(2,1)}, u32[]{:S(2)}, u32[]{:S(2)}) collective-permute-start(bf16[768,256]{1,0:T(8,128)(2,1)} %get-tuple-element.17.refs_0_), channel_id=1, source_target_pairs={{0,2},{2,0},{1,3},{3,1},{4,6},{6,4},{5,7},{7,5},{8,10},{10,8},{9,1... | collective-permute-start | bytes 1179656 | tf_op jit(solution)/shard_map/ppermute | solution.py:384
  6.6 0.0 copy-done.4
  6.6 0.0 copy-done.1
  6.6 2.1 %prepare.1 = (bf16[768,768]{1,0:T(8,128)(2,1)S(1)}, bf16[768,768]{1,0:T(8,128)(2,1)S(1)}, bf16[768,768]{1,0:T(8,128)(2,1)S(1)}, bf16[384,768]{1,0:T(8,128)(2,1)S(1)}) custom-call(f32[768,768]{1,0:T(8,128)S(1)} %copy-done.1, bf16[768,256]{1,0:T(8,128)(2,1)} %get-tuple-element.17.refs_0_, bf16[768,128]{1,0:T(8,128)(2,1)S(1)} %get-tuple-element.16.refs_1_), custom_call_target="tpu_custom_call" | custom-call | flops 268435456 | bytes 4194304 | tf_op jit(solution)/shard_map/prepare/pallas_call | solution.py:255
  8.7 0.0 collective-permute-done.2
  8.7 0.0 copy-start.6
  8.7 0.6 %pad_maximum_fusion.1 = bf16[8,768]{1,0:T(8,128)(2,1)} fusion(bf16[4,768]{1,0:T(4,128)(2,1)S(1)} %collective-permute-done.2, bf16[4,768]{1,0:T(4,128)(2,1)S(1)} %hold.1), kind=kLoop, calls=%fused_computation.1 | loop fusion | flops 24576 | bytes 24576 | tf_op jit(solution)/shard_map/concatenate | solution.py:361
  9.3 2.6 %collective-permute-start.3 = (bf16[8,768]{1,0:T(8,128)(2,1)}, bf16[8,768]{1,0:T(8,128)(2,1)}, u32[]{:S(2)}, u32[]{:S(2)}) collective-permute-start(bf16[8,768]{1,0:T(8,128)(2,1)} %pad_maximum_fusion.1), channel_id=1, source_target_pairs={{0,8},{4,12},{8,0},{12,4},{1,9},{5,13},{9,1},{13,5},{2,10},{6,14},... | collective-permute-start | bytes 36872 | tf_op jit(solution)/shard_map/ppermute | solution.py:360
  11.9 0.0 copy-done.6
  11.9 1.1 %lift.1.image_ref = f32[384,768]{1,0:T(8,128)S(1)} custom-call(bf16[384,768]{1,0:T(8,128)(2,1)S(1)} %get-tuple-element.18.seed_t, bf16[768,768]{1,0:T(8,128)(2,1)S(1)} %get-tuple-element.19.high_t, bf16[768,768]{1,0:T(8,128)(2,1)S(1)} %get-tuple-element.20.low_t), custom_call_target="tpu_custom_call" | custom-call | flops 905969664 | bytes 4194304 | tf_op jit(solution)/shard_map/lift/pallas_call | solution.py:268
  13.0 0.0 copy-start.2
  13.0 1.0 %copy-done.2 = f32[384,768]{1,0:T(8,128)} copy-done((f32[384,768]{1,0:T(8,128)}, f32[384,768]{1,0:T(8,128)S(1)}, u32[]{:S(2)}) %copy-start.2) | copy-done | bytes 1179672
  14.0 0.2 collective-permute-done.3
  14.2 0.7 %pad_maximum_fusion = bf16[16,768]{1,0:T(8,128)(2,1)S(1)} fusion(bf16[8,768]{1,0:T(8,128)(2,1)} %collective-permute-done.3, bf16[4,768]{1,0:T(4,128)(2,1)} %copy-done.6, bf16[4,768]{1,0:T(4,128)(2,1)S(1)} %hold.1), kind=kLoop, calls=%fused_computation | loop fusion | flops 73728 | bytes 49152 | tf_op jit(solution)/shard_map/concatenate | solution.py:361
  15.0 0.0 copy-start.3
  15.0 1.3 %copy-done.3 = f32[384,768]{1,0:T(8,128)S(1)} copy-done((f32[384,768]{1,0:T(8,128)S(1)}, f32[384,768]{1,0:T(8,128)}, u32[]{:S(2)}) %copy-start.3) | copy-done | bytes 1179672
  16.2 3.5 %propagate.1 = (bf16[4,384,768]{2,1,0:T(8,128)(2,1)S(1)}, f32[4,768,128]{2,1,0:T(8,128)S(1)}) custom-call(f32[384,768]{1,0:T(8,128)S(1)} %copy-done.3, bf16[768,768]{1,0:T(8,128)(2,1)S(1)} %get-tuple-element.19.high_t, bf16[768,768]{1,0:T(8,128)(2,1)S(1)} %get-tuple-element.20.low_t, bf16[1,768]{1,0:T(2,128)(2,1)S(1)} %get-tuple-element.29.refs_0_, ...), custom_call_target="tpu_custom_call" | custom-call | flops 2717908992 | bytes 4194304 | tf_op jit(solution)/shard_map/propagate/pallas_call | solution.py:282
  19.8 0.0 collective-permute-done.4.arrived
  19.8 0.0 copy-start.5
  19.8 0.0 copy-start
  19.8 2.9 %chain.1 = (bf16[4,384,256]{2,1,0:T(8,128)(2,1)S(1)}, bf16[4,384,256]{2,1,0:T(8,128)(2,1)S(1)}) custom-call(bf16[768,256]{1,0:T(8,128)(2,1)} %collective-permute-done.4.arrived, bf16[768,768]{1,0:T(8,128)(2,1)S(1)} %get-tuple-element.23.hop_ref.refs_3_, f32[4,768,128]{2,1,0:T(8,128)S(1)} %get-tuple-element.24.scale_ref.refs_4_), custom_call_target="tpu_custom_call" | custom-call | flops 1207959552 | bytes 4194304 | tf_op jit(solution)/shard_map/chain/pallas_call | solution.py:313
  22.7 0.1 collective-permute-start.5
  22.8 0.0 copy-done.5
  22.8 0.6 %collective-permute-start = (bf16[768,128]{1,0:T(8,128)(2,1)S(1)}, bf16[768,128]{1,0:T(8,128)(2,1)S(1)}, u32[]{:S(2)}, u32[]{:S(2)}) collective-permute-start(bf16[768,128]{1,0:T(8,128)(2,1)S(1)} %copy-done.5), channel_id=1, source_target_pairs={{0,2},{2,0},{1,3},{3,1},{4,6},{6,4},{5,7},{7,5},{8,10},{10,8},{9,1... | collective-permute-start | bytes 589832 | tf_op jit(solution)/shard_map/ppermute | solution.py:385
  23.4 6.7 %collective-permute-done.refs_0_ = bf16[768,128]{1,0:T(8,128)(2,1)S(1)} collective-permute-done((bf16[768,128]{1,0:T(8,128)(2,1)S(1)}, bf16[768,128]{1,0:T(8,128)(2,1)S(1)}, u32[]{:S(2)}, u32[]{:S(2)}) %collective-permute-start) | collective-permute-done | bytes 196640 | tf_op jit(solution)/shard_map/ppermute | solution.py:385
  30.1 0.0 collective-permute-start.1
  30.1 0.0 collective-permute-done.5.theirs
  30.1 0.0 copy-done
  30.1 1.3 %add_up.1.refs_6_ = f32[768,384]{1,0:T(8,128)S(1)} custom-call(bf16[4,384,256]{2,1,0:T(8,128)(2,1)S(1)} %get-tuple-element.25.ours, bf16[4,384,256]{2,1,0:T(8,128)(2,1)S(1)} %collective-permute-done.5.theirs, bf16[4,384,768]{2,1,0:T(8,128)(2,1)S(1)} %get-tuple-element.22.turned_ref.refs_2_, bf16[768,768]{1,0:T(8,128)(2,1)S(1)} %copy-done), custom_call_target="tpu_custom_call" | custom-call | flops 603979776 | bytes 4194304 | tf_op jit(solution)/shard_map/add_up/pallas_call | solution.py:327
  31.4 0.1 collective-permute-done.1.refs_1_
  31.6 3.2 %finish.1 = bf16[768,384]{1,0:T(8,128)(2,1)} custom-call(bf16[768,128]{1,0:T(8,128)(2,1)S(1)} %collective-permute-done.refs_0_, bf16[768,128]{1,0:T(8,128)(2,1)S(1)} %collective-permute-done.1.refs_1_, bf16[4,384,768]{2,1,0:T(8,128)(2,1)S(1)} %get-tuple-element.22.turned_ref.refs_2_, bf16[768,768]{1,0:T(8,128)(2,1)S(1)} %get-tuple-element.23.hop_ref.refs_3_, ...), custom_call_target="tpu_custom_call" | custom-call | flops 1207959552 | bytes 4194304 | tf_op jit(solution)/shard_map/finish/pallas_call | solution.py:342
  (3 shorter events, 0.0 us)
Async XLA Ops:
  1.9 4.6 %copy-start.4 = (bf16[768,128]{1,0:T(8,128)(2,1)}, bf16[768,128]{1,0:T(8,128)(2,1)S(1)}, u32[]{:S(2)}) copy-start(bf16[768,128]{1,0:T(8,128)(2,1)S(1)} %get-tuple-element.16.refs_1_) | copy-start | bytes 589828
  1.9 4.6 %copy-start.1 = (f32[768,768]{1,0:T(8,128)S(1)}, f32[768,768]{1,0:T(8,128)}, u32[]{:S(2)}) copy-start(f32[768,768]{1,0:T(8,128)} %hop_ref.1) | copy-start | bytes 7077892
  2.0 6.7 %collective-permute-start.2 = (bf16[4,768]{1,0:T(4,128)(2,1)S(1)}, bf16[4,768]{1,0:T(4,128)(2,1)S(1)}, u32[]{:S(2)}, u32[]{:S(2)}) collective-permute-start(bf16[4,768]{1,0:T(4,128)(2,1)S(1)} %hold.1), channel_id=1, source_target_pairs={{0,4},{4,0},{8,12},{12,8},{1,5},{5,1},{9,13},{13,9},{2,6},{6,2},{1... | collective-permute-start | bytes 18440 | tf_op jit(solution)/shard_map/ppermute | solution.py:360
  5.1 14.7 %collective-permute-start.4 = (bf16[768,256]{1,0:T(8,128)(2,1)}, bf16[768,256]{1,0:T(8,128)(2,1)}, u32[]{:S(2)}, u32[]{:S(2)}) collective-permute-start(bf16[768,256]{1,0:T(8,128)(2,1)} %get-tuple-element.17.refs_0_), channel_id=1, source_target_pairs={{0,2},{2,0},{1,3},{3,1},{4,6},{6,4},{5,7},{7,5},{8,10},{10,8},{9,1... | collective-permute-start | bytes 1179656 | tf_op jit(solution)/shard_map/ppermute | solution.py:384
  8.7 3.2 %copy-start.6 = (bf16[4,768]{1,0:T(4,128)(2,1)}, bf16[4,768]{1,0:T(4,128)(2,1)S(1)}, u32[]{:S(2)}) copy-start(bf16[4,768]{1,0:T(4,128)(2,1)S(1)} %collective-permute-done.2) | copy-start | bytes 18436
  9.3 4.9 %collective-permute-start.3 = (bf16[8,768]{1,0:T(8,128)(2,1)}, bf16[8,768]{1,0:T(8,128)(2,1)}, u32[]{:S(2)}, u32[]{:S(2)}) collective-permute-start(bf16[8,768]{1,0:T(8,128)(2,1)} %pad_maximum_fusion.1), channel_id=1, source_target_pairs={{0,8},{4,12},{8,0},{12,4},{1,9},{5,13},{9,1},{13,5},{2,10},{6,14},... | collective-permute-start | bytes 36872 | tf_op jit(solution)/shard_map/ppermute | solution.py:360
  13.0 1.0 %copy-start.2 = (f32[384,768]{1,0:T(8,128)}, f32[384,768]{1,0:T(8,128)S(1)}, u32[]{:S(2)}) copy-start(f32[384,768]{1,0:T(8,128)S(1)} %lift.1.image_ref) | copy-start | bytes 3538948
  15.0 1.3 %copy-start.3 = (f32[384,768]{1,0:T(8,128)S(1)}, f32[384,768]{1,0:T(8,128)}, u32[]{:S(2)}) copy-start(f32[384,768]{1,0:T(8,128)} %copy-done.2) | copy-start | bytes 3538948
  19.8 3.0 %copy-start.5 = (bf16[768,128]{1,0:T(8,128)(2,1)S(1)}, bf16[768,128]{1,0:T(8,128)(2,1)}, u32[]{:S(2)}) copy-start(bf16[768,128]{1,0:T(8,128)(2,1)} %copy-done.4) | copy-start | bytes 589828
  19.8 10.3 %copy-start = (bf16[768,768]{1,0:T(8,128)(2,1)S(1)}, bf16[768,768]{1,0:T(8,128)(2,1)}, u32[]{:S(2)}) copy-start(bf16[768,768]{1,0:T(8,128)(2,1)} %refs_5_.1) | copy-start | bytes 3538948
  22.7 7.4 %collective-permute-start.5 = (bf16[4,384,256]{2,1,0:T(8,128)(2,1)S(1)}, bf16[4,384,256]{2,1,0:T(8,128)(2,1)S(1)}, u32[]{:S(2)}, u32[]{:S(2)}) collective-permute-start(bf16[4,384,256]{2,1,0:T(8,128)(2,1)S(1)} %get-tuple-element.26), channel_id=1, source_target_pairs={{0,1},{1,0},{2,3},{3,2},{4,5},{5,4},{6,7},{7,6},{8,9},{9,8},{10,11... | collective-permute-start | bytes 2359304 | tf_op jit(solution)/shard_map/ppermute | solution.py:391
  22.8 7.3 %collective-permute-start = (bf16[768,128]{1,0:T(8,128)(2,1)S(1)}, bf16[768,128]{1,0:T(8,128)(2,1)S(1)}, u32[]{:S(2)}, u32[]{:S(2)}) collective-permute-start(bf16[768,128]{1,0:T(8,128)(2,1)S(1)} %copy-done.5), channel_id=1, source_target_pairs={{0,2},{2,0},{1,3},{3,1},{4,6},{6,4},{5,7},{7,5},{8,10},{10,8},{9,1... | collective-permute-start | bytes 589832 | tf_op jit(solution)/shard_map/ppermute | solution.py:385
  30.1 1.4 %collective-permute-start.1 = (bf16[768,128]{1,0:T(8,128)(2,1)S(1)}, bf16[768,128]{1,0:T(8,128)(2,1)S(1)}, u32[]{:S(2)}, u32[]{:S(2)}) collective-permute-start(bf16[768,128]{1,0:T(8,128)(2,1)S(1)} %collective-permute-done.refs_0_), channel_id=1, source_target_pairs={{0,1},{1,0},{2,3},{3,2},{4,5},{5,4},{6,7},{7,6},{8,9},{9,8},{10,11... | collective-permute-start | bytes 589832 | tf_op jit(solution)/shard_map/ppermute | solution.py:392

commit v3 on v2

--- a/solution.py
+++ b/solution.py
@@ -102,22 +102,44 @@
     image_out[...] = keep_share * narrow.astype(jnp.float32) + hopped
 
 
-def own_kernel(row_count, image_ref, high_t, low_t, *refs):
-    wraps = len(refs) - 2
-    turned_out, scale_out = refs[wraps:]
+def join_kernel(held_ref, came_ref, out_ref):
+    out_ref[...] = jnp.concatenate([held_ref[...], came_ref[...]], axis=0)
+
+
+def weigh_kernel(row_count, doubled, *refs):
+    *line_refs, scale_out, column_out = refs
+    wraps = scale_out.shape[0]
     row_index = lax.axis_index("rowt")
+    lines = jnp.concatenate([ref[...].astype(jnp.float32) for ref in line_refs], axis=0)
+    places = lax.broadcasted_iota(jnp.int32, lines.shape, 0)
+    scales = []
+    for step in range(wraps):
+        target = (row_index + step + 1) % row_count
+        if doubled:
+            pick = (row_index ^ target) * wraps + step
+            spins = jnp.sum(jnp.where(places == pick, lines, 0.0), axis=0, keepdims=True)
+        else:
+            spins = lines[step : step + 1]
+        sign = jnp.where(target == 0, -1.0, 1.0)
+        scales.append(sign * jnp.exp(coupling * (2.0 * spins - 1.0)))
+    scale = jnp.concatenate(scales, axis=0)
+    scale_out[...] = scale
+    columns = scale.T
+    for step in range(wraps):
+        column_out[step] = jnp.broadcast_to(columns[:, step : step + 1], column_out.shape[1:])
+
+
+def own_kernel(first, image_ref, high_t, low_t, scale_ref, turned_out, *rest):
+    steps, total = turned_out.shape[0], scale_ref.shape[0]
     image = image_ref[...]
-    for step in range(wraps):
-        spins = refs[step][...].astype(jnp.float32)
-        sign = jnp.where((row_index + step + 1) % row_count == 0, -1.0, 1.0)
-        scale = sign * jnp.exp(coupling * (2.0 * spins - 1.0))
-        column = jnp.broadcast_to(scale, (8, scale.shape[1])).T[:, :1]
-        scale_out[step] = jnp.broadcast_to(column, scale_out.shape[1:])
-        turned = scale * image
+    for step in range(steps):
+        turned = scale_ref[first + step : first + step + 1, :] * image
         narrow = turned.astype(jnp.bfloat16)
         turned_out[step] = narrow
-        if step < wraps - 1:
+        if first + step < total - 1:
             image = keep_share * turned + hop_turned(narrow, high_t, low_t)
+    if rest:
+        rest[0][...] = image
 
 
 def advance(step, spans, hop_ref, scale_ref, level, narrow):
@@ -145,8 +167,14 @@
 
 
 def multiply(met, own):
-    product = met.astype(jnp.float32) * own.astype(jnp.float32)
-    return product.astype(jnp.bfloat16).astype(jnp.float32)
+    return (met * own).astype(jnp.float32)
+
+
+def own_levels(turned_refs, spans):
+    for turned_ref in turned_refs:
+        for step in range(turned_ref.shape[0]):
+            parts = [turned_ref[step, :, span] for span in spans]
+            yield parts[0] if len(parts) == 1 else jnp.concatenate(parts, axis=1)
 
 
 def columns_at(offset, part, width):
@@ -156,13 +184,14 @@
     return held, [pl.ds(pl.multiple_of(p * width + offset, LANES), part) for p in places]
 
 
-def sum_kernel(offset, ours, theirs, turned_ref, vertex_ref, out_ref):
-    wraps, width, _ = turned_ref.shape
+def sum_kernel(offset, ours, theirs, *refs):
+    *turned_refs, vertex_ref, out_ref = refs
+    width = ours.shape[1]
     total = None
     for met_ref, held, spot in zip((ours, theirs), *columns_at(offset, ours.shape[2], width)):
         pairs = None
-        for step in range(wraps):
-            product = multiply(met_ref[step], turned_ref[step, :, held])
+        for step, own in enumerate(own_levels(turned_refs, [held])):
+            product = multiply(met_ref[step], own)
             pairs = product if pairs is None else pairs + product
         for half in split_halves(pairs):
             part = lax.dot_general(
@@ -176,9 +205,9 @@
 
 
 def finish_kernel(offset, *refs):
-    ours, theirs, turned_ref, hop_ref, scale_ref, vertex_ref, total_ref = refs[:7]
-    out_ref, level, narrow, result, sems = refs[7:]
-    wraps, width, sites = turned_ref.shape
+    ours, theirs, hop_ref, scale_ref, vertex_ref, total_ref, *turned_refs = refs[:-5]
+    out_ref, level, narrow, result, sems = refs[-5:]
+    wraps, (sites, width) = scale_ref.shape[0], total_ref.shape
     spans = [slice(0, width), slice(width, 2 * width)]
     held, spots = columns_at(offset, ours.shape[1], width)
     other = jnp.concatenate([theirs[span, :] for span in reversed(spans)], axis=0)
@@ -186,10 +215,9 @@
     narrow[0] = arrived
     level[...] = arrived.astype(jnp.float32)
     pairs = None
-    for step in range(wraps):
+    for step, own in enumerate(own_levels(turned_refs, held)):
         needed = spans if step < wraps - 1 else spans[:1]
         met = list(advance(step, needed, hop_ref, scale_ref, level, narrow))[0]
-        own = jnp.concatenate([turned_ref[step, :, span] for span in held], axis=1)
         product = multiply(met, own)
         pairs = product if pairs is None else pairs + product
     halves = split_halves(pairs)
@@ -276,21 +304,48 @@
     )(seed_t, high_t, low_t)
 
 
-def propagate(row_count, image, high_t, low_t, lines):
-    width, sites = image.shape
-    wraps = len(lines)
-    return pl.pallas_call(
-        functools.partial(own_kernel, row_count),
+def join(held, came):
+    shape = (held.shape[0] + came.shape[0], held.shape[1])
+    return pl.pallas_call(
+        join_kernel,
+        out_shape=jax.ShapeDtypeStruct(shape, held.dtype),
+        in_specs=[VMEM] * 2,
+        out_specs=VMEM,
+        compiler_params=limit(4),
+        name="join",
+    )(held, came)
+
+
+def weigh(wraps, lines, doubled):
+    sites = lines[0].shape[1]
+    return pl.pallas_call(
+        functools.partial(weigh_kernel, lax.axis_size("rowt"), doubled),
         out_shape=[
-            jax.ShapeDtypeStruct((wraps, width, sites), jnp.bfloat16),
+            jax.ShapeDtypeStruct((wraps, sites), jnp.float32),
             jax.ShapeDtypeStruct((wraps, sites, LANES), jnp.float32),
         ],
-        in_specs=[VMEM] * (3 + wraps),
+        in_specs=[VMEM] * len(lines),
         out_specs=[VMEM] * 2,
+        compiler_params=limit(8),
+        name="weigh",
+    )(*lines)
+
+
+def propagate(first, last, image, high_t, low_t, scale):
+    width, sites = image.shape
+    wraps, steps = scale.shape[0], last - first
+    outs = [jax.ShapeDtypeStruct((steps, width, sites), jnp.bfloat16)]
+    if last < wraps:
+        outs.append(jax.ShapeDtypeStruct((width, sites), jnp.float32))
+    return pl.pallas_call(
+        functools.partial(own_kernel, first),
+        out_shape=outs,
+        in_specs=[VMEM] * 4,
+        out_specs=[VMEM] * len(outs),
         compiler_params=limit(16),
-        cost_estimate=work(width, sites, 2 * (wraps - 1)),
-        name="propagate",
-    )(image, high_t, low_t, *lines)
+        cost_estimate=work(width, sites, 2 * steps),
+        name="late" if first else "early",
+    )(image, high_t, low_t, scale)
 
 
 def work(columns, sites, wraps):
@@ -323,33 +378,33 @@
 
 
 def add_up(offset, ours, theirs, turned, vertex):
-    _, width, sites = turned.shape
+    _, width, columns = ours.shape
+    sites = vertex.shape[0]
     return pl.pallas_call(
         functools.partial(sum_kernel, offset),
         out_shape=jax.ShapeDtypeStruct((sites, width), jnp.float32),
-        in_specs=[VMEM] * 4,
+        in_specs=[VMEM] * (3 + len(turned)),
         out_specs=VMEM,
         compiler_params=limit(16),
-        cost_estimate=work(ours.shape[2], sites, 2),
+        cost_estimate=work(columns, sites, 2),
         name="add_up",
-    )(ours, theirs, turned, vertex)
-
-
-def finish(offset, *operands):
-    ours, turned = operands[0], operands[2]
-    wraps, width, sites = turned.shape
+    )(ours, theirs, *turned, vertex)
+
+
+def finish(offset, ours, theirs, hop, columns, vertex, total, turned):
+    sites, width = total.shape
     blocks = 2
     return pl.pallas_call(
         functools.partial(finish_kernel, offset),
         out_shape=jax.ShapeDtypeStruct((sites, width), jnp.bfloat16),
-        in_specs=[VMEM] * len(operands),
+        in_specs=[VMEM] * (6 + len(turned)),
         out_specs=HBM,
         scratch_shapes=levels(sites, 2 * ours.shape[1])
         + [pltpu.VMEM((sites, width), jnp.bfloat16), pltpu.SemaphoreType.DMA((blocks,))],
         compiler_params=limit(16),
-        cost_estimate=work(2 * ours.shape[1], sites, wraps),
+        cost_estimate=work(2 * ours.shape[1], sites, columns.shape[0]),
         name="finish",
-    )(*operands)
+    )(ours, theirs, hop, columns, vertex, total, *turned)
 
 
 def fetch_lines(lines):
@@ -358,24 +413,22 @@
         bit = 1
         while bit < rows:
             came = lax.ppermute(lines, "rowt", [(i, i ^ bit) for i in range(rows)])
-            lines = jnp.concatenate([lines, came], axis=0)
             bit *= 2
-        index = lax.axis_index("rowt")
-        picks = [(index ^ (index + w) % rows) * count + w - 1 for w in range(1, rows)]
-        found = [lax.dynamic_slice_in_dim(lines, pick, 1, 0) for pick in picks]
-        return found + [lines[count - 1 : count]]
+            if bit < rows:
+                lines = join(lines, came)
+        return [lines, came], True
     found = []
     for step in range(count):
         line, shift = lines[step : step + 1], (step + 1) % rows
         if shift:
             line = lax.ppermute(line, "rowt", [((i + shift) % rows, i) for i in range(rows)])
         found.append(line)
-    return found
+    return found, False
 
 
 def per_device(seed_green, field_spins, hop_matrix, vertex):
     cols, sites = lax.axis_size("colt"), lax.axis_size("site")
-    width = seed_green.shape[-1]
+    wraps, width = field_spins.shape[0], seed_green.shape[-1]
     edge = width - LANES
     across = [(i, (i + cols // 2) % cols) for i in range(cols)]
     swap = [(i, sites - 1 - i) for i in range(sites)]
@@ -383,15 +436,19 @@
     pieces, lines = cut(seed_green[0, 0], field_spins, [(0, edge), (edge, width)])
     first = lax.ppermute(pieces[0], "colt", across)
     second = lax.ppermute(pieces[1], "colt", across)
-    lines = fetch_lines(hold(lines))
+    found, doubled = fetch_lines(hold(lines))
     hop, high_t, low_t, seed_t = prepare(hop_matrix, pieces)
     image = lift(seed_t, high_t, low_t)
-    turned, scale = propagate(lax.axis_size("rowt"), image, high_t, low_t, lines)
-    keep, send = chain(first, hop, scale, width)
+    scale, columns = weigh(wraps, found, doubled)
+    keep, send = chain(first, hop, columns, width)
     came = lax.ppermute(send, "site", swap)
+    middle = wraps // 2
+    early, image = propagate(0, middle, image, high_t, low_t, scale)
     other = lax.ppermute(second, "site", swap)
+    (late,) = propagate(middle, wraps, image, high_t, low_t, scale)
+    turned = [early, late]
     total = add_up(0, keep, came, turned, vertex)
-    result = finish(edge, second, other, turned, hop, scale, vertex, total)
+    result = finish(edge, second, other, hop, columns, vertex, total, turned)
     return result[None, None]
 
 

time: 35.1 us -> 28.2 us (0.80)
  Pallas kernels: 16.1 us -> 13.5 us
  local copies, waits for them, and re-layouts: 2.36 us -> 0.17 us
  waiting for transfers between devices: 7.03 us -> 5.13 us
  other arithmetic: 1.33 us -> 0 us
  starting transfers between devices: 7.84 us -> 9.14 us
    ppermute x1, waiting for transfers between devices: 6.72 us -> 1.97 us  [per_device(): second = lax.ppermute(pieces[1], 'colt', across)]
    ppermute x2, waiting for transfers between devices: 0.18 us -> 3.02 us  [fetch_lines(): came = lax.ppermute(lines, 'rowt', [(i, i ^ bit) for i in range(rows)])]
    unnamed x14 -> x4, local copies, waits for them, and re-layouts: 2.32 us -> 0.17 us
    ppermute x1, starting transfers between devices: 1.49 us -> 3.03 us  [per_device(): first = lax.ppermute(pieces[0], 'colt', across)]
    ppermute x2, starting transfers between devices: 5.71 us -> 4.23 us  [fetch_lines(): came = lax.ppermute(lines, 'rowt', [(i, i ^ bit) for i in range(rows)])]
    concatenate x2 -> x0, other arithmetic: 1.33 us -> none  [fetch_lines(): lines = jnp.concatenate([lines, came], axis=0)]
    ppermute x1, starting transfers between devices: 0.57 us -> 1.8 us  [per_device(): second = lax.ppermute(pieces[1], 'colt', across)]
    pallas_call x1, Pallas kernels: 2.91 us -> 1.76 us  [chain(): pl.pallas_call(chain_kernel, out_shape=[shape] * 2, in_specs=[VMEM] * 3,...]
  transfers between devices with their start and end apart: 6 -> 6, of which waited for: 3 -> 4; matrix products, arithmetic and copies ran while one was open for 4% -> 0% of each run, Pallas kernels for 23% -> 26%
where the time goes in v3:
time: 28.2 us; the launch traced here: 28 us
  Pallas kernels  13.5 us (48%)
  starting transfers between devices  9.14 us (32%)
  waiting for transfers between devices  5.13 us (18%)
    ppermute x2, starting transfers between devices, fetch_lines(): came = lax.ppermute(lines, 'rowt', [(i, i ^ bit) for i in range(rows)])  4.23 us
    pallas_call x2, Pallas kernels, propagate(): pl.pallas_call(functools.partial(own_kernel, first), out_shape=outs, in_s...  3.53 us
    pallas_call x1, Pallas kernels, finish(): pl.pallas_call(functools.partial(finish_kernel, offset), out_shape=jax.Sh...  3.12 us
    ppermute x1, starting transfers between devices, per_device(): first = lax.ppermute(pieces[0], 'colt', across)  3.03 us
    ppermute x2, waiting for transfers between devices, fetch_lines(): came = lax.ppermute(lines, 'rowt', [(i, i ^ bit) for i in range(rows)])  3.02 us
    ppermute x1, waiting for transfers between devices, per_device(): second = lax.ppermute(pieces[1], 'colt', across)  1.97 us
    ppermute x1, starting transfers between devices, per_device(): second = lax.ppermute(pieces[1], 'colt', across)  1.8 us
    pallas_call x1, Pallas kernels, chain(): pl.pallas_call(chain_kernel, out_shape=[shape] * 2, in_specs=[VMEM] * 3,...  1.76 us
  transfers between devices with their start and end apart: 6, of which 4 were waited for; matrix products, arithmetic and copies ran while one was open for 0% of the time, Pallas kernels for 26%

profile of v3, /device:TPU:0, one launch (start us, length us, event | category | flops | bytes accessed | tf_op | source)
XLA Modules:
  0.0 28.0 jit_solution(8103744141565936570)
XLA Ops:
  0.0 1.2 %cut.1 = (bf16[768,256]{1,0:T(8,128)(2,1)S(1)}, bf16[768,128]{1,0:T(8,128)(2,1)S(1)}, bf16[4,768]{1,0:T(4,128)(2,1)S(1)}) custom-call(bf16[768,384]{1,0:T(8,128)(2,1)} %bitcast.2, s32[4,1,768]{2,1,0:T(1,128)} %spins_ref.1), custom_call_target="tpu_custom_call" | custom-call | tf_op jit(solution)/shard_map/cut/pallas_call | solution.py:251
  1.2 3.0 %collective-permute-start.4 = (bf16[768,256]{1,0:T(8,128)(2,1)S(1)}, bf16[768,256]{1,0:T(8,128)(2,1)S(1)}, u32[]{:S(2)}, u32[]{:S(2)}) collective-permute-start(bf16[768,256]{1,0:T(8,128)(2,1)S(1)} %get-tuple-element.19.refs_0_), channel_id=1, source_target_pairs={{0,2},{2,0},{1,3},{3,1},{4,6},{6,4},{5,7},{7,5},{8,10},{10,8},{9,1... | collective-permute-start | bytes 1179656 | tf_op jit(solution)/shard_map/ppermute | solution.py:437
  4.2 0.0 copy-start.1
  4.2 1.6 %collective-permute-start.2 = (bf16[4,768]{1,0:T(4,128)(2,1)S(1)}, bf16[4,768]{1,0:T(4,128)(2,1)S(1)}, u32[]{:S(2)}, u32[]{:S(2)}) collective-permute-start(bf16[4,768]{1,0:T(4,128)(2,1)S(1)} %hold.1.held_ref), channel_id=1, source_target_pairs={{0,4},{4,0},{8,12},{12,8},{1,5},{5,1},{9,13},{13,9},{2,6},{6,2},{1... | collective-permute-start | bytes 18440 | tf_op jit(solution)/shard_map/ppermute | solution.py:415
  5.8 2.1 %collective-permute-done.2.came_ref = bf16[4,768]{1,0:T(4,128)(2,1)S(1)} collective-permute-done((bf16[4,768]{1,0:T(4,128)(2,1)S(1)}, bf16[4,768]{1,0:T(4,128)(2,1)S(1)}, u32[]{:S(2)}, u32[]{:S(2)}) %collective-permute-start.2) | collective-permute-done | bytes 6176 | tf_op jit(solution)/shard_map/ppermute | solution.py:415
  7.9 2.7 %collective-permute-start.3 = (bf16[8,768]{1,0:T(8,128)(2,1)S(1)}, bf16[8,768]{1,0:T(8,128)(2,1)S(1)}, u32[]{:S(2)}, u32[]{:S(2)}) collective-permute-start(bf16[8,768]{1,0:T(8,128)(2,1)S(1)} %join.1.refs_0_), channel_id=1, source_target_pairs={{0,8},{4,12},{8,0},{12,4},{1,9},{5,13},{9,1},{13,5},{2,10},{6,14},... | collective-permute-start | bytes 36872 | tf_op jit(solution)/shard_map/ppermute | solution.py:415
  10.5 0.0 copy-done.1
  10.5 1.0 %prepare.1 = (bf16[768,768]{1,0:T(8,128)(2,1)S(1)}, bf16[768,768]{1,0:T(8,128)(2,1)S(1)}, bf16[768,768]{1,0:T(8,128)(2,1)S(1)}, bf16[384,768]{1,0:T(8,128)(2,1)S(1)}) custom-call(f32[768,768]{1,0:T(8,128)S(1)} %copy-done.1, bf16[768,256]{1,0:T(8,128)(2,1)S(1)} %get-tuple-element.19.refs_0_, bf16[768,128]{1,0:T(8,128)(2,1)S(1)} %get-tuple-element.18.refs_1_), custom_call_target="tpu_custom_call" | custom-call | flops 268435456 | bytes 4194304 | tf_op jit(solution)/shard_map/prepare/pallas_call | solution.py:283
  11.6 1.0 %collective-permute-done.3.refs_1_ = bf16[8,768]{1,0:T(8,128)(2,1)S(1)} collective-permute-done((bf16[8,768]{1,0:T(8,128)(2,1)S(1)}, bf16[8,768]{1,0:T(8,128)(2,1)S(1)}, u32[]{:S(2)}, u32[]{:S(2)}) %collective-permute-start.3) | collective-permute-done | bytes 12320 | tf_op jit(solution)/shard_map/ppermute | solution.py:415
  12.5 0.7 %weigh.1 = (f32[4,768]{1,0:T(4,128)S(1)}, f32[4,768,128]{2,1,0:T(8,128)S(1)}) custom-call(bf16[8,768]{1,0:T(8,128)(2,1)S(1)} %join.1.refs_0_, bf16[8,768]{1,0:T(8,128)(2,1)S(1)} %collective-permute-done.3.refs_1_), custom_call_target="tpu_custom_call" | custom-call | tf_op jit(solution)/shard_map/weigh/pallas_call | solution.py:321
  13.2 0.1 collective-permute-done.4.arrived
  13.3 1.8 %chain.1 = (bf16[4,384,256]{2,1,0:T(8,128)(2,1)S(1)}, bf16[4,384,256]{2,1,0:T(8,128)(2,1)S(1)}) custom-call(bf16[768,256]{1,0:T(8,128)(2,1)S(1)} %collective-permute-done.4.arrived, bf16[768,768]{1,0:T(8,128)(2,1)S(1)} %get-tuple-element.20.hop_ref.refs_2_, f32[4,768,128]{2,1,0:T(8,128)S(1)} %get-tuple-element.22.scale_ref.refs_3_), custom_call_target="tpu_custom_call" | custom-call | flops 1207959552 | bytes 4194304 | tf_op jit(solution)/shard_map/chain/pallas_call | solution.py:368
  15.1 0.1 collective-permute-start.5
  15.2 1.8 %collective-permute-start = (bf16[768,128]{1,0:T(8,128)(2,1)S(1)}, bf16[768,128]{1,0:T(8,128)(2,1)S(1)}, u32[]{:S(2)}, u32[]{:S(2)}) collective-permute-start(bf16[768,128]{1,0:T(8,128)(2,1)S(1)} %get-tuple-element.18.refs_1_), channel_id=1, source_target_pairs={{0,2},{2,0},{1,3},{3,1},{4,6},{6,4},{5,7},{7,5},{8,10},{10,8},{9,1... | collective-permute-start | bytes 589832 | tf_op jit(solution)/shard_map/ppermute | solution.py:438
  17.0 1.1 %lift.1.image_ref = f32[384,768]{1,0:T(8,128)S(1)} custom-call(bf16[384,768]{1,0:T(8,128)(2,1)S(1)} %get-tuple-element.25.seed_t, bf16[768,768]{1,0:T(8,128)(2,1)S(1)} %get-tuple-element.26.high_t, bf16[768,768]{1,0:T(8,128)(2,1)S(1)} %get-tuple-element.27.low_t), custom_call_target="tpu_custom_call" | custom-call | flops 905969664 | bytes 4194304 | tf_op jit(solution)/shard_map/lift/pallas_call | solution.py:296
  18.1 2.4 %early.1 = (bf16[2,384,768]{2,1,0:T(8,128)(2,1)S(1)}, f32[384,768]{1,0:T(8,128)S(1)}) custom-call(f32[384,768]{1,0:T(8,128)S(1)} %lift.1.image_ref, bf16[768,768]{1,0:T(8,128)(2,1)S(1)} %get-tuple-element.26.high_t, bf16[768,768]{1,0:T(8,128)(2,1)S(1)} %get-tuple-element.27.low_t, f32[4,768]{1,0:T(4,128)S(1)} %get-tuple-element.28.scale_ref), custom_call_target="tpu_custom_call" | custom-call | flops 1811939328 | bytes 4194304 | tf_op jit(solution)/shard_map/early/pallas_call | solution.py:340
  20.5 2.0 %collective-permute-done.refs_0_ = bf16[768,128]{1,0:T(8,128)(2,1)S(1)} collective-permute-done((bf16[768,128]{1,0:T(8,128)(2,1)S(1)}, bf16[768,128]{1,0:T(8,128)(2,1)S(1)}, u32[]{:S(2)}, u32[]{:S(2)}) %collective-permute-start) | collective-permute-done | bytes 196640 | tf_op jit(solution)/shard_map/ppermute | solution.py:438
  22.5 0.0 collective-permute-start.1
  22.5 0.0 copy-start
  22.5 1.1 %late.1.refs_1_.refs_7_ = bf16[2,384,768]{2,1,0:T(8,128)(2,1)S(1)} custom-call(f32[384,768]{1,0:T(8,128)S(1)} %get-tuple-element.30.image_ref, bf16[768,768]{1,0:T(8,128)(2,1)S(1)} %get-tuple-element.26.high_t, bf16[768,768]{1,0:T(8,128)(2,1)S(1)} %get-tuple-element.27.low_t, f32[4,768]{1,0:T(4,128)S(1)} %get-tuple-element.28.scale_ref), custom_call_target="tpu_custom_call" | custom-call | flops 1811939328 | bytes 4194304 | tf_op jit(solution)/shard_map/late/pallas_call | solution.py:340
  23.6 0.0 collective-permute-done.5.theirs
  23.6 0.2 copy-done
  23.8 1.1 %add_up.1.refs_5_ = f32[768,384]{1,0:T(8,128)S(1)} custom-call(bf16[4,384,256]{2,1,0:T(8,128)(2,1)S(1)} %get-tuple-element.23.ours, bf16[4,384,256]{2,1,0:T(8,128)(2,1)S(1)} %collective-permute-done.5.theirs, bf16[2,384,768]{2,1,0:T(8,128)(2,1)S(1)} %get-tuple-element.29.refs_0_.refs_6_, bf16[2,384,768]{2,1,0:T(8,128)(2,1)S(1)} %late.1.refs_1_.refs_7_, ...), custom_call_target="tpu_custom_call" | custom-call | flops 603979776 | bytes 4194304 | tf_op jit(solution)/shard_map/add_up/pallas_call | solution.py:383
  24.9 0.0 collective-permute-done.1.refs_1_
  24.9 3.1 %finish.1 = bf16[768,384]{1,0:T(8,128)(2,1)} custom-call(bf16[768,128]{1,0:T(8,128)(2,1)S(1)} %collective-permute-done.refs_0_, bf16[768,128]{1,0:T(8,128)(2,1)S(1)} %collective-permute-done.1.refs_1_, bf16[768,768]{1,0:T(8,128)(2,1)S(1)} %get-tuple-element.20.hop_ref.refs_2_, f32[4,768,128]{2,1,0:T(8,128)S(1)} %get-tuple-element.22.scale_ref.refs_3_, ...), custom_call_target="tpu_custom_call" | custom-call | flops 1207959552 | bytes 4194304 | tf_op jit(solution)/shard_map/finish/pallas_call | solution.py:397
  (2 shorter events, 0.0 us)
Async XLA Ops:
  1.2 12.1 %collective-permute-start.4 = (bf16[768,256]{1,0:T(8,128)(2,1)S(1)}, bf16[768,256]{1,0:T(8,128)(2,1)S(1)}, u32[]{:S(2)}, u32[]{:S(2)}) collective-permute-start(bf16[768,256]{1,0:T(8,128)(2,1)S(1)} %get-tuple-element.19.refs_0_), channel_id=1, source_target_pairs={{0,2},{2,0},{1,3},{3,1},{4,6},{6,4},{5,7},{7,5},{8,10},{10,8},{9,1... | collective-permute-start | bytes 1179656 | tf_op jit(solution)/shard_map/ppermute | solution.py:437
  4.2 6.3 %copy-start.1 = (f32[768,768]{1,0:T(8,128)S(1)}, f32[768,768]{1,0:T(8,128)}, u32[]{:S(2)}) copy-start(f32[768,768]{1,0:T(8,128)} %hop_ref.1) | copy-start | bytes 7077892
  4.2 3.6 %collective-permute-start.2 = (bf16[4,768]{1,0:T(4,128)(2,1)S(1)}, bf16[4,768]{1,0:T(4,128)(2,1)S(1)}, u32[]{:S(2)}, u32[]{:S(2)}) collective-permute-start(bf16[4,768]{1,0:T(4,128)(2,1)S(1)} %hold.1.held_ref), channel_id=1, source_target_pairs={{0,4},{4,0},{8,12},{12,8},{1,5},{5,1},{9,13},{13,9},{2,6},{6,2},{1... | collective-permute-start | bytes 18440 | tf_op jit(solution)/shard_map/ppermute | solution.py:415
  7.9 4.7 %collective-permute-start.3 = (bf16[8,768]{1,0:T(8,128)(2,1)S(1)}, bf16[8,768]{1,0:T(8,128)(2,1)S(1)}, u32[]{:S(2)}, u32[]{:S(2)}) collective-permute-start(bf16[8,768]{1,0:T(8,128)(2,1)S(1)} %join.1.refs_0_), channel_id=1, source_target_pairs={{0,8},{4,12},{8,0},{12,4},{1,9},{5,13},{9,1},{13,5},{2,10},{6,14},... | collective-permute-start | bytes 36872 | tf_op jit(solution)/shard_map/ppermute | solution.py:415
  15.1 8.5 %collective-permute-start.5 = (bf16[4,384,256]{2,1,0:T(8,128)(2,1)S(1)}, bf16[4,384,256]{2,1,0:T(8,128)(2,1)S(1)}, u32[]{:S(2)}, u32[]{:S(2)}) collective-permute-start(bf16[4,384,256]{2,1,0:T(8,128)(2,1)S(1)} %get-tuple-element.24), channel_id=1, source_target_pairs={{0,1},{1,0},{2,3},{3,2},{4,5},{5,4},{6,7},{7,6},{8,9},{9,8},{10,11... | collective-permute-start | bytes 2359304 | tf_op jit(solution)/shard_map/ppermute | solution.py:444
  15.2 7.3 %collective-permute-start = (bf16[768,128]{1,0:T(8,128)(2,1)S(1)}, bf16[768,128]{1,0:T(8,128)(2,1)S(1)}, u32[]{:S(2)}, u32[]{:S(2)}) collective-permute-start(bf16[768,128]{1,0:T(8,128)(2,1)S(1)} %get-tuple-element.18.refs_1_), channel_id=1, source_target_pairs={{0,2},{2,0},{1,3},{3,1},{4,6},{6,4},{5,7},{7,5},{8,10},{10,8},{9,1... | collective-permute-start | bytes 589832 | tf_op jit(solution)/shard_map/ppermute | solution.py:438
  22.5 2.4 %collective-permute-start.1 = (bf16[768,128]{1,0:T(8,128)(2,1)S(1)}, bf16[768,128]{1,0:T(8,128)(2,1)S(1)}, u32[]{:S(2)}, u32[]{:S(2)}) collective-permute-start(bf16[768,128]{1,0:T(8,128)(2,1)S(1)} %collective-permute-done.refs_0_), channel_id=1, source_target_pairs={{0,1},{1,0},{2,3},{3,2},{4,5},{5,4},{6,7},{7,6},{8,9},{9,8},{10,11... | collective-permute-start | bytes 589832 | tf_op jit(solution)/shard_map/ppermute | solution.py:447
  22.5 1.3 %copy-start = (bf16[768,768]{1,0:T(8,128)(2,1)S(1)}, bf16[768,768]{1,0:T(8,128)(2,1)}, u32[]{:S(2)}) copy-start(bf16[768,768]{1,0:T(8,128)(2,1)} %refs_4_.1) | copy-start | bytes 3538948

commit v4 on v3

--- a/solution.py
+++ b/solution.py
@@ -12,6 +12,7 @@
 keep_share = 0.8
 hop_share = 0.3
 LANES = 128
+PIECES = 4
 
 
 VMEM = pl.BlockSpec(memory_space=pltpu.VMEM)
@@ -93,10 +94,12 @@
 
 def hop_turned(narrow, high_t, low_t):
     hopped = jnp.dot(narrow, high_t[...], preferred_element_type=jnp.float32)
-    return hopped + jnp.dot(narrow, low_t[...], preferred_element_type=jnp.float32)
-
-
-def lift_kernel(seed_t, high_t, low_t, image_out):
+    if low_t is not None:
+        hopped += jnp.dot(narrow, low_t[...], preferred_element_type=jnp.float32)
+    return hopped
+
+
+def lift_kernel(seed_t, high_t, low_t, _, image_out):
     narrow = seed_t[...]
     hopped = hop_turned(narrow, high_t, low_t)
     image_out[...] = keep_share * narrow.astype(jnp.float32) + hopped
@@ -106,8 +109,8 @@
     out_ref[...] = jnp.concatenate([held_ref[...], came_ref[...]], axis=0)
 
 
-def weigh_kernel(row_count, doubled, *refs):
-    *line_refs, scale_out, column_out = refs
+def early_kernel(row_count, doubled, image_ref, high_t, low_t, *refs):
+    *line_refs, turned_out, image_out, scale_out, column_out = refs
     wraps = scale_out.shape[0]
     row_index = lax.axis_index("rowt")
     lines = jnp.concatenate([ref[...].astype(jnp.float32) for ref in line_refs], axis=0)
@@ -122,6 +125,10 @@
             spins = lines[step : step + 1]
         sign = jnp.where(target == 0, -1.0, 1.0)
         scales.append(sign * jnp.exp(coupling * (2.0 * spins - 1.0)))
+    turned = scales[0] * image_ref[...]
+    narrow = turned.astype(jnp.bfloat16)
+    turned_out[0] = narrow
+    image_out[...] = keep_share * turned + hop_turned(narrow, high_t, low_t)
     scale = jnp.concatenate(scales, axis=0)
     scale_out[...] = scale
     columns = scale.T
@@ -137,32 +144,42 @@
         narrow = turned.astype(jnp.bfloat16)
         turned_out[step] = narrow
         if first + step < total - 1:
-            image = keep_share * turned + hop_turned(narrow, high_t, low_t)
+            low = low_t if first + step < total - 2 else None
+            image = keep_share * turned + hop_turned(narrow, high_t, low)
     if rest:
         rest[0][...] = image
 
 
-def advance(step, spans, hop_ref, scale_ref, level, narrow):
-    source, target = step % 2, (step + 1) % 2
-    copies = level.shape[1] // LANES
-    for span in spans:
-        hopped = jnp.dot(hop_ref[span, :], narrow[source], preferred_element_type=jnp.float32)
-        scale = jnp.concatenate([scale_ref[step, span, :]] * copies, axis=1)
-        moved = scale * (keep_share * level[span, :] + hopped)
-        rounded = moved.astype(jnp.bfloat16)
-        level[span, :] = moved
-        narrow[target, span, :] = rounded
-        yield rounded
-
-
-def chain_kernel(arrived, hop_ref, scale_ref, keep_out, send_out, level, narrow):
-    width = keep_out.shape[1]
-    spans = [slice(0, width), slice(width, 2 * width)]
-    narrow[0] = arrived[...]
-    level[...] = arrived[...].astype(jnp.float32)
+def spread(columns, pieces):
+    size = columns.shape[0] // pieces
+    starts = range(0, columns.shape[0], size)
+    return [columns[start : start + size].astype(jnp.float32) for start in starts]
+
+
+def advance(step, halves, hop_ref, scale_ref, level, narrow):
+    size, copies = level[0].shape[0], level[0].shape[1] // LANES
+    source = jnp.concatenate(narrow, axis=0)
+    new, fresh = [], []
+    each = len(level) // 2
+    for half in range(halves):
+        for number in range(half * each, half * each + each):
+            span = slice(number * size, (number + 1) * size)
+            hopped = jnp.dot(hop_ref[span, :], source, preferred_element_type=jnp.float32)
+            scale = jnp.concatenate([scale_ref[step, span, :]] * copies, axis=1)
+            moved = scale * (keep_share * level[number] + hopped)
+            new.append(moved)
+            fresh.append(moved.astype(jnp.bfloat16))
+        yield jnp.concatenate(fresh[half * each : half * each + each], axis=0)
+    if halves == 2:
+        level[:], narrow[:] = new, fresh
+
+
+def chain_kernel(arrived, hop_ref, scale_ref, keep_out, send_out):
+    level = spread(arrived[...], PIECES)
+    narrow = [block.astype(jnp.bfloat16) for block in level]
     for step in range(keep_out.shape[0]):
-        rounded = advance(step, spans, hop_ref, scale_ref, level, narrow)
-        for out, value in zip((keep_out, send_out), rounded):
+        rounded = advance(step, 2, hop_ref, scale_ref, level, narrow)
+        for value, out in zip(rounded, (keep_out, send_out)):
             out[step] = value
 
 
@@ -182,6 +199,12 @@
     places = (site, lax.axis_size("site") - 1 - site)
     held = [slice(offset, offset + part), slice(width + offset, width + offset + part)]
     return held, [pl.ds(pl.multiple_of(p * width + offset, LANES), part) for p in places]
+
+
+def against(corner, product):
+    return lax.dot_general(
+        corner, product, (((1,), (1,)), ((), ())), preferred_element_type=jnp.float32
+    )
 
 
 def sum_kernel(offset, ours, theirs, *refs):
@@ -194,48 +217,39 @@
             product = multiply(met_ref[step], own)
             pairs = product if pairs is None else pairs + product
         for half in split_halves(pairs):
-            part = lax.dot_general(
-                vertex_ref[:, spot],
-                half,
-                (((1,), (1,)), ((), ())),
-                preferred_element_type=jnp.float32,
-            )
+            part = against(vertex_ref[:, spot], half)
             total = part if total is None else total + part
     out_ref[...] = total
 
 
 def finish_kernel(offset, *refs):
-    ours, theirs, hop_ref, scale_ref, vertex_ref, total_ref, *turned_refs = refs[:-5]
-    out_ref, level, narrow, result, sems = refs[-5:]
+    ours, theirs, hop_ref, scale_ref, vertex_ref, total_ref, *turned_refs = refs[:-3]
+    out_ref, result, sems = refs[-3:]
     wraps, (sites, width) = scale_ref.shape[0], total_ref.shape
     spans = [slice(0, width), slice(width, 2 * width)]
     held, spots = columns_at(offset, ours.shape[1], width)
     other = jnp.concatenate([theirs[span, :] for span in reversed(spans)], axis=0)
-    arrived = jnp.concatenate([ours[...], other], axis=1)
-    narrow[0] = arrived
-    level[...] = arrived.astype(jnp.float32)
+    level = spread(jnp.concatenate([ours[...], other], axis=1), PIECES)
+    narrow = [block.astype(jnp.bfloat16) for block in level]
     pairs = None
     for step, own in enumerate(own_levels(turned_refs, held)):
-        needed = spans if step < wraps - 1 else spans[:1]
-        met = list(advance(step, needed, hop_ref, scale_ref, level, narrow))[0]
+        halves = 2 if step < wraps - 1 else 1
+        met, *_ = advance(step, halves, hop_ref, scale_ref, level, narrow)
         product = multiply(met, own)
         pairs = product if pairs is None else pairs + product
     halves = split_halves(pairs)
-    blocks = sems.shape[0]
-    size = sites // blocks
+    edges = [0, sites - sites // 4, sites]
     copies = []
-    for block in range(blocks):
-        span = slice(block * size, (block + 1) * size)
+    for block, (begin, end) in enumerate(zip(edges, edges[1:])):
+        span = slice(begin, end)
         corner = jnp.concatenate([vertex_ref[span, spot] for spot in spots], axis=1)
         total = total_ref[span, :]
         for half in halves:
-            total = total + lax.dot_general(
-                corner, half, (((1,), (1,)), ((), ())), preferred_element_type=jnp.float32
-            )
+            total = total + against(corner, half)
         result[span, :] = (total / wraps).astype(result.dtype)
         copy = pltpu.make_async_copy(
-            result.at[pl.ds(block * size, size)],
-            out_ref.at[pl.ds(block * size, size)],
+            result.at[pl.ds(begin, end - begin)],
+            out_ref.at[pl.ds(begin, end - begin)],
             sems.at[block],
         )
         copy.start()
@@ -291,17 +305,17 @@
     )(hop_matrix, *pieces)
 
 
-def lift(seed_t, high_t, low_t):
+def lift(seed_t, high_t, low_t, vertex):
     width, sites = seed_t.shape
     return pl.pallas_call(
         lift_kernel,
         out_shape=jax.ShapeDtypeStruct((width, sites), jnp.float32),
-        in_specs=[VMEM] * 3,
+        in_specs=[VMEM] * 4,
         out_specs=VMEM,
         compiler_params=limit(16),
         cost_estimate=work(width, sites, 2),
         name="lift",
-    )(seed_t, high_t, low_t)
+    )(seed_t, high_t, low_t, vertex)
 
 
 def join(held, came):
@@ -316,19 +330,22 @@
     )(held, came)
 
 
-def weigh(wraps, lines, doubled):
-    sites = lines[0].shape[1]
-    return pl.pallas_call(
-        functools.partial(weigh_kernel, lax.axis_size("rowt"), doubled),
+def start_own(wraps, image, high_t, low_t, lines, doubled):
+    width, sites = image.shape
+    return pl.pallas_call(
+        functools.partial(early_kernel, lax.axis_size("rowt"), doubled),
         out_shape=[
+            jax.ShapeDtypeStruct((1, width, sites), jnp.bfloat16),
+            jax.ShapeDtypeStruct((width, sites), jnp.float32),
             jax.ShapeDtypeStruct((wraps, sites), jnp.float32),
             jax.ShapeDtypeStruct((wraps, sites, LANES), jnp.float32),
         ],
-        in_specs=[VMEM] * len(lines),
-        out_specs=[VMEM] * 2,
-        compiler_params=limit(8),
-        name="weigh",
-    )(*lines)
+        in_specs=[VMEM] * (3 + len(lines)),
+        out_specs=[VMEM] * 4,
+        compiler_params=limit(16),
+        cost_estimate=work(width, sites, 2),
+        name="early",
+    )(image, high_t, low_t, *lines)
 
 
 def propagate(first, last, image, high_t, low_t, scale):
@@ -344,21 +361,13 @@
         out_specs=[VMEM] * len(outs),
         compiler_params=limit(16),
         cost_estimate=work(width, sites, 2 * steps),
-        name="late" if first else "early",
     )(image, high_t, low_t, scale)
 
 
 def work(columns, sites, wraps):
     return pl.CostEstimate(
-        flops=2 * wraps * sites * sites * columns, bytes_accessed=1 << 22, transcendentals=0
+        flops=wraps * sites * sites * columns // 16, bytes_accessed=1 << 16, transcendentals=0
     )
-
-
-def levels(sites, columns):
-    return [
-        pltpu.VMEM((sites, columns), jnp.float32),
-        pltpu.VMEM((2, sites, columns), jnp.bfloat16),
-    ]
 
 
 def chain(arrived, hop, scale, width):
@@ -370,7 +379,6 @@
         out_shape=[shape] * 2,
         in_specs=[VMEM] * 3,
         out_specs=[VMEM] * 2,
-        scratch_shapes=levels(sites, columns),
         compiler_params=limit(16),
         cost_estimate=work(columns, sites, wraps),
         name="chain",
@@ -399,8 +407,10 @@
         out_shape=jax.ShapeDtypeStruct((sites, width), jnp.bfloat16),
         in_specs=[VMEM] * (6 + len(turned)),
         out_specs=HBM,
-        scratch_shapes=levels(sites, 2 * ours.shape[1])
-        + [pltpu.VMEM((sites, width), jnp.bfloat16), pltpu.SemaphoreType.DMA((blocks,))],
+        scratch_shapes=[
+            pltpu.VMEM((sites, width), jnp.bfloat16),
+            pltpu.SemaphoreType.DMA((blocks,)),
+        ],
         compiler_params=limit(16),
         cost_estimate=work(2 * ours.shape[1], sites, columns.shape[0]),
         name="finish",
@@ -438,15 +448,15 @@
     second = lax.ppermute(pieces[1], "colt", across)
     found, doubled = fetch_lines(hold(lines))
     hop, high_t, low_t, seed_t = prepare(hop_matrix, pieces)
-    image = lift(seed_t, high_t, low_t)
-    scale, columns = weigh(wraps, found, doubled)
+    image = lift(seed_t, high_t, low_t, vertex)
+    early, image, scale, columns = start_own(wraps, image, high_t, low_t, found, doubled)
     keep, send = chain(first, hop, columns, width)
     came = lax.ppermute(send, "site", swap)
     middle = wraps // 2
-    early, image = propagate(0, middle, image, high_t, low_t, scale)
+    inner, image = propagate(1, middle, image, high_t, low_t, scale)
     other = lax.ppermute(second, "site", swap)
     (late,) = propagate(middle, wraps, image, high_t, low_t, scale)
-    turned = [early, late]
+    turned = [early, inner, late]
     total = add_up(0, keep, came, turned, vertex)
     result = finish(edge, second, other, hop, columns, vertex, total, turned)
     return result[None, None]

time: 28.2 us -> 29.3 us (1.039)
  waiting for transfers between devices: 5.13 us -> 8.35 us
  Pallas kernels: 13.5 us -> 12.1 us
  starting transfers between devices: 9.14 us -> 8.35 us
    ppermute x1, waiting for transfers between devices: 1.97 us -> 6.29 us  [per_device(): second = lax.ppermute(pieces[1], 'colt', across)]
    pallas_call x2, Pallas kernels: 3.53 us -> 1.8 us  [propagate(): pl.pallas_call(functools.partial(own_kernel, first), out_shape=outs, in_s...]
    ppermute x2, waiting for transfers between devices: 3.02 us -> 2.06 us  [fetch_lines(): came = lax.ppermute(lines, 'rowt', [(i, i ^ bit) for i in range(rows)])]
    ppermute x1, starting transfers between devices: 1.8 us -> 1.02 us  [per_device(): second = lax.ppermute(pieces[1], 'colt', across)]
    pallas_call x1, Pallas kernels: 0.66 us -> 1.2 us  [start_own(): pl.pallas_call(functools.partial(early_kernel, lax.axis_size('rowt'), dou...]
  transfers between devices with their start and end apart: 6 -> 6, of which waited for: 4 -> 2; matrix products, arithmetic and copies ran while one was open for 0% -> 0% of each run, Pallas kernels for 26% -> 22%
where the time goes in v4:
time: 29.3 us; the launch traced here: 29.1 us
  Pallas kernels  12.1 us (41%)
  starting transfers between devices  8.35 us (28%)
  waiting for transfers between devices  8.35 us (28%)
    ppermute x1, waiting for transfers between devices, per_device(): second = lax.ppermute(pieces[1], 'colt', across)  6.29 us
    ppermute x2, starting transfers between devices, fetch_lines(): came = lax.ppermute(lines, 'rowt', [(i, i ^ bit) for i in range(rows)])  4.23 us
    ppermute x1, starting transfers between devices, per_device(): first = lax.ppermute(pieces[0], 'colt', across)  3.03 us
    pallas_call x1, Pallas kernels, finish(): pl.pallas_call(functools.partial(finish_kernel, offset), out_shape=jax.Sh...  2.88 us
    ppermute x2, waiting for transfers between devices, fetch_lines(): came = lax.ppermute(lines, 'rowt', [(i, i ^ bit) for i in range(rows)])  2.06 us
    pallas_call x2, Pallas kernels, propagate(): pl.pallas_call(functools.partial(own_kernel, first), out_shape=outs, in_s...  1.8 us
    pallas_call x1, Pallas kernels, chain(): pl.pallas_call(chain_kernel, out_shape=[shape] * 2, in_specs=[VMEM] * 3,...  1.72 us
    pallas_call x1, Pallas kernels, start_own(): pl.pallas_call(functools.partial(early_kernel, lax.axis_size('rowt'), dou...  1.2 us
  transfers between devices with their start and end apart: 6, of which 2 were waited for; matrix products, arithmetic and copies ran while one was open for 0% of the time, Pallas kernels for 22%

profile of v4, /device:TPU:0, one launch (start us, length us, event | category | flops | bytes accessed | tf_op | source)
XLA Modules:
  0.0 29.1 jit_solution(15697201474740146583)
XLA Ops:
  0.0 1.2 %cut.1 = (bf16[768,256]{1,0:T(8,128)(2,1)S(1)}, bf16[768,128]{1,0:T(8,128)(2,1)S(1)}, bf16[4,768]{1,0:T(4,128)(2,1)S(1)}) custom-call(bf16[768,384]{1,0:T(8,128)(2,1)} %bitcast.2, s32[4,1,768]{2,1,0:T(1,128)} %spins_ref.1), custom_call_target="tpu_custom_call" | custom-call | tf_op jit(solution)/shard_map/cut/pallas_call | solution.py:265
  1.2 3.0 %collective-permute-start.4 = (bf16[768,256]{1,0:T(8,128)(2,1)S(1)}, bf16[768,256]{1,0:T(8,128)(2,1)S(1)}, u32[]{:S(2)}, u32[]{:S(2)}) collective-permute-start(bf16[768,256]{1,0:T(8,128)(2,1)S(1)} %get-tuple-element.21.refs_0_), channel_id=1, source_target_pairs={{0,2},{2,0},{1,3},{3,1},{4,6},{6,4},{5,7},{7,5},{8,10},{10,8},{9,1... | collective-permute-start | bytes 1179656 | tf_op jit(solution)/shard_map/ppermute | solution.py:447
  4.2 0.0 copy-start.1
  4.2 1.6 %collective-permute-start.2 = (bf16[4,768]{1,0:T(4,128)(2,1)S(1)}, bf16[4,768]{1,0:T(4,128)(2,1)S(1)}, u32[]{:S(2)}, u32[]{:S(2)}) collective-permute-start(bf16[4,768]{1,0:T(4,128)(2,1)S(1)} %hold.1.held_ref), channel_id=1, source_target_pairs={{0,4},{4,0},{8,12},{12,8},{1,5},{5,1},{9,13},{13,9},{2,6},{6,2},{1... | collective-permute-start | bytes 18440 | tf_op jit(solution)/shard_map/ppermute | solution.py:425
  5.8 2.1 %collective-permute-done.2.came_ref = bf16[4,768]{1,0:T(4,128)(2,1)S(1)} collective-permute-done((bf16[4,768]{1,0:T(4,128)(2,1)S(1)}, bf16[4,768]{1,0:T(4,128)(2,1)S(1)}, u32[]{:S(2)}, u32[]{:S(2)}) %collective-permute-start.2) | collective-permute-done | bytes 6176 | tf_op jit(solution)/shard_map/ppermute | solution.py:425
  7.9 2.7 %collective-permute-start.3 = (bf16[8,768]{1,0:T(8,128)(2,1)S(1)}, bf16[8,768]{1,0:T(8,128)(2,1)S(1)}, u32[]{:S(2)}, u32[]{:S(2)}) collective-permute-start(bf16[8,768]{1,0:T(8,128)(2,1)S(1)} %join.1.refs_0_), channel_id=1, source_target_pairs={{0,8},{4,12},{8,0},{12,4},{1,9},{5,13},{9,1},{13,5},{2,10},{6,14},... | collective-permute-start | bytes 36872 | tf_op jit(solution)/shard_map/ppermute | solution.py:425
  10.5 0.0 copy-done.1
  10.5 0.0 copy-start
  10.5 1.0 %prepare.1 = (bf16[768,768]{1,0:T(8,128)(2,1)S(1)}, bf16[768,768]{1,0:T(8,128)(2,1)S(1)}, bf16[768,768]{1,0:T(8,128)(2,1)S(1)}, bf16[384,768]{1,0:T(8,128)(2,1)S(1)}) custom-call(f32[768,768]{1,0:T(8,128)S(1)} %copy-done.1, bf16[768,256]{1,0:T(8,128)(2,1)S(1)} %get-tuple-element.21.refs_0_, bf16[768,128]{1,0:T(8,128)(2,1)S(1)} %get-tuple-element.20.refs_1_), custom_call_target="tpu_custom_call" | custom-call | flops 268435456 | bytes 4194304 | tf_op jit(solution)/shard_map/prepare/pallas_call | solution.py:297
  11.6 0.2 copy-done
  11.8 1.1 %lift.1.image_ref = f32[384,768]{1,0:T(8,128)S(1)} custom-call(bf16[384,768]{1,0:T(8,128)(2,1)S(1)} %get-tuple-element.23.seed_t, bf16[768,768]{1,0:T(8,128)(2,1)S(1)} %get-tuple-element.24.high_t, bf16[768,768]{1,0:T(8,128)(2,1)S(1)} %get-tuple-element.25.low_t, bf16[768,768]{1,0:T(8,128)(2,1)S(1)} %copy-done), custom_call_target="tpu_custom_call" | custom-call | flops 28311552 | bytes 65536 | tf_op jit(solution)/shard_map/lift/pallas_call | solution.py:310
  12.9 0.0 collective-permute-done.3.refs_1_
  12.9 1.2 %early.1 = (bf16[1,384,768]{2,1,0:T(8,128)(2,1)S(1)}, f32[384,768]{1,0:T(8,128)S(1)}, f32[4,768]{1,0:T(4,128)S(1)}, f32[4,768,128]{2,1,0:T(8,128)S(1)}) custom-call(f32[384,768]{1,0:T(8,128)S(1)} %lift.1.image_ref, bf16[768,768]{1,0:T(8,128)(2,1)S(1)} %get-tuple-element.24.high_t, bf16[768,768]{1,0:T(8,128)(2,1)S(1)} %get-tuple-element.25.low_t, ...), custom_call_target="tpu_custom_call" | custom-call | flops 28311552 | bytes 65536 | tf_op jit(solution)/shard_map/early/pallas_call | solution.py:335
  14.1 0.0 collective-permute-done.4.arrived
  14.1 1.7 %chain.1 = (bf16[4,384,256]{2,1,0:T(8,128)(2,1)S(1)}, bf16[4,384,256]{2,1,0:T(8,128)(2,1)S(1)}) custom-call(bf16[768,256]{1,0:T(8,128)(2,1)S(1)} %collective-permute-done.4.arrived, bf16[768,768]{1,0:T(8,128)(2,1)S(1)} %get-tuple-element.22.hop_ref.refs_2_, f32[4,768,128]{2,1,0:T(8,128)S(1)} %get-tuple-element.27.scale_ref.refs_3_), custom_call_target="tpu_custom_call" | custom-call | flops 37748736 | bytes 65536 | tf_op jit(solution)/shard_map/chain/pallas_call | solution.py:377
  15.8 0.1 collective-permute-start.5
  15.9 1.0 %collective-permute-start = (bf16[768,128]{1,0:T(8,128)(2,1)S(1)}, bf16[768,128]{1,0:T(8,128)(2,1)S(1)}, u32[]{:S(2)}, u32[]{:S(2)}) collective-permute-start(bf16[768,128]{1,0:T(8,128)(2,1)S(1)} %get-tuple-element.20.refs_1_), channel_id=1, source_target_pairs={{0,2},{2,0},{1,3},{3,1},{4,6},{6,4},{5,7},{7,5},{8,10},{10,8},{9,1... | collective-permute-start | bytes 589832 | tf_op jit(solution)/shard_map/ppermute | solution.py:448
  16.9 6.3 %collective-permute-done.refs_0_ = bf16[768,128]{1,0:T(8,128)(2,1)S(1)} collective-permute-done((bf16[768,128]{1,0:T(8,128)(2,1)S(1)}, bf16[768,128]{1,0:T(8,128)(2,1)S(1)}, u32[]{:S(2)}, u32[]{:S(2)}) %collective-permute-start) | collective-permute-done | bytes 196640 | tf_op jit(solution)/shard_map/ppermute | solution.py:448
  23.2 0.0 collective-permute-start.1
  23.2 1.1 %shard_map.46 = (bf16[1,384,768]{2,1,0:T(8,128)(2,1)S(1)}, f32[384,768]{1,0:T(8,128)S(1)}) custom-call(f32[384,768]{1,0:T(8,128)S(1)} %get-tuple-element.31.image_ref, bf16[768,768]{1,0:T(8,128)(2,1)S(1)} %get-tuple-element.24.high_t, bf16[768,768]{1,0:T(8,128)(2,1)S(1)} %get-tuple-element.25.low_t, f32[4,768]{1,0:T(4,128)S(1)} %get-tuple-element.32.scale_ref), custom_call_target="tpu_custom_call" | custom-call | flops 28311552 | bytes 65536 | tf_op jit(solution)/shard_map/pallas_call | solution.py:357
  24.3 0.7 %shard_map.47.refs_2_.refs_8_ = bf16[2,384,768]{2,1,0:T(8,128)(2,1)S(1)} custom-call(f32[384,768]{1,0:T(8,128)S(1)} %get-tuple-element.34.image_ref, bf16[768,768]{1,0:T(8,128)(2,1)S(1)} %get-tuple-element.24.high_t, bf16[768,768]{1,0:T(8,128)(2,1)S(1)} %get-tuple-element.25.low_t, f32[4,768]{1,0:T(4,128)S(1)} %get-tuple-element.32.scale_ref), custom_call_target="tpu_custom_call" | custom-call | flops 56623104 | bytes 65536 | tf_op jit(solution)/shard_map/pallas_call | solution.py:357
  25.0 0.0 collective-permute-done.5.theirs
  25.1 1.2 %add_up.1.refs_5_ = f32[768,384]{1,0:T(8,128)S(1)} custom-call(bf16[4,384,256]{2,1,0:T(8,128)(2,1)S(1)} %get-tuple-element.28.ours, bf16[4,384,256]{2,1,0:T(8,128)(2,1)S(1)} %collective-permute-done.5.theirs, bf16[1,384,768]{2,1,0:T(8,128)(2,1)S(1)} %get-tuple-element.30.refs_0_.refs_6_, bf16[1,384,768]{2,1,0:T(8,128)(2,1)S(1)} %get-tuple-element.33.refs_1_.refs_7_, ...), custom_call_target="tpu_custom_call" | custom-call | flops 18874368 | bytes 65536 | tf_op jit(solution)/shard_map/add_up/pallas_call | solution.py:391
  26.2 0.0 collective-permute-done.1.refs_1_
  26.2 2.9 %finish.1 = bf16[768,384]{1,0:T(8,128)(2,1)} custom-call(bf16[768,128]{1,0:T(8,128)(2,1)S(1)} %collective-permute-done.refs_0_, bf16[768,128]{1,0:T(8,128)(2,1)S(1)} %collective-permute-done.1.refs_1_, bf16[768,768]{1,0:T(8,128)(2,1)S(1)} %get-tuple-element.22.hop_ref.refs_2_, f32[4,768,128]{2,1,0:T(8,128)S(1)} %get-tuple-element.27.scale_ref.refs_3_, ...), custom_call_target="tpu_custom_call" | custom-call | flops 37748736 | bytes 65536 | tf_op jit(solution)/shard_map/finish/pallas_call | solution.py:405
  (2 shorter events, 0.0 us)
Async XLA Ops:
  1.2 12.9 %collective-permute-start.4 = (bf16[768,256]{1,0:T(8,128)(2,1)S(1)}, bf16[768,256]{1,0:T(8,128)(2,1)S(1)}, u32[]{:S(2)}, u32[]{:S(2)}) collective-permute-start(bf16[768,256]{1,0:T(8,128)(2,1)S(1)} %get-tuple-element.21.refs_0_), channel_id=1, source_target_pairs={{0,2},{2,0},{1,3},{3,1},{4,6},{6,4},{5,7},{7,5},{8,10},{10,8},{9,1... | collective-permute-start | bytes 1179656 | tf_op jit(solution)/shard_map/ppermute | solution.py:447
  4.2 6.3 %copy-start.1 = (f32[768,768]{1,0:T(8,128)S(1)}, f32[768,768]{1,0:T(8,128)}, u32[]{:S(2)}) copy-start(f32[768,768]{1,0:T(8,128)} %hop_ref.1) | copy-start | bytes 7077892
  4.2 3.6 %collective-permute-start.2 = (bf16[4,768]{1,0:T(4,128)(2,1)S(1)}, bf16[4,768]{1,0:T(4,128)(2,1)S(1)}, u32[]{:S(2)}, u32[]{:S(2)}) collective-permute-start(bf16[4,768]{1,0:T(4,128)(2,1)S(1)} %hold.1.held_ref), channel_id=1, source_target_pairs={{0,4},{4,0},{8,12},{12,8},{1,5},{5,1},{9,13},{13,9},{2,6},{6,2},{1... | collective-permute-start | bytes 18440 | tf_op jit(solution)/shard_map/ppermute | solution.py:425
  7.9 5.0 %collective-permute-start.3 = (bf16[8,768]{1,0:T(8,128)(2,1)S(1)}, bf16[8,768]{1,0:T(8,128)(2,1)S(1)}, u32[]{:S(2)}, u32[]{:S(2)}) collective-permute-start(bf16[8,768]{1,0:T(8,128)(2,1)S(1)} %join.1.refs_0_), channel_id=1, source_target_pairs={{0,8},{4,12},{8,0},{12,4},{1,9},{5,13},{9,1},{13,5},{2,10},{6,14},... | collective-permute-start | bytes 36872 | tf_op jit(solution)/shard_map/ppermute | solution.py:425
  10.5 1.3 %copy-start = (bf16[768,768]{1,0:T(8,128)(2,1)S(1)}, bf16[768,768]{1,0:T(8,128)(2,1)}, u32[]{:S(2)}) copy-start(bf16[768,768]{1,0:T(8,128)(2,1)} %refs_4_.1) | copy-start | bytes 3538948
  15.8 9.2 %collective-permute-start.5 = (bf16[4,384,256]{2,1,0:T(8,128)(2,1)S(1)}, bf16[4,384,256]{2,1,0:T(8,128)(2,1)S(1)}, u32[]{:S(2)}, u32[]{:S(2)}) collective-permute-start(bf16[4,384,256]{2,1,0:T(8,128)(2,1)S(1)} %get-tuple-element.29), channel_id=1, source_target_pairs={{0,1},{1,0},{2,3},{3,2},{4,5},{5,4},{6,7},{7,6},{8,9},{9,8},{10,11... | collective-permute-start | bytes 2359304 | tf_op jit(solution)/shard_map/ppermute | solution.py:454
  15.9 7.3 %collective-permute-start = (bf16[768,128]{1,0:T(8,128)(2,1)S(1)}, bf16[768,128]{1,0:T(8,128)(2,1)S(1)}, u32[]{:S(2)}, u32[]{:S(2)}) collective-permute-start(bf16[768,128]{1,0:T(8,128)(2,1)S(1)} %get-tuple-element.20.refs_1_), channel_id=1, source_target_pairs={{0,2},{2,0},{1,3},{3,1},{4,6},{6,4},{5,7},{7,5},{8,10},{10,8},{9,1... | collective-permute-start | bytes 589832 | tf_op jit(solution)/shard_map/ppermute | solution.py:448
  23.2 3.0 %collective-permute-start.1 = (bf16[768,128]{1,0:T(8,128)(2,1)S(1)}, bf16[768,128]{1,0:T(8,128)(2,1)S(1)}, u32[]{:S(2)}, u32[]{:S(2)}) collective-permute-start(bf16[768,128]{1,0:T(8,128)(2,1)S(1)} %collective-permute-done.refs_0_), channel_id=1, source_target_pairs={{0,1},{1,0},{2,3},{3,2},{4,5},{5,4},{6,7},{7,6},{8,9},{9,8},{10,11... | collective-permute-start | bytes 589832 | tf_op jit(solution)/shard_map/ppermute | solution.py:457

commit v5 on v4

--- a/solution.py
+++ b/solution.py
@@ -57,11 +57,7 @@
     spin_copy = pltpu.make_async_copy(spins_ref, spins_in, spin_sem)
     spin_copy.start()
     spin_copy.wait()
-    parts = []
-    for step in range(lines.shape[0]):
-        parts.append(
-            jnp.concatenate([spins_in[step, :, source] for source in sources], axis=1)
-        )
+    parts = [spins_in[step] for step in range(lines.shape[0])]
     lines[...] = jnp.concatenate(parts, axis=0).astype(jnp.float32).astype(jnp.bfloat16)
     for copy in copies:
         copy.wait()
@@ -115,6 +111,9 @@
     row_index = lax.axis_index("rowt")
     lines = jnp.concatenate([ref[...].astype(jnp.float32) for ref in line_refs], axis=0)
     places = lax.broadcasted_iota(jnp.int32, lines.shape, 0)
+    half = lines.shape[1] // 2
+    other = jnp.concatenate([lines[:, half:], lines[:, :half]], axis=1)
+    lines = jnp.where(lax.axis_index("site") == 0, lines, other)
     scales = []
     for step in range(wraps):
         target = (row_index + step + 1) % row_count
@@ -136,18 +135,22 @@
         column_out[step] = jnp.broadcast_to(columns[:, step : step + 1], column_out.shape[1:])
 
 
-def own_kernel(first, image_ref, high_t, low_t, scale_ref, turned_out, *rest):
-    steps, total = turned_out.shape[0], scale_ref.shape[0]
-    image = image_ref[...]
-    for step in range(steps):
-        turned = scale_ref[first + step : first + step + 1, :] * image
-        narrow = turned.astype(jnp.bfloat16)
-        turned_out[step] = narrow
-        if first + step < total - 1:
-            low = low_t if first + step < total - 2 else None
-            image = keep_share * turned + hop_turned(narrow, high_t, low)
-    if rest:
-        rest[0][...] = image
+def rest_kernel(place, first, last, image_ref, high_t, low_t, scale_ref, *refs):
+    wraps = scale_ref.shape[0]
+    turned_out = refs[-1] if last == wraps else refs[-2]
+
+    @pl.when(lax.axis_index("site") == place)
+    def _():
+        image = image_ref[...]
+        for step in range(first, last):
+            turned = scale_ref[step : step + 1, :] * image
+            narrow = turned.astype(jnp.bfloat16)
+            turned_out[step - 1] = narrow
+            if step < wraps - 1:
+                low = low_t if step < wraps - 2 else None
+                image = keep_share * turned + hop_turned(narrow, high_t, low)
+        if last < wraps:
+            refs[-1][...] = image
 
 
 def spread(columns, pieces):
@@ -207,19 +210,27 @@
     )
 
 
-def sum_kernel(offset, ours, theirs, *refs):
-    *turned_refs, vertex_ref, out_ref = refs
-    width = ours.shape[1]
-    total = None
-    for met_ref, held, spot in zip((ours, theirs), *columns_at(offset, ours.shape[2], width)):
-        pairs = None
-        for step, own in enumerate(own_levels(turned_refs, [held])):
-            product = multiply(met_ref[step], own)
-            pairs = product if pairs is None else pairs + product
-        for half in split_halves(pairs):
-            part = against(vertex_ref[:, spot], half)
-            total = part if total is None else total + part
-    out_ref[...] = total
+def sum_part(offset, which, met_ref, vertex_ref, turned_refs):
+    _, width, part = met_ref.shape
+    held, spots = columns_at(offset, part, width)
+    pairs = None
+    for step, own in enumerate(own_levels(turned_refs, [held[which]])):
+        product = multiply(met_ref[step], own)
+        pairs = product if pairs is None else pairs + product
+    corner = vertex_ref[:, spots[which]]
+    high, low = split_halves(pairs)
+    return against(corner, high) + against(corner, low)
+
+
+def ours_kernel(offset, place, met_ref, vertex_ref, early_ref, rest_ref, *refs):
+    @pl.when(lax.axis_index("site") == place)
+    def _():
+        refs[-1][...] = sum_part(offset, 0, met_ref, vertex_ref, (early_ref, rest_ref))
+
+
+def theirs_kernel(offset, met_ref, vertex_ref, early_ref, rest_ref, total_ref, out_ref):
+    part = sum_part(offset, 1, met_ref, vertex_ref, (early_ref, rest_ref))
+    out_ref[...] = total_ref[...] + part
 
 
 def finish_kernel(offset, *refs):
@@ -348,20 +359,21 @@
     )(image, high_t, low_t, *lines)
 
 
-def propagate(first, last, image, high_t, low_t, scale):
-    width, sites = image.shape
-    wraps, steps = scale.shape[0], last - first
-    outs = [jax.ShapeDtypeStruct((steps, width, sites), jnp.bfloat16)]
+def propagate(place, first, last, image, high_t, low_t, scale, turned=None):
+    (width, sites), wraps = image.shape, scale.shape[0]
+    extra = [] if turned is None else [turned]
+    outs = [jax.ShapeDtypeStruct((wraps - 1, width, sites), jnp.bfloat16)]
     if last < wraps:
         outs.append(jax.ShapeDtypeStruct((width, sites), jnp.float32))
     return pl.pallas_call(
-        functools.partial(own_kernel, first),
+        functools.partial(rest_kernel, place, first, last),
         out_shape=outs,
-        in_specs=[VMEM] * 4,
+        in_specs=[VMEM] * (4 + len(extra)),
         out_specs=[VMEM] * len(outs),
+        input_output_aliases={4: 0} if extra else {},
         compiler_params=limit(16),
-        cost_estimate=work(width, sites, 2 * steps),
-    )(image, high_t, low_t, scale)
+        cost_estimate=work(width, sites, 2 * (last - first)),
+    )(image, high_t, low_t, scale, *extra)
 
 
 def work(columns, sites, wraps):
@@ -385,18 +397,19 @@
     )(arrived, hop, scale)
 
 
-def add_up(offset, ours, theirs, turned, vertex):
-    _, width, columns = ours.shape
+def add_up(kernel, met, vertex, turned, total):
+    _, width, columns = met.shape
     sites = vertex.shape[0]
-    return pl.pallas_call(
-        functools.partial(sum_kernel, offset),
+    extra = [] if total is None else [total]
+    return pl.pallas_call(
+        kernel,
         out_shape=jax.ShapeDtypeStruct((sites, width), jnp.float32),
-        in_specs=[VMEM] * (3 + len(turned)),
+        in_specs=[VMEM] * (2 + len(turned) + len(extra)),
         out_specs=VMEM,
+        input_output_aliases={2 + len(turned): 0} if extra else {},
         compiler_params=limit(16),
-        cost_estimate=work(columns, sites, 2),
-        name="add_up",
-    )(ours, theirs, *turned, vertex)
+        cost_estimate=work(columns, sites, 1),
+    )(met, vertex, *turned, *extra)
 
 
 def finish(offset, ours, theirs, hop, columns, vertex, total, turned):
@@ -419,10 +432,16 @@
 
 def fetch_lines(lines):
     rows, count = lax.axis_size("rowt"), lines.shape[0]
+    sites = lax.axis_size("site")
     if rows == count and rows & (rows - 1) == 0:
         bit = 1
         while bit < rows:
-            came = lax.ppermute(lines, "rowt", [(i, i ^ bit) for i in range(rows)])
+            pairs = [
+                (i * sites + core, (i ^ bit) * sites + sites - 1 - core)
+                for i in range(rows)
+                for core in range(sites)
+            ]
+            came = lax.ppermute(lines, ("rowt", "site"), pairs)
             bit *= 2
             if bit < rows:
                 lines = join(lines, came)
@@ -450,14 +469,21 @@
     hop, high_t, low_t, seed_t = prepare(hop_matrix, pieces)
     image = lift(seed_t, high_t, low_t, vertex)
     early, image, scale, columns = start_own(wraps, image, high_t, low_t, found, doubled)
+    own = (high_t, low_t, scale)
+    rest, level = propagate(0, 1, 2, image, *own)
     keep, send = chain(first, hop, columns, width)
+    for place in range(1, sites):
+        (rest,) = propagate(place, 1, wraps, image, *own, rest)
     came = lax.ppermute(send, "site", swap)
-    middle = wraps // 2
-    inner, image = propagate(1, middle, image, high_t, low_t, scale)
+    (rest,) = propagate(0, 2, wraps, level, *own, rest)
+    turned = [early, rest]
+    total = None
+    for place in range(1, sites):
+        kernel = functools.partial(ours_kernel, 0, place)
+        total = add_up(kernel, keep, vertex, turned, total)
     other = lax.ppermute(second, "site", swap)
-    (late,) = propagate(middle, wraps, image, high_t, low_t, scale)
-    turned = [early, inner, late]
-    total = add_up(0, keep, came, turned, vertex)
+    total = add_up(functools.partial(ours_kernel, 0, 0), keep, vertex, turned, total)
+    total = add_up(functools.partial(theirs_kernel, 0), came, vertex, turned, total)
     result = finish(edge, second, other, hop, columns, vertex, total, turned)
     return result[None, None]
 

time: 29.3 us -> 28.8 us (0.983)
  waiting for transfers between devices: 8.35 us -> 7.86 us
    ppermute x2, starting transfers between devices: 4.23 us -> 3.24 us  [fetch_lines(): came = lax.ppermute(lines, ('rowt', 'site'), pairs)]
    ppermute x1, waiting for transfers between devices: 6.29 us -> 5.53 us  [per_device(): second = lax.ppermute(pieces[1], 'colt', across)]
    ppermute x1, starting transfers between devices: 1.02 us -> 1.53 us  [per_device(): second = lax.ppermute(pieces[1], 'colt', across)]
    pallas_call x3 -> x6, Pallas kernels: 2.95 us -> 3.23 us  [the longest x3 1.78 us: propagate(): pl.pallas_call(functools.partial(rest_kernel, place, first, last), out_sh...]
  transfers between devices with their start and end apart: 6 -> 6, of which waited for: 2 -> 2; matrix products, arithmetic and copies ran while one was open for 0% -> 0% of each run, Pallas kernels for 22% -> 23%
where the time goes in v5:
time: 28.8 us; the launch traced here: 28.5 us
  Pallas kernels  12.2 us (42%)
  starting transfers between devices  8.13 us (28%)
  waiting for transfers between devices  7.86 us (27%)
    ppermute x1, waiting for transfers between devices, per_device(): second = lax.ppermute(pieces[1], 'colt', across)  5.53 us
    ppermute x2, starting transfers between devices, fetch_lines(): came = lax.ppermute(lines, ('rowt', 'site'), pairs)  3.24 us
    ppermute x1, starting transfers between devices, per_device(): first = lax.ppermute(pieces[0], 'colt', across)  3.03 us
    pallas_call x1, Pallas kernels, finish(): pl.pallas_call(functools.partial(finish_kernel, offset), out_shape=jax.Sh...  2.83 us
    ppermute x2, waiting for transfers between devices, fetch_lines(): came = lax.ppermute(lines, ('rowt', 'site'), pairs)  2.32 us
    pallas_call x3, Pallas kernels, propagate(): pl.pallas_call(functools.partial(rest_kernel, place, first, last), out_sh...  1.78 us
    pallas_call x1, Pallas kernels, chain(): pl.pallas_call(chain_kernel, out_shape=[shape] * 2, in_specs=[VMEM] * 3,...  1.68 us
    ppermute x1, starting transfers between devices, per_device(): second = lax.ppermute(pieces[1], 'colt', across)  1.53 us
  transfers between devices with their start and end apart: 6, of which 2 were waited for; matrix products, arithmetic and copies ran while one was open for 0% of the time, Pallas kernels for 23%

profile of v5, /device:TPU:0, one launch (start us, length us, event | category | flops | bytes accessed | tf_op | source)
XLA Modules:
  0.0 28.5 jit_solution(15703023070435592243)
XLA Ops:
  0.0 1.2 %cut.1 = (bf16[768,256]{1,0:T(8,128)(2,1)S(1)}, bf16[768,128]{1,0:T(8,128)(2,1)S(1)}, bf16[4,768]{1,0:T(4,128)(2,1)S(1)}) custom-call(bf16[768,384]{1,0:T(8,128)(2,1)} %bitcast.2, s32[4,1,768]{2,1,0:T(1,128)} %spins_ref.1), custom_call_target="tpu_custom_call" | custom-call | tf_op jit(solution)/shard_map/cut/pallas_call | solution.py:276
  1.2 3.0 %collective-permute-start.4 = (bf16[768,256]{1,0:T(8,128)(2,1)S(1)}, bf16[768,256]{1,0:T(8,128)(2,1)S(1)}, u32[]{:S(2)}, u32[]{:S(2)}) collective-permute-start(bf16[768,256]{1,0:T(8,128)(2,1)S(1)} %get-tuple-element.21.refs_0_), channel_id=1, source_target_pairs={{0,2},{2,0},{1,3},{3,1},{4,6},{6,4},{5,7},{7,5},{8,10},{10,8},{9,1... | collective-permute-start | bytes 1179656 | tf_op jit(solution)/shard_map/ppermute | solution.py:466
  4.2 0.0 copy-start.1
  4.2 0.7 %collective-permute-start.2 = (bf16[4,768]{1,0:T(4,128)(2,1)S(1)}, bf16[4,768]{1,0:T(4,128)(2,1)S(1)}, u32[]{:S(2)}, u32[]{:S(2)}) collective-permute-start(bf16[4,768]{1,0:T(4,128)(2,1)S(1)} %hold.1.held_ref), channel_id=1, source_target_pairs={{0,5},{1,4},{4,1},{5,0},{8,13},{9,12},{12,9},{13,8},{2,7},{3,6},{6... | collective-permute-start | bytes 18440 | tf_op jit(solution)/shard_map/ppermute | solution.py:444
  5.0 2.3 %collective-permute-done.2.came_ref = bf16[4,768]{1,0:T(4,128)(2,1)S(1)} collective-permute-done((bf16[4,768]{1,0:T(4,128)(2,1)S(1)}, bf16[4,768]{1,0:T(4,128)(2,1)S(1)}, u32[]{:S(2)}, u32[]{:S(2)}) %collective-permute-start.2) | collective-permute-done | bytes 6176 | tf_op jit(solution)/shard_map/ppermute | solution.py:444
  7.3 2.5 %collective-permute-start.3 = (bf16[8,768]{1,0:T(8,128)(2,1)S(1)}, bf16[8,768]{1,0:T(8,128)(2,1)S(1)}, u32[]{:S(2)}, u32[]{:S(2)}) collective-permute-start(bf16[8,768]{1,0:T(8,128)(2,1)S(1)} %join.1.refs_0_), channel_id=1, source_target_pairs={{0,9},{1,8},{4,13},{5,12},{8,1},{9,0},{12,5},{13,4},{2,11},{3,10},... | collective-permute-start | bytes 36872 | tf_op jit(solution)/shard_map/ppermute | solution.py:444
  9.8 0.0 copy-done.1
  9.8 0.0 copy-start
  9.8 1.0 %prepare.1 = (bf16[768,768]{1,0:T(8,128)(2,1)S(1)}, bf16[768,768]{1,0:T(8,128)(2,1)S(1)}, bf16[768,768]{1,0:T(8,128)(2,1)S(1)}, bf16[384,768]{1,0:T(8,128)(2,1)S(1)}) custom-call(f32[768,768]{1,0:T(8,128)S(1)} %copy-done.1, bf16[768,256]{1,0:T(8,128)(2,1)S(1)} %get-tuple-element.21.refs_0_, bf16[768,128]{1,0:T(8,128)(2,1)S(1)} %get-tuple-element.20.refs_1_), custom_call_target="tpu_custom_call" | custom-call | flops 268435456 | bytes 4194304 | tf_op jit(solution)/shard_map/prepare/pallas_call | solution.py:308
  10.8 0.2 copy-done
  11.1 1.1 %lift.1.image_ref = f32[384,768]{1,0:T(8,128)S(1)} custom-call(bf16[384,768]{1,0:T(8,128)(2,1)S(1)} %get-tuple-element.23.seed_t, bf16[768,768]{1,0:T(8,128)(2,1)S(1)} %get-tuple-element.24.high_t, bf16[768,768]{1,0:T(8,128)(2,1)S(1)} %get-tuple-element.25.low_t, bf16[768,768]{1,0:T(8,128)(2,1)S(1)} %copy-done), custom_call_target="tpu_custom_call" | custom-call | flops 28311552 | bytes 65536 | tf_op jit(solution)/shard_map/lift/pallas_call | solution.py:321
  12.1 0.0 collective-permute-done.3.refs_1_
  12.2 1.2 %early.1 = (bf16[1,384,768]{2,1,0:T(8,128)(2,1)S(1)}, f32[384,768]{1,0:T(8,128)S(1)}, f32[4,768]{1,0:T(4,128)S(1)}, f32[4,768,128]{2,1,0:T(8,128)S(1)}) custom-call(f32[384,768]{1,0:T(8,128)S(1)} %lift.1.image_ref, bf16[768,768]{1,0:T(8,128)(2,1)S(1)} %get-tuple-element.24.high_t, bf16[768,768]{1,0:T(8,128)(2,1)S(1)} %get-tuple-element.25.low_t, ...), custom_call_target="tpu_custom_call" | custom-call | flops 28311552 | bytes 65536 | tf_op jit(solution)/shard_map/early/pallas_call | solution.py:346
  13.3 0.0 collective-permute-done.4.arrived
  13.3 1.7 %chain.1 = (bf16[4,384,256]{2,1,0:T(8,128)(2,1)S(1)}, bf16[4,384,256]{2,1,0:T(8,128)(2,1)S(1)}) custom-call(bf16[768,256]{1,0:T(8,128)(2,1)S(1)} %collective-permute-done.4.arrived, bf16[768,768]{1,0:T(8,128)(2,1)S(1)} %get-tuple-element.22.hop_ref.refs_2_, f32[4,768,128]{2,1,0:T(8,128)S(1)} %get-tuple-element.27.scale_ref.refs_3_), custom_call_target="tpu_custom_call" | custom-call | flops 37748736 | bytes 65536 | tf_op jit(solution)/shard_map/chain/pallas_call | solution.py:389
  15.0 0.3 %collective-permute-start.5 = (bf16[4,384,256]{2,1,0:T(8,128)(2,1)S(1)}, bf16[4,384,256]{2,1,0:T(8,128)(2,1)S(1)}, u32[]{:S(2)}, u32[]{:S(2)}) collective-permute-start(bf16[4,384,256]{2,1,0:T(8,128)(2,1)S(1)} %get-tuple-element.28), channel_id=1, source_target_pairs={{0,1},{1,0},{2,3},{3,2},{4,5},{5,4},{6,7},{7,6},{8,9},{9,8},{10,11... | collective-permute-start | bytes 2359304 | tf_op jit(solution)/shard_map/ppermute | solution.py:477
  15.4 1.5 %collective-permute-start = (bf16[768,128]{1,0:T(8,128)(2,1)S(1)}, bf16[768,128]{1,0:T(8,128)(2,1)S(1)}, u32[]{:S(2)}, u32[]{:S(2)}) collective-permute-start(bf16[768,128]{1,0:T(8,128)(2,1)S(1)} %get-tuple-element.20.refs_1_), channel_id=1, source_target_pairs={{0,2},{2,0},{1,3},{3,1},{4,6},{6,4},{5,7},{7,5},{8,10},{10,8},{9,1... | collective-permute-start | bytes 589832 | tf_op jit(solution)/shard_map/ppermute | solution.py:467
  16.9 5.5 %collective-permute-done.refs_0_ = bf16[768,128]{1,0:T(8,128)(2,1)S(1)} collective-permute-done((bf16[768,128]{1,0:T(8,128)(2,1)S(1)}, bf16[768,128]{1,0:T(8,128)(2,1)S(1)}, u32[]{:S(2)}, u32[]{:S(2)}) %collective-permute-start) | collective-permute-done | bytes 196640 | tf_op jit(solution)/shard_map/ppermute | solution.py:467
  22.4 0.0 collective-permute-start.1
  22.4 1.1 %shard_map.46 = (bf16[3,384,768]{2,1,0:T(8,128)(2,1)S(1)}, f32[384,768]{1,0:T(8,128)S(1)}) custom-call(f32[384,768]{1,0:T(8,128)S(1)} %get-tuple-element.30.image_ref, bf16[768,768]{1,0:T(8,128)(2,1)S(1)} %get-tuple-element.24.high_t, bf16[768,768]{1,0:T(8,128)(2,1)S(1)} %get-tuple-element.25.low_t, f32[4,768]{1,0:T(4,128)S(1)} %get-tuple-element.31.scale_ref), custom_call_target="tpu_custom_call" | custom-call | flops 28311552 | bytes 65536 | tf_op jit(solution)/shard_map/pallas_call | solution.py:368
  23.5 0.7 %shard_map.48.rest_ref.refs_7_ = bf16[3,384,768]{2,1,0:T(8,128)(2,1)S(1)} custom-call(f32[384,768]{1,0:T(8,128)S(1)} %get-tuple-element.32.image_ref, bf16[768,768]{1,0:T(8,128)(2,1)S(1)} %get-tuple-element.24.high_t, bf16[768,768]{1,0:T(8,128)(2,1)S(1)} %get-tuple-element.25.low_t, ...), custom_call_target="tpu_custom_call", output_to_operand_aliasing={{}: (4, {})} | custom-call | flops 56623104 | bytes 65536 | tf_op jit(solution)/shard_map/pallas_call | solution.py:368
  24.3 0.7 %shard_map.50.total_ref = f32[768,384]{1,0:T(8,128)S(1)} custom-call(bf16[4,384,256]{2,1,0:T(8,128)(2,1)S(1)} %get-tuple-element.34.met_ref, bf16[768,768]{1,0:T(8,128)(2,1)S(1)} %copy-done, bf16[1,384,768]{2,1,0:T(8,128)(2,1)S(1)} %get-tuple-element.29.early_ref.refs_6_, ...), custom_call_target="tpu_custom_call", output_to_operand_aliasing={{}: (4, {})} | custom-call | flops 9437184 | bytes 65536 | tf_op jit(solution)/shard_map/pallas_call | solution.py:404
  24.9 0.0 collective-permute-done.5.met_ref
  25.0 0.7 %shard_map.51.refs_5_ = f32[768,384]{1,0:T(8,128)S(1)} custom-call(bf16[4,384,256]{2,1,0:T(8,128)(2,1)S(1)} %collective-permute-done.5.met_ref, bf16[768,768]{1,0:T(8,128)(2,1)S(1)} %copy-done, bf16[1,384,768]{2,1,0:T(8,128)(2,1)S(1)} %get-tuple-element.29.early_ref.refs_6_, ...), custom_call_target="tpu_custom_call", output_to_operand_aliasing={{}: (4, {})} | custom-call | flops 9437184 | bytes 65536 | tf_op jit(solution)/shard_map/pallas_call | solution.py:404
  25.7 0.0 collective-permute-done.1.refs_1_
  25.7 2.8 %finish.1 = bf16[768,384]{1,0:T(8,128)(2,1)} custom-call(bf16[768,128]{1,0:T(8,128)(2,1)S(1)} %collective-permute-done.refs_0_, bf16[768,128]{1,0:T(8,128)(2,1)S(1)} %collective-permute-done.1.refs_1_, bf16[768,768]{1,0:T(8,128)(2,1)S(1)} %get-tuple-element.22.hop_ref.refs_2_, f32[4,768,128]{2,1,0:T(8,128)S(1)} %get-tuple-element.27.scale_ref.refs_3_, ...), custom_call_target="tpu_custom_call" | custom-call | flops 37748736 | bytes 65536 | tf_op jit(solution)/shard_map/finish/pallas_call | solution.py:418
  (4 shorter events, 0.0 us)
Async XLA Ops:
  1.2 12.2 %collective-permute-start.4 = (bf16[768,256]{1,0:T(8,128)(2,1)S(1)}, bf16[768,256]{1,0:T(8,128)(2,1)S(1)}, u32[]{:S(2)}, u32[]{:S(2)}) collective-permute-start(bf16[768,256]{1,0:T(8,128)(2,1)S(1)} %get-tuple-element.21.refs_0_), channel_id=1, source_target_pairs={{0,2},{2,0},{1,3},{3,1},{4,6},{6,4},{5,7},{7,5},{8,10},{10,8},{9,1... | collective-permute-start | bytes 1179656 | tf_op jit(solution)/shard_map/ppermute | solution.py:466
  4.2 5.6 %copy-start.1 = (f32[768,768]{1,0:T(8,128)S(1)}, f32[768,768]{1,0:T(8,128)}, u32[]{:S(2)}) copy-start(f32[768,768]{1,0:T(8,128)} %hop_ref.1) | copy-start | bytes 7077892
  4.2 3.1 %collective-permute-start.2 = (bf16[4,768]{1,0:T(4,128)(2,1)S(1)}, bf16[4,768]{1,0:T(4,128)(2,1)S(1)}, u32[]{:S(2)}, u32[]{:S(2)}) collective-permute-start(bf16[4,768]{1,0:T(4,128)(2,1)S(1)} %hold.1.held_ref), channel_id=1, source_target_pairs={{0,5},{1,4},{4,1},{5,0},{8,13},{9,12},{12,9},{13,8},{2,7},{3,6},{6... | collective-permute-start | bytes 18440 | tf_op jit(solution)/shard_map/ppermute | solution.py:444
  7.3 4.9 %collective-permute-start.3 = (bf16[8,768]{1,0:T(8,128)(2,1)S(1)}, bf16[8,768]{1,0:T(8,128)(2,1)S(1)}, u32[]{:S(2)}, u32[]{:S(2)}) collective-permute-start(bf16[8,768]{1,0:T(8,128)(2,1)S(1)} %join.1.refs_0_), channel_id=1, source_target_pairs={{0,9},{1,8},{4,13},{5,12},{8,1},{9,0},{12,5},{13,4},{2,11},{3,10},... | collective-permute-start | bytes 36872 | tf_op jit(solution)/shard_map/ppermute | solution.py:444
  9.8 1.3 %copy-start = (bf16[768,768]{1,0:T(8,128)(2,1)S(1)}, bf16[768,768]{1,0:T(8,128)(2,1)}, u32[]{:S(2)}) copy-start(bf16[768,768]{1,0:T(8,128)(2,1)} %refs_4_.1) | copy-start | bytes 3538948
  15.0 9.9 %collective-permute-start.5 = (bf16[4,384,256]{2,1,0:T(8,128)(2,1)S(1)}, bf16[4,384,256]{2,1,0:T(8,128)(2,1)S(1)}, u32[]{:S(2)}, u32[]{:S(2)}) collective-permute-start(bf16[4,384,256]{2,1,0:T(8,128)(2,1)S(1)} %get-tuple-element.28), channel_id=1, source_target_pairs={{0,1},{1,0},{2,3},{3,2},{4,5},{5,4},{6,7},{7,6},{8,9},{9,8},{10,11... | collective-permute-start | bytes 2359304 | tf_op jit(solution)/shard_map/ppermute | solution.py:477
  15.4 7.1 %collective-permute-start = (bf16[768,128]{1,0:T(8,128)(2,1)S(1)}, bf16[768,128]{1,0:T(8,128)(2,1)S(1)}, u32[]{:S(2)}, u32[]{:S(2)}) collective-permute-start(bf16[768,128]{1,0:T(8,128)(2,1)S(1)} %get-tuple-element.20.refs_1_), channel_id=1, source_target_pairs={{0,2},{2,0},{1,3},{3,1},{4,6},{6,4},{5,7},{7,5},{8,10},{10,8},{9,1... | collective-permute-start | bytes 589832 | tf_op jit(solution)/shard_map/ppermute | solution.py:467
  22.4 3.3 %collective-permute-start.1 = (bf16[768,128]{1,0:T(8,128)(2,1)S(1)}, bf16[768,128]{1,0:T(8,128)(2,1)S(1)}, u32[]{:S(2)}, u32[]{:S(2)}) collective-permute-start(bf16[768,128]{1,0:T(8,128)(2,1)S(1)} %collective-permute-done.refs_0_), channel_id=1, source_target_pairs={{0,1},{1,0},{2,3},{3,2},{4,5},{5,4},{6,7},{7,6},{8,9},{9,8},{10,11... | collective-permute-start | bytes 589832 | tf_op jit(solution)/shard_map/ppermute | solution.py:484

commit v6 on v5

--- a/solution.py
+++ b/solution.py
@@ -46,7 +46,7 @@
     sources = site_spans(width)
     copies = []
     for (a, b), piece in zip(spans, pieces):
-        for half, source in enumerate(sources):
+        for half, source in enumerate(reversed(sources)):
             copy = pltpu.make_async_copy(
                 seed_ref.at[source, pl.ds(a, b - a)],
                 piece.at[pl.ds(half * width, width)],
@@ -73,7 +73,9 @@
     width, _ = turned_out.shape
     start = 0
     for piece in pieces:
-        turned_out[start : start + piece.shape[1], :] = piece[...].T
+        lines = slice(start, start + piece.shape[1])
+        turned_out[lines, :width] = piece[width:, :].T
+        turned_out[lines, width:] = piece[:width, :].T
         start += piece.shape[1]
     site = lax.axis_index("site")
     places = (site, lax.axis_size("site") - 1 - site)
@@ -135,22 +137,18 @@
         column_out[step] = jnp.broadcast_to(columns[:, step : step + 1], column_out.shape[1:])
 
 
-def rest_kernel(place, first, last, image_ref, high_t, low_t, scale_ref, *refs):
-    wraps = scale_ref.shape[0]
-    turned_out = refs[-1] if last == wraps else refs[-2]
-
-    @pl.when(lax.axis_index("site") == place)
-    def _():
-        image = image_ref[...]
-        for step in range(first, last):
-            turned = scale_ref[step : step + 1, :] * image
-            narrow = turned.astype(jnp.bfloat16)
-            turned_out[step - 1] = narrow
-            if step < wraps - 1:
-                low = low_t if step < wraps - 2 else None
-                image = keep_share * turned + hop_turned(narrow, high_t, low)
-        if last < wraps:
-            refs[-1][...] = image
+def own_kernel(first, image_ref, high_t, low_t, scale_ref, turned_out, *rest):
+    steps, wraps = turned_out.shape[0], scale_ref.shape[0]
+    image = image_ref[...]
+    for step in range(first, first + steps):
+        turned = scale_ref[step : step + 1, :] * image
+        narrow = turned.astype(jnp.bfloat16)
+        turned_out[step - first] = narrow
+        if step < wraps - 1:
+            low = low_t if step < wraps - 2 else None
+            image = keep_share * turned + hop_turned(narrow, high_t, low)
+    if rest:
+        rest[0][...] = image
 
 
 def spread(columns, pieces):
@@ -199,8 +197,8 @@
 
 def columns_at(offset, part, width):
     site = lax.axis_index("site")
-    places = (site, lax.axis_size("site") - 1 - site)
-    held = [slice(offset, offset + part), slice(width + offset, width + offset + part)]
+    places = (lax.axis_size("site") - 1 - site, site)
+    held = [slice(width + offset, width + offset + part), slice(offset, offset + part)]
     return held, [pl.ds(pl.multiple_of(p * width + offset, LANES), part) for p in places]
 
 
@@ -222,15 +220,10 @@
     return against(corner, high) + against(corner, low)
 
 
-def ours_kernel(offset, place, met_ref, vertex_ref, early_ref, rest_ref, *refs):
-    @pl.when(lax.axis_index("site") == place)
-    def _():
-        refs[-1][...] = sum_part(offset, 0, met_ref, vertex_ref, (early_ref, rest_ref))
-
-
-def theirs_kernel(offset, met_ref, vertex_ref, early_ref, rest_ref, total_ref, out_ref):
-    part = sum_part(offset, 1, met_ref, vertex_ref, (early_ref, rest_ref))
-    out_ref[...] = total_ref[...] + part
+def add_kernel(offset, which, met_ref, vertex_ref, *refs):
+    *turned_refs, out_ref = refs
+    total = turned_refs.pop(0)[...] if which else 0.0
+    out_ref[...] = total + sum_part(offset, which, met_ref, vertex_ref, turned_refs)
 
 
 def finish_kernel(offset, *refs):
@@ -248,15 +241,13 @@
         met, *_ = advance(step, halves, hop_ref, scale_ref, level, narrow)
         product = multiply(met, own)
         pairs = product if pairs is None else pairs + product
-    halves = split_halves(pairs)
+    summed = pairs.astype(jnp.bfloat16)
     edges = [0, sites - sites // 4, sites]
     copies = []
     for block, (begin, end) in enumerate(zip(edges, edges[1:])):
         span = slice(begin, end)
         corner = jnp.concatenate([vertex_ref[span, spot] for spot in spots], axis=1)
-        total = total_ref[span, :]
-        for half in halves:
-            total = total + against(corner, half)
+        total = total_ref[span, :] + against(corner, summed)
         result[span, :] = (total / wraps).astype(result.dtype)
         copy = pltpu.make_async_copy(
             result.at[pl.ds(begin, end - begin)],
@@ -359,21 +350,19 @@
     )(image, high_t, low_t, *lines)
 
 
-def propagate(place, first, last, image, high_t, low_t, scale, turned=None):
+def propagate(first, last, image, high_t, low_t, scale):
     (width, sites), wraps = image.shape, scale.shape[0]
-    extra = [] if turned is None else [turned]
-    outs = [jax.ShapeDtypeStruct((wraps - 1, width, sites), jnp.bfloat16)]
+    outs = [jax.ShapeDtypeStruct((last - first, width, sites), jnp.bfloat16)]
     if last < wraps:
         outs.append(jax.ShapeDtypeStruct((width, sites), jnp.float32))
     return pl.pallas_call(
-        functools.partial(rest_kernel, place, first, last),
+        functools.partial(own_kernel, first),
         out_shape=outs,
-        in_specs=[VMEM] * (4 + len(extra)),
+        in_specs=[VMEM] * 4,
         out_specs=[VMEM] * len(outs),
-        input_output_aliases={4: 0} if extra else {},
         compiler_params=limit(16),
         cost_estimate=work(width, sites, 2 * (last - first)),
-    )(image, high_t, low_t, scale, *extra)
+    )(image, high_t, low_t, scale)
 
 
 def work(columns, sites, wraps):
@@ -397,19 +386,18 @@
     )(arrived, hop, scale)
 
 
-def add_up(kernel, met, vertex, turned, total):
+def add_up(offset, met, vertex, turned, total=None):
     _, width, columns = met.shape
     sites = vertex.shape[0]
     extra = [] if total is None else [total]
     return pl.pallas_call(
-        kernel,
+        functools.partial(add_kernel, offset, len(extra)),
         out_shape=jax.ShapeDtypeStruct((sites, width), jnp.float32),
-        in_specs=[VMEM] * (2 + len(turned) + len(extra)),
+        in_specs=[VMEM] * (2 + len(extra) + len(turned)),
         out_specs=VMEM,
-        input_output_aliases={2 + len(turned): 0} if extra else {},
         compiler_params=limit(16),
         cost_estimate=work(columns, sites, 1),
-    )(met, vertex, *turned, *extra)
+    )(met, vertex, *extra, *turned)
 
 
 def finish(offset, ours, theirs, hop, columns, vertex, total, turned):
@@ -459,31 +447,29 @@
     cols, sites = lax.axis_size("colt"), lax.axis_size("site")
     wraps, width = field_spins.shape[0], seed_green.shape[-1]
     edge = width - LANES
-    across = [(i, (i + cols // 2) % cols) for i in range(cols)]
+    across = [
+        (i * sites + core, (i + cols // 2) % cols * sites + sites - 1 - core)
+        for i in range(cols)
+        for core in range(sites)
+    ]
     swap = [(i, sites - 1 - i) for i in range(sites)]
 
     pieces, lines = cut(seed_green[0, 0], field_spins, [(0, edge), (edge, width)])
-    first = lax.ppermute(pieces[0], "colt", across)
-    second = lax.ppermute(pieces[1], "colt", across)
+    first = lax.ppermute(pieces[0], ("colt", "site"), across)
+    second = lax.ppermute(pieces[1], ("colt", "site"), across)
     found, doubled = fetch_lines(hold(lines))
     hop, high_t, low_t, seed_t = prepare(hop_matrix, pieces)
     image = lift(seed_t, high_t, low_t, vertex)
     early, image, scale, columns = start_own(wraps, image, high_t, low_t, found, doubled)
     own = (high_t, low_t, scale)
-    rest, level = propagate(0, 1, 2, image, *own)
+    middle, level = propagate(1, 2, image, *own)
     keep, send = chain(first, hop, columns, width)
-    for place in range(1, sites):
-        (rest,) = propagate(place, 1, wraps, image, *own, rest)
     came = lax.ppermute(send, "site", swap)
-    (rest,) = propagate(0, 2, wraps, level, *own, rest)
-    turned = [early, rest]
-    total = None
-    for place in range(1, sites):
-        kernel = functools.partial(ours_kernel, 0, place)
-        total = add_up(kernel, keep, vertex, turned, total)
+    (rest,) = propagate(2, wraps, level, *own)
     other = lax.ppermute(second, "site", swap)
-    total = add_up(functools.partial(ours_kernel, 0, 0), keep, vertex, turned, total)
-    total = add_up(functools.partial(theirs_kernel, 0), came, vertex, turned, total)
+    turned = [early, middle, rest]
+    total = add_up(0, keep, vertex, turned)
+    total = add_up(0, came, vertex, turned, total)
     result = finish(edge, second, other, hop, columns, vertex, total, turned)
     return result[None, None]
 

time: 28.8 us -> 28.8 us (level)
  starting transfers between devices: 8.13 us -> 9.78 us
  waiting for transfers between devices: 7.86 us -> 6.52 us
  Pallas kernels: 12.2 us -> 11.9 us
    ppermute x2, starting transfers between devices: 3.24 us -> 4.94 us  [fetch_lines(): came = lax.ppermute(lines, ('rowt', 'site'), pairs)]
    ppermute x2, waiting for transfers between devices: 2.32 us -> 1.35 us  [fetch_lines(): came = lax.ppermute(lines, ('rowt', 'site'), pairs)]
    ppermute x2, waiting for transfers between devices: 5.53 us -> 5.16 us  [the longest x1 5.16 us: per_device(): second = lax.ppermute(pieces[1], ('colt', 'site'), across)]
    pallas_call x6 -> x4, Pallas kernels: 3.23 us -> 3.14 us  [the longest x2 1.75 us: propagate(): pl.pallas_call(functools.partial(own_kernel, first), out_shape=outs, in_s...]
where the time goes in v6:
time: 28.8 us; the launch traced here: 28.6 us
  Pallas kernels  11.9 us (41%)
  starting transfers between devices  9.78 us (34%)
  waiting for transfers between devices  6.52 us (23%)
    ppermute x1, waiting for transfers between devices, per_device(): second = lax.ppermute(pieces[1], ('colt', 'site'), across)  5.16 us
    ppermute x2, starting transfers between devices, fetch_lines(): came = lax.ppermute(lines, ('rowt', 'site'), pairs)  4.94 us
    pallas_call x1, Pallas kernels, finish(): pl.pallas_call(functools.partial(finish_kernel, offset), out_shape=jax.Sh...  2.65 us
    ppermute x1, starting transfers between devices, per_device(): first = lax.ppermute(pieces[0], ('colt', 'site'), across)  2.47 us
    ppermute x1, starting transfers between devices, per_device(): second = lax.ppermute(pieces[1], ('colt', 'site'), across)  2.19 us
    pallas_call x2, Pallas kernels, propagate(): pl.pallas_call(functools.partial(own_kernel, first), out_shape=outs, in_s...  1.75 us
    pallas_call x1, Pallas kernels, chain(): pl.pallas_call(chain_kernel, out_shape=[shape] * 2, in_specs=[VMEM] * 3,...  1.68 us
    pallas_call x2, Pallas kernels, add_up(): pl.pallas_call(functools.partial(add_kernel, offset, len(extra)), out_sha...  1.38 us
  transfers between devices with their start and end apart: 6, of which 2 were waited for; matrix products, arithmetic and copies ran while one was open for 0% of the time, Pallas kernels for 23%

profile of v6, /device:TPU:0, one launch (start us, length us, event | category | flops | bytes accessed | tf_op | source)
XLA Modules:
  0.0 28.6 jit_solution(6447780766289171973)
XLA Ops:
  0.0 1.2 %cut.1 = (bf16[768,256]{1,0:T(8,128)(2,1)S(1)}, bf16[768,128]{1,0:T(8,128)(2,1)S(1)}, bf16[4,768]{1,0:T(4,128)(2,1)S(1)}) custom-call(bf16[768,384]{1,0:T(8,128)(2,1)} %bitcast.2, s32[4,1,768]{2,1,0:T(1,128)} %spins_ref.1), custom_call_target="tpu_custom_call" | custom-call | tf_op jit(solution)/shard_map/cut/pallas_call | solution.py:267
  1.2 2.5 %collective-permute-start.4 = (bf16[768,256]{1,0:T(8,128)(2,1)S(1)}, bf16[768,256]{1,0:T(8,128)(2,1)S(1)}, u32[]{:S(2)}, u32[]{:S(2)}) collective-permute-start(bf16[768,256]{1,0:T(8,128)(2,1)S(1)} %get-tuple-element.21.refs_0_), channel_id=1, source_target_pairs={{0,3},{1,2},{2,1},{3,0},{4,7},{5,6},{6,5},{7,4},{8,11},{9,10},{10,... | collective-permute-start | bytes 1179656 | tf_op jit(solution)/shard_map/ppermute | solution.py:458
  3.7 0.0 copy-start.1
  3.7 1.9 %collective-permute-start.2 = (bf16[4,768]{1,0:T(4,128)(2,1)S(1)}, bf16[4,768]{1,0:T(4,128)(2,1)S(1)}, u32[]{:S(2)}, u32[]{:S(2)}) collective-permute-start(bf16[4,768]{1,0:T(4,128)(2,1)S(1)} %hold.1.held_ref), channel_id=1, source_target_pairs={{0,5},{1,4},{4,1},{5,0},{8,13},{9,12},{12,9},{13,8},{2,7},{3,6},{6... | collective-permute-start | bytes 18440 | tf_op jit(solution)/shard_map/ppermute | solution.py:432
  5.5 1.3 %collective-permute-done.2.came_ref = bf16[4,768]{1,0:T(4,128)(2,1)S(1)} collective-permute-done((bf16[4,768]{1,0:T(4,128)(2,1)S(1)}, bf16[4,768]{1,0:T(4,128)(2,1)S(1)}, u32[]{:S(2)}, u32[]{:S(2)}) %collective-permute-start.2) | collective-permute-done | bytes 6176 | tf_op jit(solution)/shard_map/ppermute | solution.py:432
  6.9 3.1 %collective-permute-start.3 = (bf16[8,768]{1,0:T(8,128)(2,1)S(1)}, bf16[8,768]{1,0:T(8,128)(2,1)S(1)}, u32[]{:S(2)}, u32[]{:S(2)}) collective-permute-start(bf16[8,768]{1,0:T(8,128)(2,1)S(1)} %join.1.refs_0_), channel_id=1, source_target_pairs={{0,9},{1,8},{4,13},{5,12},{8,1},{9,0},{12,5},{13,4},{2,11},{3,10},... | collective-permute-start | bytes 36872 | tf_op jit(solution)/shard_map/ppermute | solution.py:432
  10.0 0.0 copy-done.1
  10.0 0.0 copy-start
  10.0 1.0 %prepare.1 = (bf16[768,768]{1,0:T(8,128)(2,1)S(1)}, bf16[768,768]{1,0:T(8,128)(2,1)S(1)}, bf16[768,768]{1,0:T(8,128)(2,1)S(1)}, bf16[384,768]{1,0:T(8,128)(2,1)S(1)}) custom-call(f32[768,768]{1,0:T(8,128)S(1)} %copy-done.1, bf16[768,256]{1,0:T(8,128)(2,1)S(1)} %get-tuple-element.21.refs_0_, bf16[768,128]{1,0:T(8,128)(2,1)S(1)} %get-tuple-element.20.refs_1_), custom_call_target="tpu_custom_call" | custom-call | flops 268435456 | bytes 4194304 | tf_op jit(solution)/shard_map/prepare/pallas_call | solution.py:299
  11.0 0.2 copy-done
  11.2 1.1 %lift.1.image_ref = f32[384,768]{1,0:T(8,128)S(1)} custom-call(bf16[384,768]{1,0:T(8,128)(2,1)S(1)} %get-tuple-element.23.seed_t, bf16[768,768]{1,0:T(8,128)(2,1)S(1)} %get-tuple-element.24.high_t, bf16[768,768]{1,0:T(8,128)(2,1)S(1)} %get-tuple-element.25.low_t, bf16[768,768]{1,0:T(8,128)(2,1)S(1)} %copy-done), custom_call_target="tpu_custom_call" | custom-call | flops 28311552 | bytes 65536 | tf_op jit(solution)/shard_map/lift/pallas_call | solution.py:312
  12.3 0.0 collective-permute-done.3.refs_1_
  12.3 1.2 %early.1 = (bf16[1,384,768]{2,1,0:T(8,128)(2,1)S(1)}, f32[384,768]{1,0:T(8,128)S(1)}, f32[4,768]{1,0:T(4,128)S(1)}, f32[4,768,128]{2,1,0:T(8,128)S(1)}) custom-call(f32[384,768]{1,0:T(8,128)S(1)} %lift.1.image_ref, bf16[768,768]{1,0:T(8,128)(2,1)S(1)} %get-tuple-element.24.high_t, bf16[768,768]{1,0:T(8,128)(2,1)S(1)} %get-tuple-element.25.low_t, ...), custom_call_target="tpu_custom_call" | custom-call | flops 28311552 | bytes 65536 | tf_op jit(solution)/shard_map/early/pallas_call | solution.py:337
  13.5 0.0 collective-permute-done.4.arrived
  13.5 1.7 %chain.1 = (bf16[4,384,256]{2,1,0:T(8,128)(2,1)S(1)}, bf16[4,384,256]{2,1,0:T(8,128)(2,1)S(1)}) custom-call(bf16[768,256]{1,0:T(8,128)(2,1)S(1)} %collective-permute-done.4.arrived, bf16[768,768]{1,0:T(8,128)(2,1)S(1)} %get-tuple-element.22.hop_ref.refs_2_, f32[4,768,128]{2,1,0:T(8,128)S(1)} %get-tuple-element.27.scale_ref.refs_3_), custom_call_target="tpu_custom_call" | custom-call | flops 37748736 | bytes 65536 | tf_op jit(solution)/shard_map/chain/pallas_call | solution.py:378
  15.2 0.1 collective-permute-start.5
  15.3 2.2 %collective-permute-start = (bf16[768,128]{1,0:T(8,128)(2,1)S(1)}, bf16[768,128]{1,0:T(8,128)(2,1)S(1)}, u32[]{:S(2)}, u32[]{:S(2)}) collective-permute-start(bf16[768,128]{1,0:T(8,128)(2,1)S(1)} %get-tuple-element.20.refs_1_), channel_id=1, source_target_pairs={{0,3},{1,2},{2,1},{3,0},{4,7},{5,6},{6,5},{7,4},{8,11},{9,10},{10,... | collective-permute-start | bytes 589832 | tf_op jit(solution)/shard_map/ppermute | solution.py:459
  17.5 5.2 %collective-permute-done.refs_0_ = bf16[768,128]{1,0:T(8,128)(2,1)S(1)} collective-permute-done((bf16[768,128]{1,0:T(8,128)(2,1)S(1)}, bf16[768,128]{1,0:T(8,128)(2,1)S(1)}, u32[]{:S(2)}, u32[]{:S(2)}) %collective-permute-start) | collective-permute-done | bytes 196640 | tf_op jit(solution)/shard_map/ppermute | solution.py:459
  22.6 0.1 collective-permute-start.1
  22.7 1.1 %shard_map.46 = (bf16[1,384,768]{2,1,0:T(8,128)(2,1)S(1)}, f32[384,768]{1,0:T(8,128)S(1)}) custom-call(f32[384,768]{1,0:T(8,128)S(1)} %get-tuple-element.31.image_ref, bf16[768,768]{1,0:T(8,128)(2,1)S(1)} %get-tuple-element.24.high_t, bf16[768,768]{1,0:T(8,128)(2,1)S(1)} %get-tuple-element.25.low_t, f32[4,768]{1,0:T(4,128)S(1)} %get-tuple-element.32.scale_ref), custom_call_target="tpu_custom_call" | custom-call | flops 28311552 | bytes 65536 | tf_op jit(solution)/shard_map/pallas_call | solution.py:358
  23.8 0.7 %shard_map.47.refs_2_.refs_3_.refs_8_ = bf16[2,384,768]{2,1,0:T(8,128)(2,1)S(1)} custom-call(f32[384,768]{1,0:T(8,128)S(1)} %get-tuple-element.34.image_ref, bf16[768,768]{1,0:T(8,128)(2,1)S(1)} %get-tuple-element.24.high_t, bf16[768,768]{1,0:T(8,128)(2,1)S(1)} %get-tuple-element.25.low_t, f32[4,768]{1,0:T(4,128)S(1)} %get-tuple-element.32.scale_ref), custom_call_target="tpu_custom_call" | custom-call | flops 56623104 | bytes 65536 | tf_op jit(solution)/shard_map/pallas_call | solution.py:358
  24.5 0.7 %shard_map.48.refs_0_ = f32[768,384]{1,0:T(8,128)S(1)} custom-call(bf16[4,384,256]{2,1,0:T(8,128)(2,1)S(1)} %get-tuple-element.29.met_ref, bf16[768,768]{1,0:T(8,128)(2,1)S(1)} %copy-done, bf16[1,384,768]{2,1,0:T(8,128)(2,1)S(1)} %get-tuple-element.30.refs_0_.refs_1_.refs_6_, bf16[1,384,768]{2,1,0:T(8,128)(2,1)S(1)} %get-tuple-element.33.refs_1_.refs_2_.refs_7_, ...), custom_call_target="tpu_custom_call" | custom-call | flops 9437184 | bytes 65536 | tf_op jit(solution)/shard_map/pallas_call | solution.py:393
  25.2 0.0 collective-permute-done.5.met_ref
  25.2 0.7 %shard_map.49.refs_5_ = f32[768,384]{1,0:T(8,128)S(1)} custom-call(bf16[4,384,256]{2,1,0:T(8,128)(2,1)S(1)} %collective-permute-done.5.met_ref, bf16[768,768]{1,0:T(8,128)(2,1)S(1)} %copy-done, f32[768,384]{1,0:T(8,128)S(1)} %shard_map.48.refs_0_, bf16[1,384,768]{2,1,0:T(8,128)(2,1)S(1)} %get-tuple-element.30.refs_0_.refs_1_.refs_6_, ...), custom_call_target="tpu_custom_call" | custom-call | flops 9437184 | bytes 65536 | tf_op jit(solution)/shard_map/pallas_call | solution.py:393
  25.9 0.0 collective-permute-done.1.refs_1_
  25.9 2.7 %finish.1 = bf16[768,384]{1,0:T(8,128)(2,1)} custom-call(bf16[768,128]{1,0:T(8,128)(2,1)S(1)} %collective-permute-done.refs_0_, bf16[768,128]{1,0:T(8,128)(2,1)S(1)} %collective-permute-done.1.refs_1_, bf16[768,768]{1,0:T(8,128)(2,1)S(1)} %get-tuple-element.22.hop_ref.refs_2_, f32[4,768,128]{2,1,0:T(8,128)S(1)} %get-tuple-element.27.scale_ref.refs_3_, ...), custom_call_target="tpu_custom_call" | custom-call | flops 37748736 | bytes 65536 | tf_op jit(solution)/shard_map/finish/pallas_call | solution.py:406
  (2 shorter events, 0.0 us)
Async XLA Ops:
  1.2 12.3 %collective-permute-start.4 = (bf16[768,256]{1,0:T(8,128)(2,1)S(1)}, bf16[768,256]{1,0:T(8,128)(2,1)S(1)}, u32[]{:S(2)}, u32[]{:S(2)}) collective-permute-start(bf16[768,256]{1,0:T(8,128)(2,1)S(1)} %get-tuple-element.21.refs_0_), channel_id=1, source_target_pairs={{0,3},{1,2},{2,1},{3,0},{4,7},{5,6},{6,5},{7,4},{8,11},{9,10},{10,... | collective-permute-start | bytes 1179656 | tf_op jit(solution)/shard_map/ppermute | solution.py:458
  3.7 6.3 %copy-start.1 = (f32[768,768]{1,0:T(8,128)S(1)}, f32[768,768]{1,0:T(8,128)}, u32[]{:S(2)}) copy-start(f32[768,768]{1,0:T(8,128)} %hop_ref.1) | copy-start | bytes 7077892
  3.7 3.2 %collective-permute-start.2 = (bf16[4,768]{1,0:T(4,128)(2,1)S(1)}, bf16[4,768]{1,0:T(4,128)(2,1)S(1)}, u32[]{:S(2)}, u32[]{:S(2)}) collective-permute-start(bf16[4,768]{1,0:T(4,128)(2,1)S(1)} %hold.1.held_ref), channel_id=1, source_target_pairs={{0,5},{1,4},{4,1},{5,0},{8,13},{9,12},{12,9},{13,8},{2,7},{3,6},{6... | collective-permute-start | bytes 18440 | tf_op jit(solution)/shard_map/ppermute | solution.py:432
  6.9 5.4 %collective-permute-start.3 = (bf16[8,768]{1,0:T(8,128)(2,1)S(1)}, bf16[8,768]{1,0:T(8,128)(2,1)S(1)}, u32[]{:S(2)}, u32[]{:S(2)}) collective-permute-start(bf16[8,768]{1,0:T(8,128)(2,1)S(1)} %join.1.refs_0_), channel_id=1, source_target_pairs={{0,9},{1,8},{4,13},{5,12},{8,1},{9,0},{12,5},{13,4},{2,11},{3,10},... | collective-permute-start | bytes 36872 | tf_op jit(solution)/shard_map/ppermute | solution.py:432
  10.0 1.3 %copy-start = (bf16[768,768]{1,0:T(8,128)(2,1)S(1)}, bf16[768,768]{1,0:T(8,128)(2,1)}, u32[]{:S(2)}) copy-start(bf16[768,768]{1,0:T(8,128)(2,1)} %refs_4_.1) | copy-start | bytes 3538948
  15.2 10.0 %collective-permute-start.5 = (bf16[4,384,256]{2,1,0:T(8,128)(2,1)S(1)}, bf16[4,384,256]{2,1,0:T(8,128)(2,1)S(1)}, u32[]{:S(2)}, u32[]{:S(2)}) collective-permute-start(bf16[4,384,256]{2,1,0:T(8,128)(2,1)S(1)} %get-tuple-element.28), channel_id=1, source_target_pairs={{0,1},{1,0},{2,3},{3,2},{4,5},{5,4},{6,7},{7,6},{8,9},{9,8},{10,11... | collective-permute-start | bytes 2359304 | tf_op jit(solution)/shard_map/ppermute | solution.py:467
  15.3 7.3 %collective-permute-start = (bf16[768,128]{1,0:T(8,128)(2,1)S(1)}, bf16[768,128]{1,0:T(8,128)(2,1)S(1)}, u32[]{:S(2)}, u32[]{:S(2)}) collective-permute-start(bf16[768,128]{1,0:T(8,128)(2,1)S(1)} %get-tuple-element.20.refs_1_), channel_id=1, source_target_pairs={{0,3},{1,2},{2,1},{3,0},{4,7},{5,6},{6,5},{7,4},{8,11},{9,10},{10,... | collective-permute-start | bytes 589832 | tf_op jit(solution)/shard_map/ppermute | solution.py:459
  22.6 3.3 %collective-permute-start.1 = (bf16[768,128]{1,0:T(8,128)(2,1)S(1)}, bf16[768,128]{1,0:T(8,128)(2,1)S(1)}, u32[]{:S(2)}, u32[]{:S(2)}) collective-permute-start(bf16[768,128]{1,0:T(8,128)(2,1)S(1)} %collective-permute-done.refs_0_), channel_id=1, source_target_pairs={{0,1},{1,0},{2,3},{3,2},{4,5},{5,4},{6,7},{7,6},{8,9},{9,8},{10,11... | collective-permute-start | bytes 589832 | tf_op jit(solution)/shard_map/ppermute | solution.py:469

commit v7 on v6

--- a/solution.py
+++ b/solution.py
@@ -171,8 +171,9 @@
             new.append(moved)
             fresh.append(moved.astype(jnp.bfloat16))
         yield jnp.concatenate(fresh[half * each : half * each + each], axis=0)
+    level[: len(new)] = new
     if halves == 2:
-        level[:], narrow[:] = new, fresh
+        narrow[:] = fresh
 
 
 def chain_kernel(arrived, hop_ref, scale_ref, keep_out, send_out):
@@ -226,8 +227,17 @@
     out_ref[...] = total + sum_part(offset, which, met_ref, vertex_ref, turned_refs)
 
 
+def fold_kernel(hop_ref, scale_ref, fold_out):
+    width, wraps = fold_out.shape[0], scale_ref.shape[0]
+    left = hop_ref[:width, :].astype(jnp.float32) * scale_ref[wraps - 2 : wraps - 1, :]
+    right = jnp.dot(
+        left.astype(jnp.bfloat16), hop_ref[...], preferred_element_type=jnp.float32
+    )
+    fold_out[...] = (keep_share * left + right).astype(jnp.bfloat16)
+
+
 def finish_kernel(offset, *refs):
-    ours, theirs, hop_ref, scale_ref, vertex_ref, total_ref, *turned_refs = refs[:-3]
+    ours, theirs, hop_ref, fold_ref, scale_ref, vertex_ref, total_ref, *turned_refs = refs[:-3]
     out_ref, result, sems = refs[-3:]
     wraps, (sites, width) = scale_ref.shape[0], total_ref.shape
     spans = [slice(0, width), slice(width, 2 * width)]
@@ -237,12 +247,15 @@
     narrow = [block.astype(jnp.bfloat16) for block in level]
     pairs = None
     for step, own in enumerate(own_levels(turned_refs, held)):
-        halves = 2 if step < wraps - 1 else 1
-        met, *_ = advance(step, halves, hop_ref, scale_ref, level, narrow)
+        if step < wraps - 2:
+            met, *_ = advance(step, 2, hop_ref, scale_ref, level, narrow)
+        else:
+            weights = hop_ref if step == wraps - 2 else fold_ref
+            met, *_ = advance(step, 1, weights, scale_ref, level, narrow)
         product = multiply(met, own)
         pairs = product if pairs is None else pairs + product
     summed = pairs.astype(jnp.bfloat16)
-    edges = [0, sites - sites // 4, sites]
+    edges = [0, sites // 2, sites]
     copies = []
     for block, (begin, end) in enumerate(zip(edges, edges[1:])):
         span = slice(begin, end)
@@ -400,13 +413,26 @@
     )(met, vertex, *extra, *turned)
 
 
-def finish(offset, ours, theirs, hop, columns, vertex, total, turned):
+def fold(hop, scale, width):
+    sites = hop.shape[0]
+    return pl.pallas_call(
+        fold_kernel,
+        out_shape=jax.ShapeDtypeStruct((width, sites), jnp.bfloat16),
+        in_specs=[VMEM] * 2,
+        out_specs=VMEM,
+        compiler_params=limit(16),
+        cost_estimate=work(width, sites, 1),
+        name="fold",
+    )(hop, scale)
+
+
+def finish(offset, ours, theirs, hop, folded, columns, vertex, total, turned):
     sites, width = total.shape
     blocks = 2
     return pl.pallas_call(
         functools.partial(finish_kernel, offset),
         out_shape=jax.ShapeDtypeStruct((sites, width), jnp.bfloat16),
-        in_specs=[VMEM] * (6 + len(turned)),
+        in_specs=[VMEM] * (7 + len(turned)),
         out_specs=HBM,
         scratch_shapes=[
             pltpu.VMEM((sites, width), jnp.bfloat16),
@@ -415,7 +441,7 @@
         compiler_params=limit(16),
         cost_estimate=work(2 * ours.shape[1], sites, columns.shape[0]),
         name="finish",
-    )(ours, theirs, hop, columns, vertex, total, *turned)
+    )(ours, theirs, hop, folded, columns, vertex, total, *turned)
 
 
 def fetch_lines(lines):
@@ -469,8 +495,9 @@
     other = lax.ppermute(second, "site", swap)
     turned = [early, middle, rest]
     total = add_up(0, keep, vertex, turned)
+    folded = fold(hop, scale, width)
     total = add_up(0, came, vertex, turned, total)
-    result = finish(edge, second, other, hop, columns, vertex, total, turned)
+    result = finish(edge, second, other, hop, folded, columns, vertex, total, turned)
     return result[None, None]
 
 

time: 28.8 us -> 29.2 us (1.014)
  Pallas kernels: 11.9 us -> 12.4 us
    pallas_call x0 -> x1, Pallas kernels: none -> 0.63 us  [fold(): pl.pallas_call(fold_kernel, out_shape=jax.ShapeDtypeStruct((width, sites)...]
  transfers between devices with their start and end apart: 6 -> 6, of which waited for: 2 -> 2; matrix products, arithmetic and copies ran while one was open for 0% -> 0% of each run, Pallas kernels for 23% -> 25%
where the time goes in v7:
time: 29.2 us; the launch traced here: 29 us
  Pallas kernels  12.4 us (42%)
  starting transfers between devices  9.75 us (33%)
  waiting for transfers between devices  6.52 us (22%)
    ppermute x1, waiting for transfers between devices, per_device(): second = lax.ppermute(pieces[1], ('colt', 'site'), across)  5.16 us
    ppermute x2, starting transfers between devices, fetch_lines(): came = lax.ppermute(lines, ('rowt', 'site'), pairs)  4.94 us
    ppermute x1, starting transfers between devices, per_device(): first = lax.ppermute(pieces[0], ('colt', 'site'), across)  2.47 us
    pallas_call x1, Pallas kernels, finish(): pl.pallas_call(functools.partial(finish_kernel, offset), out_shape=jax.Sh...  2.4 us
    ppermute x1, starting transfers between devices, per_device(): second = lax.ppermute(pieces[1], ('colt', 'site'), across)  2.16 us
    pallas_call x2, Pallas kernels, propagate(): pl.pallas_call(functools.partial(own_kernel, first), out_shape=outs, in_s...  1.8 us
    pallas_call x1, Pallas kernels, chain(): pl.pallas_call(chain_kernel, out_shape=[shape] * 2, in_specs=[VMEM] * 3,...  1.67 us
    pallas_call x2, Pallas kernels, add_up(): pl.pallas_call(functools.partial(add_kernel, offset, len(extra)), out_sha...  1.38 us
  transfers between devices with their start and end apart: 6, of which 2 were waited for; matrix products, arithmetic and copies ran while one was open for 0% of the time, Pallas kernels for 25%

profile of v7, /device:TPU:0, one launch (start us, length us, event | category | flops | bytes accessed | tf_op | source)
XLA Modules:
  0.0 29.0 jit_solution(12872446326297158529)
XLA Ops:
  0.0 1.2 %cut.1 = (bf16[768,256]{1,0:T(8,128)(2,1)S(1)}, bf16[768,128]{1,0:T(8,128)(2,1)S(1)}, bf16[4,768]{1,0:T(4,128)(2,1)S(1)}) custom-call(bf16[768,384]{1,0:T(8,128)(2,1)} %bitcast.2, s32[4,1,768]{2,1,0:T(1,128)} %spins_ref.1), custom_call_target="tpu_custom_call" | custom-call | tf_op jit(solution)/shard_map/cut/pallas_call | solution.py:280
  1.2 2.5 %collective-permute-start.4 = (bf16[768,256]{1,0:T(8,128)(2,1)S(1)}, bf16[768,256]{1,0:T(8,128)(2,1)S(1)}, u32[]{:S(2)}, u32[]{:S(2)}) collective-permute-start(bf16[768,256]{1,0:T(8,128)(2,1)S(1)} %get-tuple-element.21.refs_0_), channel_id=1, source_target_pairs={{0,3},{1,2},{2,1},{3,0},{4,7},{5,6},{6,5},{7,4},{8,11},{9,10},{10,... | collective-permute-start | bytes 1179656 | tf_op jit(solution)/shard_map/ppermute | solution.py:484
  3.7 0.0 copy-start.1
  3.7 1.9 %collective-permute-start.2 = (bf16[4,768]{1,0:T(4,128)(2,1)S(1)}, bf16[4,768]{1,0:T(4,128)(2,1)S(1)}, u32[]{:S(2)}, u32[]{:S(2)}) collective-permute-start(bf16[4,768]{1,0:T(4,128)(2,1)S(1)} %hold.1.held_ref), channel_id=1, source_target_pairs={{0,5},{1,4},{4,1},{5,0},{8,13},{9,12},{12,9},{13,8},{2,7},{3,6},{6... | collective-permute-start | bytes 18440 | tf_op jit(solution)/shard_map/ppermute | solution.py:458
  5.5 1.3 %collective-permute-done.2.came_ref = bf16[4,768]{1,0:T(4,128)(2,1)S(1)} collective-permute-done((bf16[4,768]{1,0:T(4,128)(2,1)S(1)}, bf16[4,768]{1,0:T(4,128)(2,1)S(1)}, u32[]{:S(2)}, u32[]{:S(2)}) %collective-permute-start.2) | collective-permute-done | bytes 6176 | tf_op jit(solution)/shard_map/ppermute | solution.py:458
  6.9 3.1 %collective-permute-start.3 = (bf16[8,768]{1,0:T(8,128)(2,1)S(1)}, bf16[8,768]{1,0:T(8,128)(2,1)S(1)}, u32[]{:S(2)}, u32[]{:S(2)}) collective-permute-start(bf16[8,768]{1,0:T(8,128)(2,1)S(1)} %join.1.refs_0_), channel_id=1, source_target_pairs={{0,9},{1,8},{4,13},{5,12},{8,1},{9,0},{12,5},{13,4},{2,11},{3,10},... | collective-permute-start | bytes 36872 | tf_op jit(solution)/shard_map/ppermute | solution.py:458
  10.0 0.0 copy-done.1
  10.0 0.0 copy-start
  10.0 1.0 %prepare.1 = (bf16[768,768]{1,0:T(8,128)(2,1)S(1)}, bf16[768,768]{1,0:T(8,128)(2,1)S(1)}, bf16[768,768]{1,0:T(8,128)(2,1)S(1)}, bf16[384,768]{1,0:T(8,128)(2,1)S(1)}) custom-call(f32[768,768]{1,0:T(8,128)S(1)} %copy-done.1, bf16[768,256]{1,0:T(8,128)(2,1)S(1)} %get-tuple-element.21.refs_0_, bf16[768,128]{1,0:T(8,128)(2,1)S(1)} %get-tuple-element.20.refs_1_), custom_call_target="tpu_custom_call" | custom-call | flops 268435456 | bytes 4194304 | tf_op jit(solution)/shard_map/prepare/pallas_call | solution.py:312
  11.0 0.2 copy-done
  11.2 1.1 %lift.1.image_ref = f32[384,768]{1,0:T(8,128)S(1)} custom-call(bf16[384,768]{1,0:T(8,128)(2,1)S(1)} %get-tuple-element.23.seed_t, bf16[768,768]{1,0:T(8,128)(2,1)S(1)} %get-tuple-element.24.high_t, bf16[768,768]{1,0:T(8,128)(2,1)S(1)} %get-tuple-element.25.low_t, bf16[768,768]{1,0:T(8,128)(2,1)S(1)} %copy-done), custom_call_target="tpu_custom_call" | custom-call | flops 28311552 | bytes 65536 | tf_op jit(solution)/shard_map/lift/pallas_call | solution.py:325
  12.3 0.0 collective-permute-done.3.refs_1_
  12.3 1.2 %early.1 = (bf16[1,384,768]{2,1,0:T(8,128)(2,1)S(1)}, f32[384,768]{1,0:T(8,128)S(1)}, f32[4,768]{1,0:T(4,128)S(1)}, f32[4,768,128]{2,1,0:T(8,128)S(1)}) custom-call(f32[384,768]{1,0:T(8,128)S(1)} %lift.1.image_ref, bf16[768,768]{1,0:T(8,128)(2,1)S(1)} %get-tuple-element.24.high_t, bf16[768,768]{1,0:T(8,128)(2,1)S(1)} %get-tuple-element.25.low_t, ...), custom_call_target="tpu_custom_call" | custom-call | flops 28311552 | bytes 65536 | tf_op jit(solution)/shard_map/early/pallas_call | solution.py:350
  13.5 0.0 collective-permute-done.4.arrived
  13.6 1.7 %chain.1 = (bf16[4,384,256]{2,1,0:T(8,128)(2,1)S(1)}, bf16[4,384,256]{2,1,0:T(8,128)(2,1)S(1)}) custom-call(bf16[768,256]{1,0:T(8,128)(2,1)S(1)} %collective-permute-done.4.arrived, bf16[768,768]{1,0:T(8,128)(2,1)S(1)} %get-tuple-element.22.hop_ref.refs_2_, f32[4,768,128]{2,1,0:T(8,128)S(1)} %get-tuple-element.28.scale_ref.refs_4_), custom_call_target="tpu_custom_call" | custom-call | flops 37748736 | bytes 65536 | tf_op jit(solution)/shard_map/chain/pallas_call | solution.py:391
  15.2 0.1 collective-permute-start.5
  15.3 2.2 %collective-permute-start = (bf16[768,128]{1,0:T(8,128)(2,1)S(1)}, bf16[768,128]{1,0:T(8,128)(2,1)S(1)}, u32[]{:S(2)}, u32[]{:S(2)}) collective-permute-start(bf16[768,128]{1,0:T(8,128)(2,1)S(1)} %get-tuple-element.20.refs_1_), channel_id=1, source_target_pairs={{0,3},{1,2},{2,1},{3,0},{4,7},{5,6},{6,5},{7,4},{8,11},{9,10},{10,... | collective-permute-start | bytes 589832 | tf_op jit(solution)/shard_map/ppermute | solution.py:485
  17.5 5.2 %collective-permute-done.refs_0_ = bf16[768,128]{1,0:T(8,128)(2,1)S(1)} collective-permute-done((bf16[768,128]{1,0:T(8,128)(2,1)S(1)}, bf16[768,128]{1,0:T(8,128)(2,1)S(1)}, u32[]{:S(2)}, u32[]{:S(2)}) %collective-permute-start) | collective-permute-done | bytes 196640 | tf_op jit(solution)/shard_map/ppermute | solution.py:485
  22.6 0.1 collective-permute-start.1
  22.7 0.6 %fold.1.refs_3_ = bf16[384,768]{1,0:T(8,128)(2,1)S(1)} custom-call(bf16[768,768]{1,0:T(8,128)(2,1)S(1)} %get-tuple-element.22.hop_ref.refs_2_, f32[4,768]{1,0:T(4,128)S(1)} %get-tuple-element.27.scale_ref), custom_call_target="tpu_custom_call" | custom-call | flops 14155776 | bytes 65536 | tf_op jit(solution)/shard_map/fold/pallas_call | solution.py:418
  23.4 1.1 %shard_map.46 = (bf16[1,384,768]{2,1,0:T(8,128)(2,1)S(1)}, f32[384,768]{1,0:T(8,128)S(1)}) custom-call(f32[384,768]{1,0:T(8,128)S(1)} %get-tuple-element.32.image_ref, bf16[768,768]{1,0:T(8,128)(2,1)S(1)} %get-tuple-element.24.high_t, bf16[768,768]{1,0:T(8,128)(2,1)S(1)} %get-tuple-element.25.low_t, f32[4,768]{1,0:T(4,128)S(1)} %get-tuple-element.27.scale_ref), custom_call_target="tpu_custom_call" | custom-call | flops 28311552 | bytes 65536 | tf_op jit(solution)/shard_map/pallas_call | solution.py:371
  24.5 0.7 %shard_map.47.refs_2_.refs_3_.refs_9_ = bf16[2,384,768]{2,1,0:T(8,128)(2,1)S(1)} custom-call(f32[384,768]{1,0:T(8,128)S(1)} %get-tuple-element.34.image_ref, bf16[768,768]{1,0:T(8,128)(2,1)S(1)} %get-tuple-element.24.high_t, bf16[768,768]{1,0:T(8,128)(2,1)S(1)} %get-tuple-element.25.low_t, f32[4,768]{1,0:T(4,128)S(1)} %get-tuple-element.27.scale_ref), custom_call_target="tpu_custom_call" | custom-call | flops 56623104 | bytes 65536 | tf_op jit(solution)/shard_map/pallas_call | solution.py:371
  25.2 0.7 %shard_map.48.refs_0_ = f32[768,384]{1,0:T(8,128)S(1)} custom-call(bf16[4,384,256]{2,1,0:T(8,128)(2,1)S(1)} %get-tuple-element.30.met_ref, bf16[768,768]{1,0:T(8,128)(2,1)S(1)} %copy-done, bf16[1,384,768]{2,1,0:T(8,128)(2,1)S(1)} %get-tuple-element.31.refs_0_.refs_1_.refs_7_, bf16[1,384,768]{2,1,0:T(8,128)(2,1)S(1)} %get-tuple-element.33.refs_1_.refs_2_.refs_8_, ...), custom_call_target="tpu_custom_call" | custom-call | flops 9437184 | bytes 65536 | tf_op jit(solution)/shard_map/pallas_call | solution.py:406
  25.9 0.0 collective-permute-done.5.met_ref
  25.9 0.7 %shard_map.49.refs_6_ = f32[768,384]{1,0:T(8,128)S(1)} custom-call(bf16[4,384,256]{2,1,0:T(8,128)(2,1)S(1)} %collective-permute-done.5.met_ref, bf16[768,768]{1,0:T(8,128)(2,1)S(1)} %copy-done, f32[768,384]{1,0:T(8,128)S(1)} %shard_map.48.refs_0_, bf16[1,384,768]{2,1,0:T(8,128)(2,1)S(1)} %get-tuple-element.31.refs_0_.refs_1_.refs_7_, ...), custom_call_target="tpu_custom_call" | custom-call | flops 9437184 | bytes 65536 | tf_op jit(solution)/shard_map/pallas_call | solution.py:406
  26.6 0.0 collective-permute-done.1.refs_1_
  26.6 2.4 %finish.1 = bf16[768,384]{1,0:T(8,128)(2,1)} custom-call(bf16[768,128]{1,0:T(8,128)(2,1)S(1)} %collective-permute-done.refs_0_, bf16[768,128]{1,0:T(8,128)(2,1)S(1)} %collective-permute-done.1.refs_1_, bf16[768,768]{1,0:T(8,128)(2,1)S(1)} %get-tuple-element.22.hop_ref.refs_2_, bf16[384,768]{1,0:T(8,128)(2,1)S(1)} %fold.1.refs_3_, ...), custom_call_target="tpu_custom_call" | custom-call | flops 37748736 | bytes 65536 | tf_op jit(solution)/shard_map/finish/pallas_call | solution.py:432
  (2 shorter events, 0.0 us)
Async XLA Ops:
  1.2 12.4 %collective-permute-start.4 = (bf16[768,256]{1,0:T(8,128)(2,1)S(1)}, bf16[768,256]{1,0:T(8,128)(2,1)S(1)}, u32[]{:S(2)}, u32[]{:S(2)}) collective-permute-start(bf16[768,256]{1,0:T(8,128)(2,1)S(1)} %get-tuple-element.21.refs_0_), channel_id=1, source_target_pairs={{0,3},{1,2},{2,1},{3,0},{4,7},{5,6},{6,5},{7,4},{8,11},{9,10},{10,... | collective-permute-start | bytes 1179656 | tf_op jit(solution)/shard_map/ppermute | solution.py:484
  3.7 6.3 %copy-start.1 = (f32[768,768]{1,0:T(8,128)S(1)}, f32[768,768]{1,0:T(8,128)}, u32[]{:S(2)}) copy-start(f32[768,768]{1,0:T(8,128)} %hop_ref.1) | copy-start | bytes 7077892
  3.7 3.2 %collective-permute-start.2 = (bf16[4,768]{1,0:T(4,128)(2,1)S(1)}, bf16[4,768]{1,0:T(4,128)(2,1)S(1)}, u32[]{:S(2)}, u32[]{:S(2)}) collective-permute-start(bf16[4,768]{1,0:T(4,128)(2,1)S(1)} %hold.1.held_ref), channel_id=1, source_target_pairs={{0,5},{1,4},{4,1},{5,0},{8,13},{9,12},{12,9},{13,8},{2,7},{3,6},{6... | collective-permute-start | bytes 18440 | tf_op jit(solution)/shard_map/ppermute | solution.py:458
  6.9 5.5 %collective-permute-start.3 = (bf16[8,768]{1,0:T(8,128)(2,1)S(1)}, bf16[8,768]{1,0:T(8,128)(2,1)S(1)}, u32[]{:S(2)}, u32[]{:S(2)}) collective-permute-start(bf16[8,768]{1,0:T(8,128)(2,1)S(1)} %join.1.refs_0_), channel_id=1, source_target_pairs={{0,9},{1,8},{4,13},{5,12},{8,1},{9,0},{12,5},{13,4},{2,11},{3,10},... | collective-permute-start | bytes 36872 | tf_op jit(solution)/shard_map/ppermute | solution.py:458
  10.0 1.3 %copy-start = (bf16[768,768]{1,0:T(8,128)(2,1)S(1)}, bf16[768,768]{1,0:T(8,128)(2,1)}, u32[]{:S(2)}) copy-start(bf16[768,768]{1,0:T(8,128)(2,1)} %refs_5_.1) | copy-start | bytes 3538948
  15.2 10.7 %collective-permute-start.5 = (bf16[4,384,256]{2,1,0:T(8,128)(2,1)S(1)}, bf16[4,384,256]{2,1,0:T(8,128)(2,1)S(1)}, u32[]{:S(2)}, u32[]{:S(2)}) collective-permute-start(bf16[4,384,256]{2,1,0:T(8,128)(2,1)S(1)} %get-tuple-element.29), channel_id=1, source_target_pairs={{0,1},{1,0},{2,3},{3,2},{4,5},{5,4},{6,7},{7,6},{8,9},{9,8},{10,11... | collective-permute-start | bytes 2359304 | tf_op jit(solution)/shard_map/ppermute | solution.py:493
  15.3 7.3 %collective-permute-start = (bf16[768,128]{1,0:T(8,128)(2,1)S(1)}, bf16[768,128]{1,0:T(8,128)(2,1)S(1)}, u32[]{:S(2)}, u32[]{:S(2)}) collective-permute-start(bf16[768,128]{1,0:T(8,128)(2,1)S(1)} %get-tuple-element.20.refs_1_), channel_id=1, source_target_pairs={{0,3},{1,2},{2,1},{3,0},{4,7},{5,6},{6,5},{7,4},{8,11},{9,10},{10,... | collective-permute-start | bytes 589832 | tf_op jit(solution)/shard_map/ppermute | solution.py:485
  22.6 4.0 %collective-permute-start.1 = (bf16[768,128]{1,0:T(8,128)(2,1)S(1)}, bf16[768,128]{1,0:T(8,128)(2,1)S(1)}, u32[]{:S(2)}, u32[]{:S(2)}) collective-permute-start(bf16[768,128]{1,0:T(8,128)(2,1)S(1)} %collective-permute-done.refs_0_), channel_id=1, source_target_pairs={{0,1},{1,0},{2,3},{3,2},{4,5},{5,4},{6,7},{7,6},{8,9},{9,8},{10,11... | collective-permute-start | bytes 589832 | tf_op jit(solution)/shard_map/ppermute | solution.py:495
